TPU v7x, 32 devices: a whole 2x2x4 slice. The times are simulated.
32 devices in a mesh: row: 4 (over y, x), col: 4 (over z), depth: 2 (over core).
Axes of the slice: x: 2, y: 2, z: 4, core: 2. Of those that a mesh axis runs over, the one named last changes fastest.
Arguments:
- sequence_stack: bfloat16 [256, 96, 64], P('depth', ('row', 'col')), may hold values from -6 to 6
- present_sequence_flags: int32 [256], replicated, may hold values 0 or 1
- genuine_residue_flags: int32 [96], replicated, may hold values 0 or 1
- couple_state: bfloat16 [96, 96, 128], P('row', 'col'), may hold values from -6 to 6
- tensor_scale: float32 [64], replicated, may hold values from 0.1 to 1.9
- tensor_entry_matrix: bfloat16 [64, 64], replicated, may hold values from -0.75 to 0.75
- tensor_final_matrix: bfloat16 [1024, 128], replicated, may hold values from -1 to 1
- tensor_offset: float32 [128], replicated, may hold values from -3 to 3
- mean_sequence_scale: float32 [64], replicated, may hold values from 0.1 to 1.9
- mean_couple_scale: float32 [128], replicated, may hold values from 0.1 to 1.9
- mean_score_matrix: float32 [128, 8], replicated, may hold values from -64 to 64
- mean_content_matrix: bfloat16 [64, 256], replicated, may hold values from -0.75 to 0.75
- mean_sigmoid_matrix: bfloat16 [64, 256], replicated, may hold values from -0.75 to 0.75
- mean_final_matrix: bfloat16 [256, 64], replicated, may hold values from -0.375 to 0.375
- trimul_scale: float32 [128], replicated, may hold values from 0.1 to 1.9
- trimul_entry_matrix: bfloat16 [128, 640], replicated, may hold values from -0.5 to 0.5
- trimul_result_scale: float32 [128], replicated, may hold values from 0.1 to 1.9
- trimul_final_matrix: bfloat16 [128, 128], replicated, may hold values from -0.5 to 0.5
Outputs:
- revised_sequences: bfloat16 [256, 96, 64], P('depth', ('row', 'col'))
- pair_output: bfloat16 [96, 96, 128], P('row', 'col')
All inputs are finite; a program needn't handle non-finite values.
Results may differ from a plain program's by a relative error of at most 0.012.
The roundings to bfloat16 on the way count: a program that leaves them out, or rounds other values in their place, can miss the bound.
Values may be sent and summed in bfloat16 or wider, within the bound.
No kernel may reach another device: no remote copies, remote signals or barrier semaphores. Data moves between devices by JAX's collectives and lax.ppermute only.
A program may use at most 128 MiB of HBM per device.

v0:
```python
import jax
import jax.numpy as jnp
from jax import lax
from jax.sharding import PartitionSpec as P

epsilon = 1e-05


def from_root(array, axis, root):
    mine = lax.axis_index(axis) == root
    return lax.psum(jnp.where(mine, array, jnp.zeros_like(array)), axis)


def standardize_features(value_rows, scale):
    value_rows = value_rows.astype(jnp.float32)
    average = jnp.mean(value_rows, -1, keepdims=True)
    centred = value_rows - average
    variance = jnp.mean(centred * centred, -1, keepdims=True)
    return centred * lax.rsqrt(variance + epsilon) * scale


def on_device(
    sequence_stack,
    present_sequence_flags,
    genuine_residue_flags,
    couple_state,
    tensor_scale,
    tensor_entry_matrix,
    tensor_final_matrix,
    tensor_offset,
    mean_sequence_scale,
    mean_couple_scale,
    mean_score_matrix,
    mean_content_matrix,
    mean_sigmoid_matrix,
    mean_final_matrix,
    trimul_scale,
    trimul_entry_matrix,
    trimul_result_scale,
    trimul_final_matrix,
):
    n_row = lax.axis_size("row")
    n_col = lax.axis_size("col")
    row_index = lax.axis_index("row")
    col_index = lax.axis_index("col")
    depth_position = lax.axis_index("depth")
    piece_rows, piece_columns, width = couple_state.shape
    sequence_count, shard_residues, ignored_quantity = sequence_stack.shape
    hidden = tensor_entry_matrix.shape[1] // 2
    head_split = mean_score_matrix.shape[1]
    head_channels = mean_content_matrix.shape[1] // head_split
    token_weight = genuine_residue_flags.astype(jnp.float32)
    mask_as_float = present_sequence_flags.astype(jnp.float32)
    row_softmax_weight = lax.dynamic_slice_in_dim(
        mask_as_float, depth_position * sequence_count, sequence_count
    )
    row_count = jnp.sum(mask_as_float)
    entire_sequences = lax.all_gather(sequence_stack, "col", axis=1, tiled=True)
    root_row = col_index * n_row // n_col
    offset = col_index * piece_columns - root_row * piece_rows
    column_piece = lax.dynamic_slice_in_dim(entire_sequences, offset, piece_columns, 1)
    whole_cols = from_root(column_piece, "row", root_row)
    opm_rows = standardize_features(entire_sequences, tensor_scale).astype(jnp.bfloat16)
    opm_cols = standardize_features(whole_cols, tensor_scale).astype(jnp.bfloat16)
    left_projection = (
        jnp.dot(opm_rows, tensor_entry_matrix[:, :hidden], preferred_element_type=jnp.float32)
        * row_softmax_weight[:, None, None]
    ).astype(jnp.bfloat16)
    right_proj = (
        jnp.dot(opm_cols, tensor_entry_matrix[:, hidden:], preferred_element_type=jnp.float32)
        * row_softmax_weight[:, None, None]
    ).astype(jnp.bfloat16)
    outer_sum = jnp.einsum(
        "sic,sjd->ijcd", left_projection, right_proj, preferred_element_type=jnp.float32
    )
    outer_sum = outer_sum.reshape(piece_rows, piece_columns, hidden * hidden)
    out_float = tensor_final_matrix.astype(jnp.float32)
    outer_share = lax.psum_scatter(outer_sum, "depth", scatter_dimension=0, tiled=True)
    share_rows = outer_share.shape[0]
    pair_share = lax.dynamic_slice_in_dim(couple_state, depth_position * share_rows, share_rows, 0)
    update = (
        jnp.dot(outer_share, out_float, precision=lax.Precision.HIGHEST) / (row_count + 0.001)
        + tensor_offset
    )
    new_share = (pair_share.astype(jnp.float32) + update).astype(jnp.bfloat16)
    pair_one = lax.all_gather(new_share, "depth", axis=0, tiled=True)
    row_tokens = lax.dynamic_slice_in_dim(token_weight, row_index * piece_rows, piece_rows)
    col_tokens = lax.dynamic_slice_in_dim(token_weight, col_index * piece_columns, piece_columns)
    logits = jnp.einsum(
        "ijc,ch->ijh",
        standardize_features(pair_one, mean_couple_scale),
        mean_score_matrix,
        precision=lax.Precision.HIGHEST,
    )
    logits = logits + 1000000000.0 * (col_tokens - 1.0)[None, :, None]
    peak = lax.pmax(jnp.max(logits, axis=1), "col")
    expo = jnp.exp(logits - peak[:, None, :])
    total = lax.psum(jnp.sum(expo, axis=1), "col")
    weights = (expo / total[:, None, :]).astype(jnp.bfloat16)
    col_normed = standardize_features(whole_cols, mean_sequence_scale).astype(jnp.bfloat16)
    value_rows = jnp.dot(
        col_normed, mean_content_matrix, preferred_element_type=jnp.float32
    ).astype(jnp.bfloat16)
    value_rows = value_rows.reshape(sequence_count, piece_columns, head_split, head_channels)
    averaged_values = jnp.einsum(
        "ijh,sjhe->sihe", weights, value_rows, preferred_element_type=jnp.float32
    )
    averaged_values = averaged_values.reshape(
        sequence_count, piece_rows, head_split * head_channels
    )
    output_weight = mean_final_matrix.astype(jnp.float32)
    local_portion = lax.psum_scatter(
        averaged_values.astype(jnp.bfloat16), "col", scatter_dimension=1, tiled=True
    ).astype(jnp.float32)
    shard_standardized = standardize_features(sequence_stack, mean_sequence_scale).astype(
        jnp.bfloat16
    )
    gate_values = jax.nn.sigmoid(
        jnp.dot(shard_standardized, mean_sigmoid_matrix, preferred_element_type=jnp.float32)
    )
    sequence_delta = jnp.dot(
        gate_values * local_portion, output_weight, precision=lax.Precision.HIGHEST
    )
    revised_sequences = (sequence_stack.astype(jnp.float32) + sequence_delta).astype(jnp.bfloat16)
    tri_normed = standardize_features(pair_one, trimul_scale).astype(jnp.bfloat16)
    projected = jnp.dot(tri_normed, trimul_entry_matrix, preferred_element_type=jnp.float32)
    pair_mask = (row_tokens[:, None] * col_tokens[None, :])[..., None]
    tri_left = (
        jax.nn.sigmoid(projected[..., 0:width]) * projected[..., width : 2 * width] * pair_mask
    ).astype(jnp.bfloat16)
    tri_right = (
        jax.nn.sigmoid(projected[..., 2 * width : 3 * width])
        * projected[..., 3 * width : 4 * width]
        * pair_mask
    ).astype(jnp.bfloat16)
    out_gate = jax.nn.sigmoid(projected[..., 4 * width : 5 * width])
    left_rows, right_rows = (
        lax.all_gather(tri_left, "col", axis=1, tiled=True),
        lax.all_gather(tri_right, "col", axis=1, tiled=True),
    )
    right_piece = lax.dynamic_slice_in_dim(right_rows, offset, piece_columns, 0)
    right_needed = from_root(right_piece, "row", root_row)
    product = jnp.einsum(
        "ikc,jkc->ijc", left_rows, right_needed, preferred_element_type=jnp.float32
    )
    final = out_gate * jnp.dot(
        standardize_features(product, trimul_result_scale).astype(jnp.bfloat16),
        trimul_final_matrix,
        preferred_element_type=jnp.float32,
    )
    pair_output = (pair_one.astype(jnp.float32) + final).astype(jnp.bfloat16)
    return (revised_sequences, pair_output)


def solution(mesh):
    placed = (
        P("depth", ("row", "col"), None),
        P(),
        P(),
        P("row", "col", None),
        P(),
        P(),
        P(),
        P(),
        P(),
        P(),
        P(),
        P(),
        P(),
        P(),
        P(),
        P(),
        P(),
        P(),
    )
    return jax.shard_map(
        on_device,
        mesh=mesh,
        in_specs=placed,
        out_specs=(P("depth", ("row", "col"), None), P("row", "col", None)),
        check_vma=False,
    )
```

profile of v0, /device:TPU:0, one launch (start us, length us, event | category | flops | bytes accessed | tf_op | source)
XLA Modules:
  0.0 226.4 jit_solution(14383358346844943532)
XLA Ops:
  7.3 16.6 %all_gather.12 = bf16[128,24,64]{0,2,1:T(8,128)(2,1)S(1)} all-gather(bf16[128,6,64]{0,2,1:T(8,128)(2,1)} %param.18), channel_id=1, replica_groups=mesh['row'=4,'col'=4,'depth'=2] {'col'}, dimensions={1}, use_global_device_ids=true | all-gather | bytes 491520 | tf_op jit(solution)/shard_map/all_gather | solution.py:58
  25.4 45.3 %all-reduce.3.cloned.1.call-done = bf16[128,24,64]{0,2,1:T(8,128)(2,1)} async-done(((bf16[128,24,64]{0,2,1:T(8,128)(2,1)}), bf16[128,24,64]{0,2,1:T(8,128)(2,1)}) %all-reduce.3.cloned.1.call-update) | async-done | bytes 393232 | tf_op jit(solution)/shard_map/psum | solution.py:11
  70.7 1.1 convert_reduce_fusion.1
  71.8 1.1 fusion.25
  72.9 6.3 %convolution_bitcast_fusion = f32[24,24,32,32]{2,3,0,1:T(8,128)} fusion(bf16[128,24,32,1]{0,2,1,3:T(8,128)(2,1)S(1)} %fusion.8, bf16[128,24,64]{0,2,1:T(8,128)(2,1)} %all-reduce.3.cloned.1.call-done, f32[64]{0:T(128)S(1)} %copy-done.17, f32[128,24]{0,1:T(8,128)S(1)} %add_rsqrt_fusion.3, f32[128,24]{0,1:T(8,128)S(1)} %broadcast_multiply_fusion.4, ...), kind=kOutput, calls=%fused_computation | convolution fusion | flops 164757504 | bytes 2982656 | tf_op jit(solution)/shard_map/sic,sjd->ijcd/dot_general | solution.py:73
  79.2 9.7 %copy.81 = f32[24,24,32,32]{3,2,1,0:T(8,128)} copy(f32[24,24,32,32]{2,3,0,1:T(8,128)} %convolution_bitcast_fusion) | data formatting | bytes 4718592 | tf_op jit(solution)/shard_map/sic,sjd->ijcd/transpose | solution.py:73
  88.8 8.2 %reshape.111 = f32[24,24,1024]{2,1,0:T(8,128)} reshape(f32[24,24,32,32]{3,2,1,0:T(8,128)} %copy.81) | data formatting | bytes 4718592 | tf_op jit(solution)/shard_map/reshape | solution.py:76
  101.0 1.1 copy.95
  102.1 5.2 %reduce-scatter.3.cloned.1.call-done = f32[12,24,1024]{2,1,0:T(8,128)} async-done(((f32[24,24,1024]{2,1,0:T(8,128)}), f32[12,24,1024]{2,1,0:T(8,128)}) %reduce-scatter.3.cloned.1.call-update) | async-done | bytes 1179664 | tf_op jit(solution)/shard_map/reduce_scatter | solution.py:78
  107.3 1.9 fusion.13
  109.3 1.9 all_gather.13
  112.2 1.1 copy-done.2
  114.1 17.5 %all_gather.14 = bf16[24,96,128]{2,1,0:T(8,128)(2,1)S(1)} all-gather(bf16[24,24,128]{2,1,0:T(8,128)(2,1)S(1)} %get-tuple-element.5), channel_id=1, replica_groups=mesh['row'=4,'col'=4,'depth'=2] {'col'}, dimensions={1}, use_global_device_ids=true | all-gather | bytes 737280 | tf_op jit(solution)/shard_map/all_gather | solution.py:139
  132.6 1.7 fusion.99
  134.3 18.7 %pmax.7 = f32[24,8]{1,0:T(8,128)S(1)} all-reduce(f32[24,8]{1,0:T(8,128)S(1)} %get-tuple-element.7), channel_id=1, replica_groups=mesh['row'=4,'col'=4,'depth'=2] {'col'}, use_global_device_ids=true, to_apply=%region_12.13 | all-reduce | flops 192 | bytes 1536 | tf_op jit(solution)/shard_map/pmax | solution.py:96
  153.2 15.6 %psum.22 = f32[24,8]{1,0:T(8,128)S(1)} all-reduce(f32[24,8]{1,0:T(8,128)S(1)} %fusion.85), channel_id=1, replica_groups=mesh['row'=4,'col'=4,'depth'=2] {'col'}, use_global_device_ids=true, to_apply=%region_14.15 | all-reduce | flops 192 | bytes 1536 | tf_op jit(solution)/shard_map/psum | solution.py:98
  169.5 1.9 copy.85
  172.9 15.2 %all_gather.15 = bf16[24,96,128]{2,1,0:T(8,128)(2,1)S(1)} all-gather(bf16[24,24,128]{2,1,0:T(8,128)(2,1)S(1)} %copy-done.5), channel_id=1, replica_groups=mesh['row'=4,'col'=4,'depth'=2] {'col'}, dimensions={1}, use_global_device_ids=true | all-gather | bytes 737280 | tf_op jit(solution)/shard_map/all_gather | solution.py:138
  188.6 1.5 copy.86
  190.1 1.2 bitcast_reduce_fusion
  192.3 2.0 fusion.7
  194.3 22.9 %reduce-scatter.5.cloned.1.call-done = bf16[128,6,256]{2,0,1:T(8,128)(2,1)} async-done(((bf16[128,24,256]{2,0,1:T(8,128)(2,1)}), bf16[128,6,256]{2,0,1:T(8,128)(2,1)}) %reduce-scatter.5.cloned.1.call-update) | async-done | bytes 393232 | tf_op jit(solution)/shard_map/reduce_scatter | solution.py:112
  217.2 1.5 fusion.3
  218.7 1.2 fusion.10
  (99 shorter events, 11.3 us)
Async XLA Ops:
  7.2 100.1 %copy-start = (bf16[1024,128]{1,0:T(8,128)(2,1)S(1)}, bf16[1024,128]{1,0:T(8,128)(2,1)}, u32[]{:S(2)}) copy-start(bf16[1024,128]{1,0:T(8,128)(2,1)} %param.24) | copy-start | bytes 786436
  7.2 17.8 %copy-start.16 = (s32[256]{0:T(256)S(1)}, s32[256]{0:T(256)}, u32[]{:S(2)}) copy-start(s32[256]{0:T(256)} %param.19) | copy-start | bytes 3076
  7.2 17.9 %copy-start.17 = (f32[64]{0:T(128)S(1)}, f32[64]{0:T(128)}, u32[]{:S(2)}) copy-start(f32[64]{0:T(128)} %param.22) | copy-start | bytes 772
  7.2 17.9 %copy-start.12 = (bf16[64,64]{1,0:T(8,128)(2,1)S(1)}, bf16[64,64]{1,0:T(8,128)(2,1)}, u32[]{:S(2)}) copy-start(bf16[64,64]{1,0:T(8,128)(2,1)} %param.23) | copy-start | bytes 24580
  7.2 63.5 %all-reduce.3.cloned.1.call-start = ((), (), s32[]{:S(2)}) async-start(), calls=%async_computation.2 | async-start | bytes 786432 | tf_op jit(solution)/shard_map/psum | solution.py:11
  24.7 82.6 %reduce-scatter.3.cloned.1.call-start = ((), (), s32[]{:S(2)}) async-start(), calls=%async_computation.3 | async-start | bytes 3538944 | tf_op jit(solution)/shard_map/reduce_scatter | solution.py:78
  97.0 3.2 %copy-start.1 = (bf16[128,24,64]{0,2,1:T(8,128)(2,1)S(1)}, bf16[128,24,64]{0,2,1:T(8,128)(2,1)}, u32[]{:S(2)}) copy-start(bf16[128,24,64]{0,2,1:T(8,128)(2,1)} %all-reduce.3.cloned.1.call-done) | copy-start | bytes 1179652
  97.0 3.2 %copy-start.10 = (bf16[64,256]{1,0:T(8,128)(2,1)S(1)}, bf16[64,256]{1,0:T(8,128)(2,1)}, u32[]{:S(2)}) copy-start(bf16[64,256]{1,0:T(8,128)(2,1)} %param.29) | copy-start | bytes 98308
  97.0 3.2 %copy-start.18 = (f32[64]{0:T(128)S(1)}, f32[64]{0:T(128)}, u32[]{:S(2)}) copy-start(f32[64]{0:T(128)} %param.26) | copy-start | bytes 772
  97.0 91.6 %all-reduce.5.cloned.1.call-start = ((), (), s32[]{:S(2)}) async-start(), calls=%async_computation.5 | async-start | bytes 1179648 | tf_op jit(solution)/shard_map/psum | solution.py:11
  100.9 6.4 %copy-start.9 = (bf16[24,24,128]{2,1,0:T(8,128)(2,1)S(1)}, bf16[24,24,128]{2,1,0:T(8,128)(2,1)}, u32[]{:S(2)}) copy-start(bf16[24,24,128]{2,1,0:T(8,128)(2,1)} %param.21) | copy-start | bytes 442372
  102.1 9.5 %copy-start.6 = (bf16[128,640]{1,0:T(8,128)(2,1)S(1)}, bf16[128,640]{1,0:T(8,128)(2,1)}, u32[]{:S(2)}) copy-start(bf16[128,640]{1,0:T(8,128)(2,1)} %param.33) | copy-start | bytes 491524
  102.1 9.5 %copy-start.21 = (f32[128]{0:T(128)S(1)}, f32[128]{0:T(128)}, u32[]{:S(2)}) copy-start(f32[128]{0:T(128)} %param.32) | copy-start | bytes 1540
  109.3 4.0 %copy-start.8 = (f32[24,24]{1,0:T(8,128)S(1)}, f32[24,24]{1,0:T(8,128)}, u32[]{:S(2)}) copy-start(f32[24,24]{1,0:T(8,128)} %broadcast_multiply_fusion) | copy-start | bytes 6916
  114.1 18.4 %copy-start.20 = (f32[24]{0:T(128)S(1)}, f32[24]{0:T(128)}, u32[]{:S(2)}) copy-start(f32[24]{0:T(128)} %get-tuple-element.2) | copy-start | bytes 292
  114.1 18.5 %copy-start.24 = (f32[128,8]{0,1:T(8,128)S(1)}, f32[128,8]{0,1:T(8,128)}, u32[]{:S(2)}) copy-start(f32[128,8]{0,1:T(8,128)} %param.28) | copy-start | bytes 12292
  114.1 18.5 %copy-start.26 = (f32[128]{0:T(128)S(1)}, f32[128]{0:T(128)}, u32[]{:S(2)}) copy-start(f32[128]{0:T(128)} %param.27) | copy-start | bytes 1540
  132.5 84.7 %reduce-scatter.5.cloned.1.call-start = ((), (), s32[]{:S(2)}) async-start(), calls=%async_computation.4 | async-start | bytes 1966080 | tf_op jit(solution)/shard_map/reduce_scatter | solution.py:112
  191.7 25.5 %copy-start.4 = (bf16[128,6,64]{0,2,1:T(8,128)(2,1)S(1)}, bf16[128,6,64]{0,2,1:T(8,128)(2,1)}, u32[]{:S(2)}) copy-start(bf16[128,6,64]{0,2,1:T(8,128)(2,1)} %param.18) | copy-start | bytes 294916
  191.8 25.5 %copy-start.14 = (f32[128,6]{0,1:T(8,128)S(1)}, f32[128,6]{0,1:T(8,128)}, u32[]{:S(2)}) copy-start(f32[128,6]{0,1:T(8,128)} %copy-done.13) | copy-start | bytes 9220
  191.8 25.5 %copy-start.15 = (f32[128,6]{0,1:T(8,128)S(1)}, f32[128,6]{0,1:T(8,128)}, u32[]{:S(2)}) copy-start(f32[128,6]{0,1:T(8,128)} %add_rsqrt_fusion.4) | copy-start | bytes 9220
  191.8 25.5 %copy-start.19 = (f32[64]{0:T(128)S(1)}, f32[64]{0:T(128)}, u32[]{:S(2)}) copy-start(f32[64]{0:T(128)} %param.26) | copy-start | bytes 772
  191.8 25.4 %copy-start.23 = (bf16[64,256]{1,0:T(8,128)(2,1)S(1)}, bf16[64,256]{1,0:T(8,128)(2,1)}, u32[]{:S(2)}) copy-start(bf16[64,256]{1,0:T(8,128)(2,1)} %param.30) | copy-start | bytes 98308
  194.3 24.4 %copy-start.11 = (bf16[256,64]{0,1:T(8,128)(2,1)S(1)}, bf16[256,64]{0,1:T(8,128)(2,1)}, u32[]{:S(2)}) copy-start(bf16[256,64]{0,1:T(8,128)(2,1)} %param.31) | copy-start | bytes 98308
  (8 other events, 7.8 us)
Sparse Core Ops, SparseCore 0:
  24.8 45.8 all-reduce.2
  97.2 10.0 reduce-scatter.2
  132.6 46.8 all-reduce.4
  181.8 35.4 reduce-scatter.4
where the time goes:
time: 227 us; the launch traced here: 226 us
  blocking collectives  85.5 us (38%)
  waiting for transfers between devices  73.5 us (32%)
  local copies, waits for them, and re-layouts  26.2 us (12%)
  matrix products  17.7 us (8%)
  between operations  14.9 us (7%)
  other arithmetic  8.51 us (4%)
    psum x2, waiting for transfers between devices, from_root(): return lax.psum(jnp.where(mine, array, jnp.zeros_like(array)), axis)  45.3 us
    reduce_scatter x1, waiting for transfers between devices, on_device(): lax.psum_scatter(averaged_values.astype(jnp.bfloat16), 'col', scatter_dim...  22.9 us
    pmax x1, blocking collectives, on_device(): peak = lax.pmax(jnp.max(logits, axis=1), 'col')  18.7 us
    all_gather x1, blocking collectives, on_device(): lax.all_gather(tri_right, 'col', axis=1, tiled=True)  17.5 us
    all_gather x1, blocking collectives, on_device(): entire_sequences = lax.all_gather(sequence_stack, 'col', axis=1, tiled=True)  16.6 us
    psum x1, blocking collectives, on_device(): total = lax.psum(jnp.sum(expo, axis=1), 'col')  15.6 us
    all_gather x1, blocking collectives, on_device(): lax.all_gather(tri_left, 'col', axis=1, tiled=True)  15.2 us
    transpose x1, local copies, waits for them, and re-layouts, on_device(): jnp.einsum('sic,sjd->ijcd', left_projection, right_proj, preferred_elemen...  9.65 us
  transfers between devices with their start and end apart: 4, of which 3 were waited for; matrix products, arithmetic and copies ran while one was open for 7% of the time, Pallas kernels for 0%

commit v1 on v0

--- a/solution.py
+++ b/solution.py
@@ -4,6 +4,8 @@
 from jax.sharding import PartitionSpec as P
 
 epsilon = 1e-05
+bf16 = jnp.bfloat16
+f32 = jnp.float32
 
 
 def from_root(array, axis, root):
@@ -19,7 +21,7 @@
     return centred * lax.rsqrt(variance + epsilon) * scale
 
 
-def on_device(
+def on_device_generic(
     sequence_stack,
     present_sequence_flags,
     genuine_residue_flags,
@@ -152,29 +154,228 @@
     return (revised_sequences, pair_output)
 
 
+def split_pieces(value, count):
+    pieces = []
+    for _ in range(count):
+        piece = lax.reduce_precision(value, 8, 7)
+        pieces.append(piece.astype(bf16))
+        value = value - piece
+    return pieces
+
+
+def factor_stage(tokens, flags, scale, entry):
+    value = tokens.astype(f32)
+    average = jnp.mean(value, 1, keepdims=True)
+    centred = value - average
+    variance = jnp.mean(centred * centred, 1, keepdims=True)
+    normed = (centred * lax.rsqrt(variance + epsilon) * scale[None, :, None]).astype(bf16)
+    factors = jnp.einsum("tcs,cf->tfs", normed, entry, preferred_element_type=f32)
+    return (factors * flags[None, None, :]).astype(bf16)
+
+
+def outer_stage(left, right, final):
+    n, t, hidden, s = left.shape
+    outer = jnp.einsum(
+        "ics,jds->ijcd",
+        left.reshape(n * t, hidden, s),
+        right.reshape(n * t, hidden, s),
+        preferred_element_type=f32,
+    ).reshape(n * t * n * t, hidden * hidden)
+    high = outer.astype(bf16)
+    low = (outer - high.astype(f32)).astype(bf16)
+    update = jnp.dot(high, final, preferred_element_type=f32) + jnp.dot(
+        low, final, preferred_element_type=f32
+    )
+    return update.reshape(n * t, n * t, -1)
+
+
+def pair_stage(update, couple, inverse, offset, row_tokens, col_tokens, couple_scale, score, tri_scale, entry, half, parts):
+    rows, cols, width = couple.shape
+    pair_one = (couple.astype(f32) + update * inverse + offset).astype(bf16)
+    value = pair_one.astype(f32)
+    average = jnp.mean(value, -1, keepdims=True)
+    centred = value - average
+    variance = jnp.mean(centred * centred, -1, keepdims=True)
+    unit = centred * lax.rsqrt(variance + epsilon)
+    logits = jnp.einsum("ijc,ch->ihj", unit * couple_scale, score, precision=lax.Precision.HIGHEST)
+    logits = logits + 1000000000.0 * (col_tokens - 1.0)[None, None, :]
+    peak = jnp.max(logits, -1)
+    expo = jnp.exp(logits - peak[..., None]).astype(bf16).reshape(rows, -1)
+    normed = (unit * tri_scale).astype(bf16)
+    mine = lax.dynamic_slice_in_dim(
+        entry[:, : 4 * width].reshape(width, 4, 2, width // 2), half, 1, 2
+    ).reshape(width, 2 * width)
+    projected = jnp.einsum("ijz,zc->cij", normed, mine, preferred_element_type=f32)
+    projected = projected.reshape(4, width // 2, rows, cols)
+    mask = (row_tokens[:, None] * col_tokens[None, :])[None]
+    left = (jax.nn.sigmoid(projected[0]) * projected[1] * mask).astype(bf16)
+    right = (jax.nn.sigmoid(projected[2]) * projected[3] * mask).astype(bf16)
+
+    def by_peer(operand):
+        operand = operand.reshape(parts, -1, rows, cols)
+        return operand.transpose(0, 2, 1, 3).reshape(parts, rows, -1)
+
+    left, right = by_peer(left), by_peer(right)
+    spare = 128 - left.shape[-1]
+
+    def everyone(piece):
+        return jnp.broadcast_to(piece[None], (parts,) + piece.shape)
+
+    stats = jnp.concatenate(split_pieces(peak, 3), -1)
+    lanes = stats.shape[-1]
+    stats = stats.reshape(rows // 8, 8, lanes).transpose(1, 0, 2).reshape(8, -1)
+    stats = jnp.pad(stats, ((0, 0), (0, 128 - stats.shape[-1])))
+    block = jnp.concatenate(
+        [
+            jnp.concatenate([left, everyone(expo[:, 128 : 128 + spare])], -1),
+            jnp.concatenate([right, everyone(expo[:, 128 + spare : 128 + 2 * spare])], -1),
+            everyone(expo[:, :128]),
+            everyone(stats),
+        ],
+        1,
+    )
+    return pair_one, block
+
+
+def middle_stage(block, n, rows, cols, heads, seq_scale, content, sigmoid_matrix, final):
+    parts = n * n
+    ch = final.shape[1]
+    feats = 128 // cols - (1 if (128 // cols) * cols > 96 else 0)
+    left = block[:, :rows]
+    right = block[:, rows : 2 * rows]
+    expo = jnp.concatenate([block[:, 2 * rows : 3 * rows], left[..., feats * cols :], right[..., feats * cols :]], -1)
+    stats = block[:, 3 * rows : 3 * rows + 8]
+    slab = block[:, 3 * rows + 8 :]
+
+    def whole(operand):
+        operand = operand[..., : feats * cols].reshape(n, n, rows, feats, cols)
+        return operand.transpose(3, 0, 2, 1, 4).reshape(feats, n * rows, n * cols)
+
+    product = jnp.einsum("fik,fjk->fij", whole(left), whole(right), preferred_element_type=f32)
+    product = product.astype(bf16).reshape(feats, n, rows, n, cols)
+    product = product.transpose(1, 3, 2, 0, 4).reshape(parts, rows, feats * cols)
+    product = jnp.pad(product, ((0, 0), (0, 0), (0, 128 - feats * cols)))
+    stats = stats[..., : rows // 8 * 3 * heads].reshape(parts, 8, rows // 8, 3, heads)
+    peak = stats.astype(f32).sum(3).transpose(0, 2, 1, 3).reshape(n, n, rows, heads)
+    expo = expo.reshape(n, n, rows, heads, cols).astype(f32)
+    top = jnp.max(peak, 1, keepdims=True)
+    factor = jnp.exp(peak - top)
+    total = jnp.sum(factor * jnp.sum(expo, -1), 1, keepdims=True)
+    weights = (expo * (factor / total)[..., None]).astype(bf16)
+    weights = weights.transpose(3, 0, 2, 1, 4).reshape(heads, n * rows, n * cols)
+    groups = slab.shape[1] // 8
+    tokens = slab.reshape(parts, groups, 8, 128 // ch, ch).transpose(2, 0, 1, 3, 4).reshape(8, n * rows, ch)
+    normed = standardize_features(tokens, seq_scale).astype(bf16)
+    values = jnp.dot(normed, content, preferred_element_type=f32).astype(bf16)
+    gates = jax.nn.sigmoid(jnp.dot(normed, sigmoid_matrix, preferred_element_type=f32))
+    values = values.reshape(8, n * rows, heads, -1)
+    averaged = jnp.einsum("hij,sjhe->sihe", weights, values, preferred_element_type=f32)
+    gated = gates * averaged.reshape(8, n * rows, -1)
+    delta = jnp.dot(gated, final.astype(f32), precision=lax.Precision.HIGHEST)
+    revised = (tokens.astype(f32) + delta).astype(bf16)
+    revised = revised.reshape(8, parts, groups, 128 // ch, ch).transpose(1, 2, 0, 3, 4)
+    revised = revised.reshape(parts, groups * 8, 128)
+    return jnp.concatenate([product, revised], 1)
+
+
+def final_stage(product, pair_one, tri_scale, entry, result_scale, final):
+    rows, cols, width = pair_one.shape
+    depth, parts = product.shape[:2]
+    feats = width // (depth * parts)
+    product = product[..., : feats * cols].reshape(depth, parts, rows, feats, cols)
+    product = product.transpose(2, 4, 0, 1, 3).reshape(rows, cols, width)
+    normed = standardize_features(pair_one, tri_scale).astype(bf16)
+    gate = jax.nn.sigmoid(jnp.dot(normed, entry[:, 4 * width :], preferred_element_type=f32))
+    final = gate * jnp.dot(
+        standardize_features(product, result_scale).astype(bf16), final, preferred_element_type=f32
+    )
+    return (pair_one.astype(f32) + final).astype(bf16)
+
+
+def on_device(
+    sequence_stack,
+    present_sequence_flags,
+    genuine_residue_flags,
+    couple_state,
+    tensor_scale,
+    tensor_entry_matrix,
+    tensor_final_matrix,
+    tensor_offset,
+    mean_sequence_scale,
+    mean_couple_scale,
+    mean_score_matrix,
+    mean_content_matrix,
+    mean_sigmoid_matrix,
+    mean_final_matrix,
+    trimul_scale,
+    trimul_entry_matrix,
+    trimul_result_scale,
+    trimul_final_matrix,
+):
+    n = lax.axis_size("row")
+    parts = n * n
+    row_index = lax.axis_index("row")
+    col_index = lax.axis_index("col")
+    half = lax.axis_index("depth")
+    rows, cols, width = couple_state.shape
+    count, t, ch = sequence_stack.shape
+    hidden = tensor_entry_matrix.shape[1] // 2
+    heads = mean_score_matrix.shape[1]
+    token_weight = genuine_residue_flags.astype(f32)
+    flags = present_sequence_flags.astype(f32)
+    inverse = 1.0 / (jnp.sum(flags) + 0.001)
+    my_flags = lax.dynamic_slice_in_dim(flags, half * count, count)
+    tokens = sequence_stack.transpose(1, 2, 0)
+    factors = factor_stage(tokens, my_flags, tensor_scale, tensor_entry_matrix)
+    left, right = factors[:, :hidden], factors[:, hidden:]
+
+    def move(array, where):
+        pairs = [(r * n + c, where(r, c)[0] * n + where(r, c)[1]) for r in range(n) for c in range(n)]
+        return lax.ppermute(array, ("row", "col"), pairs)
+
+    lefts = [left] + [move(left, lambda r, c, k=k: (r, (c + k) % n)) for k in range(1, n)]
+    rights = [move(right, lambda r, c, k=k: ((c + k) % n, r)) for k in range(n)]
+    all_left = jnp.zeros((n,) + left.shape, bf16)
+    all_right = jnp.zeros((n,) + left.shape, bf16)
+    for k in range(n):
+        all_left = lax.dynamic_update_index_in_dim(all_left, lefts[k], (col_index - k) % n, 0)
+        all_right = lax.dynamic_update_index_in_dim(all_right, rights[k], (row_index - k) % n, 0)
+    update = outer_stage(all_left, all_right, tensor_final_matrix)
+    update = update + lax.ppermute(update, "depth", [(0, 1), (1, 0)])
+    row_tokens = lax.dynamic_slice_in_dim(token_weight, row_index * rows, rows)
+    col_tokens = lax.dynamic_slice_in_dim(token_weight, col_index * cols, cols)
+    pair_one, block = pair_stage(
+        update, couple_state, inverse, tensor_offset, row_tokens, col_tokens, mean_couple_scale,
+        mean_score_matrix, trimul_scale, trimul_entry_matrix, half, parts,
+    )
+    slab = sequence_stack.reshape(parts, 8, t * ch // 128, 128).transpose(0, 2, 1, 3)
+    slab = slab.reshape(parts, -1, 128)
+    block = lax.all_to_all(jnp.concatenate([block, slab], 1), ("row", "col"), 0, 0, tiled=True)
+    block = middle_stage(
+        block, n, rows, cols, heads, mean_sequence_scale, mean_content_matrix, mean_sigmoid_matrix,
+        mean_final_matrix,
+    )
+    block = lax.all_to_all(block, ("row", "col"), 0, 0, tiled=True)
+    product = block[:, :rows]
+    other = lax.ppermute(product, "depth", [(0, 1), (1, 0)])
+    first = half == 0
+    product = jnp.stack([jnp.where(first, product, other), jnp.where(first, other, product)])
+    revised = block[:, rows:].reshape(parts, t * ch // 128, 8, 128).transpose(0, 2, 1, 3)
+    revised = revised.reshape(count, t, ch)
+    pair_output = final_stage(
+        product, pair_one, trimul_scale, trimul_entry_matrix, trimul_result_scale, trimul_final_matrix
+    )
+    return (revised, pair_output)
+
+
+def suits(mesh):
+    return mesh.shape["row"] == mesh.shape["col"] and mesh.shape["depth"] == 2
+
+
 def solution(mesh):
-    placed = (
-        P("depth", ("row", "col"), None),
-        P(),
-        P(),
-        P("row", "col", None),
-        P(),
-        P(),
-        P(),
-        P(),
-        P(),
-        P(),
-        P(),
-        P(),
-        P(),
-        P(),
-        P(),
-        P(),
-        P(),
-        P(),
-    )
+    placed = (P("depth", ("row", "col"), None), P(), P(), P("row", "col", None)) + (P(),) * 14
     return jax.shard_map(
-        on_device,
+        on_device if suits(mesh) else on_device_generic,
         mesh=mesh,
         in_specs=placed,
         out_specs=(P("depth", ("row", "col"), None), P("row", "col", None)),

time: 227 us -> 115 us (0.51)
  blocking collectives: 85.5 us -> 18.2 us
  waiting for transfers between devices: 73.5 us -> 14.4 us
  starting transfers between devices: 0.16 us -> 20.7 us
  between operations: 14.9 us -> 2.43 us
  local copies, waits for them, and re-layouts: 26.2 us -> 32 us
  matrix products: 17.7 us -> 13.8 us
  other arithmetic: 8.51 us -> 12.1 us
    all_gather x4 -> x0, blocking collectives: 51.2 us -> none  [the longest x1 17.5 us: on_device(): lax.all_gather(tri_right, 'col', axis=1, tiled=True)]
    psum x2 -> x0, waiting for transfers between devices: 45.3 us -> none  [from_root(): return lax.psum(jnp.where(mine, array, jnp.zeros_like(array)), axis)]
    reduce_scatter x2 -> x0, waiting for transfers between devices: 28.1 us -> none  [the longest x1 22.9 us: on_device(): lax.psum_scatter(averaged_values.astype(jnp.bfloat16), 'col', scatter_dim...]
    pmax x1 -> x0, blocking collectives: 18.7 us -> none  [on_device(): peak = lax.pmax(jnp.max(logits, axis=1), 'col')]
    all_to_all x0 -> x1, blocking collectives: none -> 18.2 us  [on_device(): lax.all_to_all(jnp.concatenate([block, slab], 1), ('row', 'col'), 0, 0, t...]
    ppermute x0 -> x9, starting transfers between devices: none -> 16.9 us  [the longest x7 16.8 us: move(): return lax.ppermute(array, ('row', 'col'), pairs)]
    psum x1 -> x0, blocking collectives: 15.6 us -> none  [on_device(): total = lax.psum(jnp.sum(expo, axis=1), 'col')]
    all_to_all x0 -> x1, waiting for transfers between devices: none -> 8.35 us  [on_device(): block = lax.all_to_all(block, ('row', 'col'), 0, 0, tiled=True)]
  transfers between devices with their start and end apart: 4 -> 10, of which waited for: 3 -> 4; matrix products, arithmetic and copies ran while one was open for 7% -> 4% of each run, Pallas kernels for 0% -> 0%
where the time goes in v1:
time: 115 us; the launch traced here: 114 us
  local copies, waits for them, and re-layouts  32 us (28%)
  starting transfers between devices  20.7 us (18%)
  blocking collectives  18.2 us (16%)
  waiting for transfers between devices  14.4 us (13%)
  matrix products  13.8 us (12%)
  other arithmetic  12.1 us (11%)
  between operations  2.43 us (2%)
    all_to_all x1, blocking collectives, on_device(): lax.all_to_all(jnp.concatenate([block, slab], 1), ('row', 'col'), 0, 0, t...  18.2 us
    ppermute x7, starting transfers between devices, move(): return lax.ppermute(array, ('row', 'col'), pairs)  16.8 us
    transpose x1, local copies, waits for them, and re-layouts, outer_stage(): jnp.einsum('ics,jds->ijcd', left.reshape(n * t, hidden, s), right.reshape...  9.61 us
    all_to_all x1, waiting for transfers between devices, on_device(): block = lax.all_to_all(block, ('row', 'col'), 0, 0, tiled=True)  8.35 us
    reshape x1, local copies, waits for them, and re-layouts, outer_stage(): outer = jnp.einsum('ics,jds->ijcd', left.reshape(n * t, hidden, s), right...  7.18 us
    dot_general x1, matrix products, outer_stage(): jnp.einsum('ics,jds->ijcd', left.reshape(n * t, hidden, s), right.reshape...  5.03 us
    ppermute x7, waiting for transfers between devices, move(): return lax.ppermute(array, ('row', 'col'), pairs)  4.66 us
    all_to_all x1, starting transfers between devices, on_device(): block = lax.all_to_all(block, ('row', 'col'), 0, 0, tiled=True)  3.74 us
  transfers between devices with their start and end apart: 10, of which 4 were waited for; matrix products, arithmetic and copies ran while one was open for 4% of the time, Pallas kernels for 0%

profile of v1, /device:TPU:0, one launch (start us, length us, event | category | flops | bytes accessed | tf_op | source)
XLA Modules:
  0.0 113.7 jit_solution(3794289611005770110)
XLA Ops:
  1.4 0.9 bitcast_reduce_fusion
  2.3 0.9 fusion.45
  3.4 1.2 %fusion.16 = bf16[6,64,128]{2,1,0:T(8,128)(2,1)S(1)} fusion(bf16[128,6,64]{0,2,1:T(8,128)(2,1)} %param.18, f32[128]{0:T(128)S(1)} %dynamic_slice.13, f32[64]{0:T(128)} %param.22, f32[6,128]{1,0:T(8,128)S(1)} %add_rsqrt_fusion.3, f32[6,128]{1,0:T(8,128)S(1)} %broadcast_multiply_fusion.4, bf16[64,64]{1,0:T(8,128)(2,1)} %param.23), kind=kOutput, calls=%fused_computation.29 | convolution fusion | flops 6635520 | bytes 211712 | tf_op jit(solution)/shard_map/tcs,cf->tfs/dot_general | solution.py:172
  4.5 3.1 %collective-permute-start.4 = (bf16[6,32,128]{2,1,0:T(8,128)(2,1)S(1)}, bf16[6,32,128]{2,1,0:T(8,128)(2,1)S(1)}, u32[]{:S(2)}, u32[]{:S(2)}) collective-permute-start(bf16[6,32,128]{2,1,0:T(8,128)(2,1)S(1)} %get-tuple-element.27), channel_id=1, source_target_pairs={{0,2},{2,4},{4,6},{6,0},{8,10},{10,12},{12,14},{14,8},{16,18},{18,... | collective-permute-start | bytes 147464 | tf_op jit(solution)/shard_map/ppermute | solution.py:334
  7.7 2.6 %collective-permute-start.5 = (bf16[6,32,128]{2,1,0:T(8,128)(2,1)S(1)}, bf16[6,32,128]{2,1,0:T(8,128)(2,1)S(1)}, u32[]{:S(2)}, u32[]{:S(2)}) collective-permute-start(bf16[6,32,128]{2,1,0:T(8,128)(2,1)S(1)} %get-tuple-element.27), channel_id=1, source_target_pairs={{0,4},{2,6},{4,0},{6,2},{8,12},{10,14},{12,8},{14,10},{16,20},{18,... | collective-permute-start | bytes 147464 | tf_op jit(solution)/shard_map/ppermute | solution.py:334
  10.2 1.3 %collective-permute-start.6 = (bf16[6,32,128]{2,1,0:T(8,128)(2,1)S(1)}, bf16[6,32,128]{2,1,0:T(8,128)(2,1)S(1)}, u32[]{:S(2)}, u32[]{:S(2)}) collective-permute-start(bf16[6,32,128]{2,1,0:T(8,128)(2,1)S(1)} %get-tuple-element.27), channel_id=1, source_target_pairs={{0,6},{2,0},{4,2},{6,4},{8,14},{10,8},{12,10},{14,12},{16,22},{18,... | collective-permute-start | bytes 147464 | tf_op jit(solution)/shard_map/ppermute | solution.py:334
  12.3 3.4 %collective-permute-start.1 = (bf16[6,32,128]{2,1,0:T(8,128)(2,1)S(1)}, bf16[6,32,128]{2,1,0:T(8,128)(2,1)S(1)}, u32[]{:S(2)}, u32[]{:S(2)}) collective-permute-start(bf16[6,32,128]{2,1,0:T(8,128)(2,1)S(1)} %get-tuple-element.28), channel_id=1, source_target_pairs={{0,8},{2,16},{4,24},{6,0},{8,10},{10,18},{12,26},{14,2},{16,12},{1... | collective-permute-start | bytes 147464 | tf_op jit(solution)/shard_map/ppermute | solution.py:334
  15.7 0.9 slice.75
  18.6 3.4 %collective-permute-start.2 = (bf16[6,32,128]{2,1,0:T(8,128)(2,1)S(1)}, bf16[6,32,128]{2,1,0:T(8,128)(2,1)S(1)}, u32[]{:S(2)}, u32[]{:S(2)}) collective-permute-start(bf16[6,32,128]{2,1,0:T(8,128)(2,1)S(1)} %get-tuple-element.28), channel_id=1, source_target_pairs={{0,16},{2,24},{4,0},{6,8},{8,18},{10,26},{12,2},{14,10},{16,20},{1... | collective-permute-start | bytes 147464 | tf_op jit(solution)/shard_map/ppermute | solution.py:334
  22.0 2.3 %collective-permute-start.3 = (bf16[6,32,128]{2,1,0:T(8,128)(2,1)S(1)}, bf16[6,32,128]{2,1,0:T(8,128)(2,1)S(1)}, u32[]{:S(2)}, u32[]{:S(2)}) collective-permute-start(bf16[6,32,128]{2,1,0:T(8,128)(2,1)S(1)} %get-tuple-element.28), channel_id=1, source_target_pairs={{0,24},{2,0},{4,8},{6,16},{8,26},{10,2},{12,10},{14,18},{16,28},{1... | collective-permute-start | bytes 147464 | tf_op jit(solution)/shard_map/ppermute | solution.py:334
  25.1 3.9 %collective-permute-done.3 = bf16[6,32,128]{2,1,0:T(8,128)(2,1)S(1)} collective-permute-done((bf16[6,32,128]{2,1,0:T(8,128)(2,1)S(1)}, bf16[6,32,128]{2,1,0:T(8,128)(2,1)S(1)}, u32[]{:S(2)}, u32[]{:S(2)}) %collective-permute-start.3) | collective-permute-done | bytes 49184 | tf_op jit(solution)/shard_map/ppermute | solution.py:334
  29.1 5.0 %convolution_bitcast_fusion = f32[24,24,32,32]{2,3,0,1:T(8,128)} fusion(bf16[24,32,128,1]{2,1,3,0:T(8,128)(2,1)S(1)} %bitcast.166, bf16[24,32,128,1]{2,1,0,3:T(8,128)(2,1)S(1)} %bitcast.165), kind=kOutput, calls=%fused_computation | convolution fusion | flops 150994944 | bytes 2752512 | tf_op jit(solution)/shard_map/ics,jds->ijcd/dot_general | solution.py:178
  34.1 9.6 %copy.164 = f32[24,24,32,32]{3,2,1,0:T(8,128)} copy(f32[24,24,32,32]{2,3,0,1:T(8,128)} %convolution_bitcast_fusion) | data formatting | bytes 4718592 | tf_op jit(solution)/shard_map/ics,jds->ijcd/transpose | solution.py:178
  43.7 7.2 %reshape.257 = f32[576,1024]{1,0:T(8,128)S(1)} reshape(f32[24,24,32,32]{3,2,1,0:T(8,128)} %copy.164) | data formatting | bytes 4718592 | tf_op jit(solution)/shard_map/reshape | solution.py:183
  52.2 1.4 %collective-permute-done.7 = f32[24,24,128]{2,1,0:T(8,128)S(1)} collective-permute-done((f32[24,24,128]{2,1,0:T(8,128)S(1)}, f32[24,24,128]{2,1,0:T(8,128)S(1)}, u32[]{:S(2)}, u32[]{:S(2)}) %collective-permute-start.7) | collective-permute-done | bytes 294944 | tf_op jit(solution)/shard_map/ppermute | solution.py:344
  54.1 1.7 %fusion.74 = (f32[24,8]{1,0:T(8,128)S(1)}, f32[24,8,24]{2,1,0:T(8,128)S(1)}) fusion(f32[24]{0:T(128)S(1)} %get-tuple-element.12, f32[128,8]{0,1:T(8,128)S(1)} %copy-done.21, bf16[24,24,128]{2,1,0:T(8,128)(2,1)S(1)} %get-tuple-element.15, f32[128]{0:T(128)S(1)} %copy-done.23, f32[24,24]{1,0:T(8,128)S(1)} %add_rsqrt_fusion.2, ...), kind=kOutput, calls=%fused_computation.141 | convolution fusion | flops 7381824 | bytes 175968 | tf_op jit(solution)/shard_map/ijc,ch->ihj/dot_general | solution.py:200
  58.9 18.2 %all_to_all.10 = bf16[16,104,128]{2,1,0:T(8,128)(2,1)S(1)} all-to-all(bf16[16,104,128]{2,1,0:T(8,128)(2,1)S(1)} %bitcast_dynamic-update-slice_fusion), channel_id=1, replica_groups=mesh['row'=4,'col'=4,'depth'=2] {'row','col'}, dimensions={0} | all-to-all | bytes 851968 | tf_op jit(solution)/shard_map/all_to_all | solution.py:353
  81.1 1.2 %copy.189 = f32[16,3,8,8]{2,1,3,0:T(4,128)S(1)} copy(f32[16,3,8,8]{0,3,1,2:T(8,128)} %bitcast.168) | data formatting | bytes 24576 | tf_op jit(solution)/shard_map/transpose | solution.py:259
  84.3 0.9 multiply_reduce_fusion.1
  92.6 3.7 %all-to-all-start.1 = ((bf16[16,48,128]{2,1,0:T(8,128)(2,1)}), bf16[16,48,128]{2,1,0:T(8,128)(2,1)S(1)}, u32[]{:S(2)}, u32[]{:S(2)}) async-start(bf16[16,48,128]{2,1,0:T(8,128)(2,1)} %fusion.40), calls=%async_computation.1 | async-start | bytes 393216 | tf_op jit(solution)/shard_map/all_to_all | solution.py:358
  96.4 8.3 %all-to-all-done.1 = bf16[16,48,128]{2,1,0:T(8,128)(2,1)S(1)} async-done(((bf16[16,48,128]{2,1,0:T(8,128)(2,1)}), bf16[16,48,128]{2,1,0:T(8,128)(2,1)S(1)}, u32[]{:S(2)}, u32[]{:S(2)}) %all-to-all-start.1) | async-done | bytes 196640 | tf_op jit(solution)/shard_map/all_to_all | solution.py:358
  104.8 1.8 %fusion.11 = f32[24,24,128]{2,1,0:T(8,128)} fusion(bf16[24,24,128]{2,1,0:T(8,128)(2,1)S(1)} %get-tuple-element.15, f32[128]{0:T(128)S(1)} %copy-done.19, f32[24,24]{1,0:T(8,128)S(1)} %copy-done.11, f32[24,24]{1,0:T(8,128)S(1)} %copy-done.8, bf16[128,640]{1,0:T(8,128)(2,1)} %param.33), kind=kOutput, calls=%fused_computation.21 | convolution fusion | flops 19464192 | bytes 480256 | tf_op jit(solution)/shard_map/dot_general | solution.py:288
  111.5 1.1 fusion.2
  112.7 1.0 fusion.13
  (177 shorter events, 25.9 us)
Async XLA Ops:
  0.6 50.3 %copy-start = (bf16[1024,128]{1,0:T(8,128)(2,1)S(1)}, bf16[1024,128]{1,0:T(8,128)(2,1)}, u32[]{:S(2)}) copy-start(bf16[1024,128]{1,0:T(8,128)(2,1)} %param.24) | copy-start | bytes 786436
  0.6 16.2 %copy-start.15 = (s32[256]{0:T(256)S(1)}, s32[256]{0:T(256)}, u32[]{:S(2)}) copy-start(s32[256]{0:T(256)} %param.19) | copy-start | bytes 3076
  0.7 16.8 %copy-start.1 = (bf16[128,6,64]{0,2,1:T(8,128)(2,1)S(1)}, bf16[128,6,64]{0,2,1:T(8,128)(2,1)}, u32[]{:S(2)}) copy-start(bf16[128,6,64]{0,2,1:T(8,128)(2,1)} %param.18) | copy-start | bytes 294916
  0.7 17.0 %copy-start.22 = (s32[96]{0:T(128)S(1)}, s32[96]{0:T(128)}, u32[]{:S(2)}) copy-start(s32[96]{0:T(128)} %param.20) | copy-start | bytes 1156
  4.5 14.0 %collective-permute-start.4 = (bf16[6,32,128]{2,1,0:T(8,128)(2,1)S(1)}, bf16[6,32,128]{2,1,0:T(8,128)(2,1)S(1)}, u32[]{:S(2)}, u32[]{:S(2)}) collective-permute-start(bf16[6,32,128]{2,1,0:T(8,128)(2,1)S(1)} %get-tuple-element.27), channel_id=1, source_target_pairs={{0,2},{2,4},{4,6},{6,0},{8,10},{10,12},{12,14},{14,8},{16,18},{18,... | collective-permute-start | bytes 147464 | tf_op jit(solution)/shard_map/ppermute | solution.py:334
  7.7 14.3 %collective-permute-start.5 = (bf16[6,32,128]{2,1,0:T(8,128)(2,1)S(1)}, bf16[6,32,128]{2,1,0:T(8,128)(2,1)S(1)}, u32[]{:S(2)}, u32[]{:S(2)}) collective-permute-start(bf16[6,32,128]{2,1,0:T(8,128)(2,1)S(1)} %get-tuple-element.27), channel_id=1, source_target_pairs={{0,4},{2,6},{4,0},{6,2},{8,12},{10,14},{12,8},{14,10},{16,20},{18,... | collective-permute-start | bytes 147464 | tf_op jit(solution)/shard_map/ppermute | solution.py:334
  10.2 14.0 %collective-permute-start.6 = (bf16[6,32,128]{2,1,0:T(8,128)(2,1)S(1)}, bf16[6,32,128]{2,1,0:T(8,128)(2,1)S(1)}, u32[]{:S(2)}, u32[]{:S(2)}) collective-permute-start(bf16[6,32,128]{2,1,0:T(8,128)(2,1)S(1)} %get-tuple-element.27), channel_id=1, source_target_pairs={{0,6},{2,0},{4,2},{6,4},{8,14},{10,8},{12,10},{14,12},{16,22},{18,... | collective-permute-start | bytes 147464 | tf_op jit(solution)/shard_map/ppermute | solution.py:334
  11.6 12.7 %collective-permute-start = (bf16[6,32,128]{2,1,0:T(8,128)(2,1)S(1)}, bf16[6,32,128]{2,1,0:T(8,128)(2,1)S(1)}, u32[]{:S(2)}, u32[]{:S(2)}) collective-permute-start(bf16[6,32,128]{2,1,0:T(8,128)(2,1)S(1)} %get-tuple-element.28), channel_id=1, source_target_pairs={{0,0},{2,8},{4,16},{6,24},{8,2},{10,10},{12,18},{14,26},{16,4},{18... | collective-permute-start | bytes 147464 | tf_op jit(solution)/shard_map/ppermute | solution.py:334
  12.3 12.1 %collective-permute-start.1 = (bf16[6,32,128]{2,1,0:T(8,128)(2,1)S(1)}, bf16[6,32,128]{2,1,0:T(8,128)(2,1)S(1)}, u32[]{:S(2)}, u32[]{:S(2)}) collective-permute-start(bf16[6,32,128]{2,1,0:T(8,128)(2,1)S(1)} %get-tuple-element.28), channel_id=1, source_target_pairs={{0,8},{2,16},{4,24},{6,0},{8,10},{10,18},{12,26},{14,2},{16,12},{1... | collective-permute-start | bytes 147464 | tf_op jit(solution)/shard_map/ppermute | solution.py:334
  18.6 6.5 %collective-permute-start.2 = (bf16[6,32,128]{2,1,0:T(8,128)(2,1)S(1)}, bf16[6,32,128]{2,1,0:T(8,128)(2,1)S(1)}, u32[]{:S(2)}, u32[]{:S(2)}) collective-permute-start(bf16[6,32,128]{2,1,0:T(8,128)(2,1)S(1)} %get-tuple-element.28), channel_id=1, source_target_pairs={{0,16},{2,24},{4,0},{6,8},{8,18},{10,26},{12,2},{14,10},{16,20},{1... | collective-permute-start | bytes 147464 | tf_op jit(solution)/shard_map/ppermute | solution.py:334
  22.0 7.1 %collective-permute-start.3 = (bf16[6,32,128]{2,1,0:T(8,128)(2,1)S(1)}, bf16[6,32,128]{2,1,0:T(8,128)(2,1)S(1)}, u32[]{:S(2)}, u32[]{:S(2)}) collective-permute-start(bf16[6,32,128]{2,1,0:T(8,128)(2,1)S(1)} %get-tuple-element.28), channel_id=1, source_target_pairs={{0,24},{2,0},{4,8},{6,16},{8,26},{10,2},{12,10},{14,18},{16,28},{1... | collective-permute-start | bytes 147464 | tf_op jit(solution)/shard_map/ppermute | solution.py:334
  51.4 2.2 %copy-start.5 = (bf16[24,24,128]{2,1,0:T(8,128)(2,1)S(1)}, bf16[24,24,128]{2,1,0:T(8,128)(2,1)}, u32[]{:S(2)}) copy-start(bf16[24,24,128]{2,1,0:T(8,128)(2,1)} %param.21) | copy-start | bytes 442372
  51.4 2.2 %copy-start.16 = (f32[128]{0:T(128)S(1)}, f32[128]{0:T(128)}, u32[]{:S(2)}) copy-start(f32[128]{0:T(128)} %param.25) | copy-start | bytes 1540
  51.4 2.7 %copy-start.21 = (f32[128,8]{0,1:T(8,128)S(1)}, f32[128,8]{0,1:T(8,128)}, u32[]{:S(2)}) copy-start(f32[128,8]{0,1:T(8,128)} %param.28) | copy-start | bytes 12292
  51.4 2.7 %copy-start.23 = (f32[128]{0:T(128)S(1)}, f32[128]{0:T(128)}, u32[]{:S(2)}) copy-start(f32[128]{0:T(128)} %param.27) | copy-start | bytes 1540
  51.9 4.4 %copy-start.18 = (f32[128]{0:T(128)S(1)}, f32[128]{0:T(128)}, u32[]{:S(2)}) copy-start(f32[128]{0:T(128)} %param.32) | copy-start | bytes 1540
  51.9 1.6 %collective-permute-start.7 = (f32[24,24,128]{2,1,0:T(8,128)S(1)}, f32[24,24,128]{2,1,0:T(8,128)S(1)}, u32[]{:S(2)}, u32[]{:S(2)}) collective-permute-start(f32[24,24,128]{2,1,0:T(8,128)S(1)} %bitcast.161), channel_id=1, source_target_pairs={{0,1},{1,0},{2,3},{3,2},{4,5},{5,4},{6,7},{7,6},{8,9},{9,8},{10,11... | collective-permute-start | bytes 884744 | tf_op jit(solution)/shard_map/ppermute | solution.py:344
  53.8 3.1 %copy-start.7 = (f32[24,24]{1,0:T(8,128)}, f32[24,24]{1,0:T(8,128)S(1)}, u32[]{:S(2)}) copy-start(f32[24,24]{1,0:T(8,128)S(1)} %broadcast_multiply_fusion.3) | copy-start | bytes 6916
  54.1 2.8 %copy-start.10 = (f32[24,24]{1,0:T(8,128)}, f32[24,24]{1,0:T(8,128)S(1)}, u32[]{:S(2)}) copy-start(f32[24,24]{1,0:T(8,128)S(1)} %add_rsqrt_fusion.2) | copy-start | bytes 6916
  90.9 13.9 %copy-start.8 = (f32[24,24]{1,0:T(8,128)S(1)}, f32[24,24]{1,0:T(8,128)}, u32[]{:S(2)}) copy-start(f32[24,24]{1,0:T(8,128)} %copy-done.7) | copy-start | bytes 6916
  91.0 13.9 %copy-start.11 = (f32[24,24]{1,0:T(8,128)S(1)}, f32[24,24]{1,0:T(8,128)}, u32[]{:S(2)}) copy-start(f32[24,24]{1,0:T(8,128)} %copy-done.10) | copy-start | bytes 6916
  91.0 13.9 %copy-start.19 = (f32[128]{0:T(128)S(1)}, f32[128]{0:T(128)}, u32[]{:S(2)}) copy-start(f32[128]{0:T(128)} %param.32) | copy-start | bytes 1540
  92.6 12.1 %all-to-all-start.1 = ((bf16[16,48,128]{2,1,0:T(8,128)(2,1)}), bf16[16,48,128]{2,1,0:T(8,128)(2,1)S(1)}, u32[]{:S(2)}, u32[]{:S(2)}) async-start(bf16[16,48,128]{2,1,0:T(8,128)(2,1)} %fusion.40), calls=%async_computation.1 | async-start | bytes 393216 | tf_op jit(solution)/shard_map/all_to_all | solution.py:358
  104.7 2.0 %collective-permute-start.8 = (bf16[16,24,128]{2,1,0:T(8,128)(2,1)S(1)}, bf16[16,24,128]{2,1,0:T(8,128)(2,1)S(1)}, u32[]{:S(2)}, u32[]{:S(2)}) collective-permute-start(bf16[16,24,128]{2,1,0:T(8,128)(2,1)S(1)} %slice.113), channel_id=1, source_target_pairs={{0,1},{1,0},{2,3},{3,2},{4,5},{5,4},{6,7},{7,6},{8,9},{9,8},{10,11... | collective-permute-start | bytes 294920 | tf_op jit(solution)/shard_map/ppermute | solution.py:360
  (11 other events, 15.6 us)

commit v2 on v1

--- a/solution.py
+++ b/solution.py
@@ -1,6 +1,8 @@
 import jax
 import jax.numpy as jnp
 from jax import lax
+from jax.experimental import pallas as pl
+from jax.experimental.pallas import tpu as pltpu
 from jax.sharding import PartitionSpec as P
 
 epsilon = 1e-05
@@ -173,20 +175,78 @@
     return (factors * flags[None, None, :]).astype(bf16)
 
 
-def outer_stage(left, right, final):
-    n, t, hidden, s = left.shape
-    outer = jnp.einsum(
-        "ics,jds->ijcd",
-        left.reshape(n * t, hidden, s),
-        right.reshape(n * t, hidden, s),
+def outer_kernel(place, *refs):
+    n, t, hidden = place.shape[0] // 2, refs[0].shape[0], refs[0].shape[1]
+    s = refs[0].shape[2]
+    lefts, rights = refs[:n], refs[n : 2 * n]
+    final, out, left, pieces, right, plain, turned, outer, high, low = refs[2 * n :]
+    tokens, ratio = n * t, 128 // hidden
+    for k in range(n):
+        left[place[k]] = lefts[k][...].reshape(t * hidden, s)
+        pieces[place[n + k]] = rights[k][...].reshape(t * hidden, s).astype(f32)
+    for k in range(n):
+        for u in range(t):
+            right[pl.ds(k * t + u, hidden, stride=tokens), :] = pieces[k, u * hidden : (u + 1) * hidden, :]
+    plain[...] = final[...].astype(f32)
+    for d in range(hidden):
+        turned[d * hidden : (d + 1) * hidden, :] = plain[pl.ds(d, hidden, stride=hidden), :].astype(bf16)
+    outer[...] = lax.dot_general(
+        right[...].astype(bf16),
+        left[...].reshape(tokens * hidden, s),
+        (((1,), (1,)), ((), ())),
         preferred_element_type=f32,
-    ).reshape(n * t * n * t, hidden * hidden)
-    high = outer.astype(bf16)
-    low = (outer - high.astype(f32)).astype(bf16)
-    update = jnp.dot(high, final, preferred_element_type=f32) + jnp.dot(
-        low, final, preferred_element_type=f32
-    )
-    return update.reshape(n * t, n * t, -1)
+    )
+    lane = lax.broadcasted_iota(jnp.int32, (tokens, 128), 1)
+    for g in range(tokens // ratio):
+        for q in range(hidden // ratio):
+            tiles = [
+                outer[(q * ratio + d) * tokens : (q * ratio + d + 1) * tokens, g * 128 : (g + 1) * 128]
+                for d in range(ratio)
+            ]
+            bit = 1
+            while bit < ratio:
+                upper = (lane // (hidden * bit)) % 2 == 1
+                for x in range(ratio):
+                    if x & bit:
+                        continue
+                    a, b = tiles[x], tiles[x | bit]
+                    tiles[x] = jnp.where(upper, pltpu.roll(b, hidden * bit, 1), a)
+                    tiles[x | bit] = jnp.where(upper, b, pltpu.roll(a, 128 - hidden * bit, 1))
+                bit *= 2
+            for x in range(ratio):
+                i = g * ratio + x
+                rounded = tiles[x].astype(bf16)
+                high[i * tokens : (i + 1) * tokens, q * 128 : (q + 1) * 128] = rounded
+                low[i * tokens : (i + 1) * tokens, q * 128 : (q + 1) * 128] = (
+                    tiles[x] - rounded.astype(f32)
+                ).astype(bf16)
+    out[...] = jnp.dot(high[...], turned[...], preferred_element_type=f32) + jnp.dot(
+        low[...], turned[...], preferred_element_type=f32
+    )
+
+
+def outer_stage(place, lefts, rights, final):
+    n = len(lefts)
+    t, hidden, s = lefts[0].shape
+    tokens, width = n * t, final.shape[1]
+    vmem = pl.BlockSpec(memory_space=pltpu.VMEM)
+    return pl.pallas_call(
+        outer_kernel,
+        out_shape=jax.ShapeDtypeStruct((tokens * tokens, width), f32),
+        in_specs=[pl.BlockSpec(memory_space=pltpu.SMEM)] + [vmem] * (2 * n + 1),
+        out_specs=vmem,
+        scratch_shapes=[
+            pltpu.VMEM((n, t * hidden, s), bf16),
+            pltpu.VMEM((n, t * hidden, s), f32),
+            pltpu.VMEM((tokens * hidden, s), f32),
+            pltpu.VMEM((hidden * hidden, width), f32),
+            pltpu.VMEM((hidden * hidden, width), bf16),
+            pltpu.VMEM((tokens * hidden, tokens * hidden), f32),
+            pltpu.VMEM((tokens * tokens, hidden * hidden), bf16),
+            pltpu.VMEM((tokens * tokens, hidden * hidden), bf16),
+        ],
+        name="outer_stage",
+    )(place, *lefts, *rights, final)
 
 
 def pair_stage(update, couple, inverse, offset, row_tokens, col_tokens, couple_scale, score, tri_scale, entry, half, parts):
@@ -335,17 +395,13 @@
 
     lefts = [left] + [move(left, lambda r, c, k=k: (r, (c + k) % n)) for k in range(1, n)]
     rights = [move(right, lambda r, c, k=k: ((c + k) % n, r)) for k in range(n)]
-    all_left = jnp.zeros((n,) + left.shape, bf16)
-    all_right = jnp.zeros((n,) + left.shape, bf16)
-    for k in range(n):
-        all_left = lax.dynamic_update_index_in_dim(all_left, lefts[k], (col_index - k) % n, 0)
-        all_right = lax.dynamic_update_index_in_dim(all_right, rights[k], (row_index - k) % n, 0)
-    update = outer_stage(all_left, all_right, tensor_final_matrix)
+    place = jnp.stack([(col_index - k) % n for k in range(n)] + [(row_index - k) % n for k in range(n)])
+    update = outer_stage(place.astype(jnp.int32), lefts, rights, tensor_final_matrix)
     update = update + lax.ppermute(update, "depth", [(0, 1), (1, 0)])
     row_tokens = lax.dynamic_slice_in_dim(token_weight, row_index * rows, rows)
     col_tokens = lax.dynamic_slice_in_dim(token_weight, col_index * cols, cols)
     pair_one, block = pair_stage(
-        update, couple_state, inverse, tensor_offset, row_tokens, col_tokens, mean_couple_scale,
+        update.reshape(rows, cols, width), couple_state, inverse, tensor_offset, row_tokens, col_tokens, mean_couple_scale,
         mean_score_matrix, trimul_scale, trimul_entry_matrix, half, parts,
     )
     slab = sequence_stack.reshape(parts, 8, t * ch // 128, 128).transpose(0, 2, 1, 3)

time: 115 us -> 92.2 us (0.80)
  local copies, waits for them, and re-layouts: 32 us -> 14 us
  matrix products: 13.8 us -> 7.86 us
  Pallas kernels: 0 us -> 4.25 us
    transpose x1 -> x0, local copies, waits for them, and re-layouts: 9.61 us -> none  [outer_stage(): jnp.einsum('ics,jds->ijcd', left.reshape(n * t, hidden, s), right.reshape...]
    reshape x1 -> x0, local copies, waits for them, and re-layouts: 7.18 us -> none  [outer_stage(): outer = jnp.einsum('ics,jds->ijcd', left.reshape(n * t, hidden, s), right...]
    dot_general x3 -> x0, matrix products: 5.97 us -> none  [the longest x1 5.03 us: outer_stage(): jnp.einsum('ics,jds->ijcd', left.reshape(n * t, hidden, s), right.reshape...]
    pallas_call x0 -> x1, Pallas kernels: none -> 4.25 us  [outer_stage(): pl.pallas_call(outer_kernel, out_shape=jax.ShapeDtypeStruct((tokens * tok...]
    ppermute x7, waiting for transfers between devices: 4.66 us -> 3.38 us  [move(): return lax.ppermute(array, ('row', 'col'), pairs)]
    unnamed x53 -> x51, local copies, waits for them, and re-layouts: 2.66 us -> 2.48 us
  transfers between devices with their start and end apart: 10 -> 10, of which waited for: 4 -> 3; matrix products, arithmetic and copies ran while one was open for 4% -> 6% of each run, Pallas kernels for 0% -> 0%
where the time goes in v2:
time: 92.2 us; the launch traced here: 91.5 us
  starting transfers between devices  20.6 us (22%)
  blocking collectives  18 us (20%)
  local copies, waits for them, and re-layouts  14 us (15%)
  waiting for transfers between devices  13.4 us (15%)
  other arithmetic  11.1 us (12%)
  matrix products  7.86 us (9%)
  Pallas kernels  4.25 us (5%)
  between operations  2.42 us (3%)
    all_to_all x1, blocking collectives, on_device(): lax.all_to_all(jnp.concatenate([block, slab], 1), ('row', 'col'), 0, 0, t...  18 us
    ppermute x7, starting transfers between devices, move(): return lax.ppermute(array, ('row', 'col'), pairs)  16.7 us
    all_to_all x1, waiting for transfers between devices, on_device(): block = lax.all_to_all(block, ('row', 'col'), 0, 0, tiled=True)  8.35 us
    pallas_call x1, Pallas kernels, outer_stage(): pl.pallas_call(outer_kernel, out_shape=jax.ShapeDtypeStruct((tokens * tok...  4.25 us
    all_to_all x1, starting transfers between devices, on_device(): block = lax.all_to_all(block, ('row', 'col'), 0, 0, tiled=True)  3.74 us
    ppermute x7, waiting for transfers between devices, move(): return lax.ppermute(array, ('row', 'col'), pairs)  3.38 us
    unnamed x51, local copies, waits for them, and re-layouts  2.48 us
  transfers between devices with their start and end apart: 10, of which 3 were waited for; matrix products, arithmetic and copies ran while one was open for 6% of the time, Pallas kernels for 0%

profile of v2, /device:TPU:0, one launch (start us, length us, event | category | flops | bytes accessed | tf_op | source)
XLA Modules:
  0.0 91.5 jit_solution(1022755490514071580)
XLA Ops:
  0.7 0.7 convert_element_type.138
  1.4 0.9 bitcast_reduce_fusion
  2.3 0.9 %fusion.40 = f32[6,128]{1,0:T(8,128)S(1)} fusion(bf16[128,6,64]{0,2,1:T(8,128)(2,1)} %param.18, f32[6,128]{1,0:T(8,128)S(1)} %broadcast_multiply_fusion.4), kind=kLoop, calls=%fused_computation.69 | loop fusion | flops 195840 | bytes 104448 | tf_op jit(solution)/shard_map/reduce_sum | solution.py:172
  3.4 1.2 %fusion.14 = bf16[6,64,128]{2,1,0:T(8,128)(2,1)S(1)} fusion(bf16[128,6,64]{0,2,1:T(8,128)(2,1)} %param.18, f32[128]{0:T(128)S(1)} %dynamic_slice.13, f32[64]{0:T(128)} %param.22, f32[6,128]{1,0:T(8,128)S(1)} %add_rsqrt_fusion.3, f32[6,128]{1,0:T(8,128)S(1)} %broadcast_multiply_fusion.4, bf16[64,64]{1,0:T(8,128)(2,1)} %param.23), kind=kOutput, calls=%fused_computation.25 | convolution fusion | flops 6635520 | bytes 211712 | tf_op jit(solution)/shard_map/tcs,cf->tfs/dot_general | solution.py:174
  4.5 3.1 %collective-permute-start = (bf16[6,32,128]{2,1,0:T(8,128)(2,1)S(1)}, bf16[6,32,128]{2,1,0:T(8,128)(2,1)S(1)}, u32[]{:S(2)}, u32[]{:S(2)}) collective-permute-start(bf16[6,32,128]{2,1,0:T(8,128)(2,1)S(1)} %get-tuple-element.28.refs_0_), channel_id=1, source_target_pairs={{0,2},{2,4},{4,6},{6,0},{8,10},{10,12},{12,14},{14,8},{16,18},{18,... | collective-permute-start | bytes 147464 | tf_op jit(solution)/shard_map/ppermute | solution.py:394
  7.6 2.6 %collective-permute-start.1 = (bf16[6,32,128]{2,1,0:T(8,128)(2,1)S(1)}, bf16[6,32,128]{2,1,0:T(8,128)(2,1)S(1)}, u32[]{:S(2)}, u32[]{:S(2)}) collective-permute-start(bf16[6,32,128]{2,1,0:T(8,128)(2,1)S(1)} %get-tuple-element.28.refs_0_), channel_id=1, source_target_pairs={{0,4},{2,6},{4,0},{6,2},{8,12},{10,14},{12,8},{14,10},{16,20},{18,... | collective-permute-start | bytes 147464 | tf_op jit(solution)/shard_map/ppermute | solution.py:394
  10.2 1.3 %collective-permute-start.2 = (bf16[6,32,128]{2,1,0:T(8,128)(2,1)S(1)}, bf16[6,32,128]{2,1,0:T(8,128)(2,1)S(1)}, u32[]{:S(2)}, u32[]{:S(2)}) collective-permute-start(bf16[6,32,128]{2,1,0:T(8,128)(2,1)S(1)} %get-tuple-element.28.refs_0_), channel_id=1, source_target_pairs={{0,6},{2,0},{4,2},{6,4},{8,14},{10,8},{12,10},{14,12},{16,22},{18,... | collective-permute-start | bytes 147464 | tf_op jit(solution)/shard_map/ppermute | solution.py:394
  12.2 3.4 %collective-permute-start.4 = (bf16[6,32,128]{2,1,0:T(8,128)(2,1)S(1)}, bf16[6,32,128]{2,1,0:T(8,128)(2,1)S(1)}, u32[]{:S(2)}, u32[]{:S(2)}) collective-permute-start(bf16[6,32,128]{2,1,0:T(8,128)(2,1)S(1)} %get-tuple-element.27), channel_id=1, source_target_pairs={{0,8},{2,16},{4,24},{6,0},{8,10},{10,18},{12,26},{14,2},{16,12},{1... | collective-permute-start | bytes 147464 | tf_op jit(solution)/shard_map/ppermute | solution.py:394
  15.7 0.9 slice.75
  16.8 3.4 %collective-permute-start.5 = (bf16[6,32,128]{2,1,0:T(8,128)(2,1)S(1)}, bf16[6,32,128]{2,1,0:T(8,128)(2,1)S(1)}, u32[]{:S(2)}, u32[]{:S(2)}) collective-permute-start(bf16[6,32,128]{2,1,0:T(8,128)(2,1)S(1)} %get-tuple-element.27), channel_id=1, source_target_pairs={{0,16},{2,24},{4,0},{6,8},{8,18},{10,26},{12,2},{14,10},{16,20},{1... | collective-permute-start | bytes 147464 | tf_op jit(solution)/shard_map/ppermute | solution.py:394
  20.2 2.2 %collective-permute-start.6 = (bf16[6,32,128]{2,1,0:T(8,128)(2,1)S(1)}, bf16[6,32,128]{2,1,0:T(8,128)(2,1)S(1)}, u32[]{:S(2)}, u32[]{:S(2)}) collective-permute-start(bf16[6,32,128]{2,1,0:T(8,128)(2,1)S(1)} %get-tuple-element.27), channel_id=1, source_target_pairs={{0,24},{2,0},{4,8},{6,16},{8,26},{10,2},{12,10},{14,18},{16,28},{1... | collective-permute-start | bytes 147464 | tf_op jit(solution)/shard_map/ppermute | solution.py:394
  22.4 1.4 %convert_reduce_fusion.1 = f32[]{:T(128)} fusion(s32[256]{0:T(256)} %param.19), kind=kLoop, calls=%fused_computation.121 | loop fusion | flops 511 | bytes 1028 | tf_op jit(solution)/shard_map/reduce_sum | solution.py:386
  25.7 3.4 %collective-permute-done.6.refs_7_ = bf16[6,32,128]{2,1,0:T(8,128)(2,1)S(1)} collective-permute-done((bf16[6,32,128]{2,1,0:T(8,128)(2,1)S(1)}, bf16[6,32,128]{2,1,0:T(8,128)(2,1)S(1)}, u32[]{:S(2)}, u32[]{:S(2)}) %collective-permute-start.6) | collective-permute-done | bytes 49184 | tf_op jit(solution)/shard_map/ppermute | solution.py:394
  29.7 4.2 %outer_stage.1 = f32[576,128]{1,0:T(8,128)} custom-call(s32[8]{0:T(128)} %stack.44.place, bf16[6,32,128]{2,1,0:T(8,128)(2,1)} %copy-done.3, bf16[6,32,128]{2,1,0:T(8,128)(2,1)} %copy-done.6, bf16[6,32,128]{2,1,0:T(8,128)(2,1)} %copy-done.7, bf16[6,32,128]{2,1,0:T(8,128)(2,1)} %copy-done.8, bf16[6,32,128]{2,1,0:T(8,128)(2,1)} %copy-done.9, ...), custom_call_target="tpu_custom_call" | custom-call | tf_op jit(solution)/shard_map/outer_stage/pallas_call | solution.py:233
  34.1 1.6 %collective-permute-done.7 = f32[576,128]{1,0:T(8,128)S(1)} collective-permute-done((f32[576,128]{1,0:T(8,128)}, f32[576,128]{1,0:T(8,128)S(1)}, u32[]{:S(2)}, u32[]{:S(2)}) %collective-permute-start.7) | collective-permute-done | bytes 294944 | tf_op jit(solution)/shard_map/ppermute | solution.py:400
  35.8 1.0 %add_multiply_fusion = f32[576,128]{1,0:T(8,128)S(1)} fusion(f32[576,128]{1,0:T(8,128)} %outer_stage.1, f32[576,128]{1,0:T(8,128)S(1)} %collective-permute-done.7, f32[]{:T(128)S(6)} %div.65), kind=kLoop, calls=%fused_computation.59 | loop fusion | flops 147456 | bytes 884740 | tf_op jit(solution)/shard_map/mul | solution.py:254
  37.3 1.7 %fusion.69 = (f32[24,8]{1,0:T(8,128)S(1)}, f32[24,8,24]{2,1,0:T(8,128)S(1)}) fusion(f32[24]{0:T(128)S(1)} %get-tuple-element.12, f32[128,8]{0,1:T(8,128)S(1)} %copy-done.20, bf16[24,24,128]{2,1,0:T(8,128)(2,1)S(1)} %get-tuple-element.15, f32[128]{0:T(128)S(1)} %copy-done.22, f32[24,24]{1,0:T(8,128)S(1)} %add_rsqrt_fusion.2, ...), kind=kOutput, calls=%fused_computation.127 | convolution fusion | flops 7381824 | bytes 175968 | tf_op jit(solution)/shard_map/ijc,ch->ihj/dot_general | solution.py:260
  42.1 18.0 %all_to_all.10 = bf16[16,104,128]{2,1,0:T(8,128)(2,1)S(1)} all-to-all(bf16[16,104,128]{2,1,0:T(8,128)(2,1)S(1)} %bitcast_dynamic-update-slice_fusion), channel_id=1, replica_groups=mesh['row'=4,'col'=4,'depth'=2] {'row','col'}, dimensions={0} | all-to-all | bytes 851968 | tf_op jit(solution)/shard_map/all_to_all | solution.py:409
  65.1 0.9 %multiply_reduce_fusion.1 = f32[8,16,3,2]{3,0,2,1:T(8,128)S(1)} fusion(f32[8,16,3,2]{3,0,2,1:T(8,128)S(1)} %copy.177, f32[16,3,8,2,64]{4,3,2,1,0:T(2,128)S(1)} %reshape.274), kind=kLoop, calls=%fused_computation.40 | loop fusion | flops 146688 | bytes 202752 | tf_op jit(solution)/shard_map/reduce_sum | solution.py:22
  73.4 3.7 %all-to-all-start.1 = ((bf16[16,48,128]{2,1,0:T(8,128)(2,1)}), bf16[16,48,128]{2,1,0:T(8,128)(2,1)S(1)}, u32[]{:S(2)}, u32[]{:S(2)}) async-start(bf16[16,48,128]{2,1,0:T(8,128)(2,1)} %fusion.35), calls=%async_computation.1 | async-start | bytes 393216 | tf_op jit(solution)/shard_map/all_to_all | solution.py:414
  77.1 8.3 %all-to-all-done.1 = bf16[16,48,128]{2,1,0:T(8,128)(2,1)S(1)} async-done(((bf16[16,48,128]{2,1,0:T(8,128)(2,1)}), bf16[16,48,128]{2,1,0:T(8,128)(2,1)S(1)}, u32[]{:S(2)}, u32[]{:S(2)}) %all-to-all-start.1) | async-done | bytes 196640 | tf_op jit(solution)/shard_map/all_to_all | solution.py:414
  85.5 1.8 %fusion.9 = f32[24,24,128]{2,1,0:T(8,128)} fusion(bf16[24,24,128]{2,1,0:T(8,128)(2,1)S(1)} %get-tuple-element.15, f32[128]{0:T(128)S(1)} %copy-done.17, f32[24,24]{1,0:T(8,128)S(1)} %add_rsqrt_fusion.2, f32[24,24]{1,0:T(8,128)S(1)} %broadcast_multiply_fusion.3, bf16[128,640]{1,0:T(8,128)(2,1)} %param.33), kind=kOutput, calls=%fused_computation.17 | convolution fusion | flops 19464192 | bytes 480256 | tf_op jit(solution)/shard_map/dot_general | solution.py:348
  89.4 0.8 copy.197
  90.5 1.0 %fusion.11 = bf16[24,24,128]{2,1,0:T(8,128)(2,1)} fusion(f32[24,24,128]{2,1,0:T(8,128)S(1)} %copy-done.2, bf16[24,24,128]{1,0,2:T(8,128)(2,1)S(1)} %fusion.2, bf16[24,24,128]{2,1,0:T(8,128)(2,1)S(1)} %get-tuple-element.15, bf16[128,128]{1,0:T(8,128)(2,1)S(1)} %copy-done.14), kind=kOutput, calls=%fused_computation.20 | convolution fusion | flops 19169280 | bytes 770048 | tf_op jit(solution)/shard_map/dot_general | solution.py:349
  (163 shorter events, 20.4 us)
Async XLA Ops:
  0.6 66.2 %copy-start = (bf16[64,256]{1,0:T(8,128)(2,1)S(1)}, bf16[64,256]{1,0:T(8,128)(2,1)}, u32[]{:S(2)}) copy-start(bf16[64,256]{1,0:T(8,128)(2,1)} %param.29) | copy-start | bytes 98308
  0.6 23.1 %copy-start.1 = (bf16[128,6,64]{0,2,1:T(8,128)(2,1)S(1)}, bf16[128,6,64]{0,2,1:T(8,128)(2,1)}, u32[]{:S(2)}) copy-start(bf16[128,6,64]{0,2,1:T(8,128)(2,1)} %param.18) | copy-start | bytes 294916
  0.7 23.3 %copy-start.21 = (s32[96]{0:T(128)S(1)}, s32[96]{0:T(128)}, u32[]{:S(2)}) copy-start(s32[96]{0:T(128)} %param.20) | copy-start | bytes 1156
  4.5 24.5 %copy-start.3 = (bf16[6,32,128]{2,1,0:T(8,128)(2,1)}, bf16[6,32,128]{2,1,0:T(8,128)(2,1)S(1)}, u32[]{:S(2)}) copy-start(bf16[6,32,128]{2,1,0:T(8,128)(2,1)S(1)} %get-tuple-element.28.refs_0_) | copy-start | bytes 147460
  4.5 12.2 %collective-permute-start = (bf16[6,32,128]{2,1,0:T(8,128)(2,1)S(1)}, bf16[6,32,128]{2,1,0:T(8,128)(2,1)S(1)}, u32[]{:S(2)}, u32[]{:S(2)}) collective-permute-start(bf16[6,32,128]{2,1,0:T(8,128)(2,1)S(1)} %get-tuple-element.28.refs_0_), channel_id=1, source_target_pairs={{0,2},{2,4},{4,6},{6,0},{8,10},{10,12},{12,14},{14,8},{16,18},{18,... | collective-permute-start | bytes 147464 | tf_op jit(solution)/shard_map/ppermute | solution.py:394
  7.6 12.5 %collective-permute-start.1 = (bf16[6,32,128]{2,1,0:T(8,128)(2,1)S(1)}, bf16[6,32,128]{2,1,0:T(8,128)(2,1)S(1)}, u32[]{:S(2)}, u32[]{:S(2)}) collective-permute-start(bf16[6,32,128]{2,1,0:T(8,128)(2,1)S(1)} %get-tuple-element.28.refs_0_), channel_id=1, source_target_pairs={{0,4},{2,6},{4,0},{6,2},{8,12},{10,14},{12,8},{14,10},{16,20},{18,... | collective-permute-start | bytes 147464 | tf_op jit(solution)/shard_map/ppermute | solution.py:394
  10.2 15.4 %collective-permute-start.2 = (bf16[6,32,128]{2,1,0:T(8,128)(2,1)S(1)}, bf16[6,32,128]{2,1,0:T(8,128)(2,1)S(1)}, u32[]{:S(2)}, u32[]{:S(2)}) collective-permute-start(bf16[6,32,128]{2,1,0:T(8,128)(2,1)S(1)} %get-tuple-element.28.refs_0_), channel_id=1, source_target_pairs={{0,6},{2,0},{4,2},{6,4},{8,14},{10,8},{12,10},{14,12},{16,22},{18,... | collective-permute-start | bytes 147464 | tf_op jit(solution)/shard_map/ppermute | solution.py:394
  11.6 14.1 %collective-permute-start.3 = (bf16[6,32,128]{2,1,0:T(8,128)(2,1)S(1)}, bf16[6,32,128]{2,1,0:T(8,128)(2,1)S(1)}, u32[]{:S(2)}, u32[]{:S(2)}) collective-permute-start(bf16[6,32,128]{2,1,0:T(8,128)(2,1)S(1)} %get-tuple-element.27), channel_id=1, source_target_pairs={{0,0},{2,8},{4,16},{6,24},{8,2},{10,10},{12,18},{14,26},{16,4},{18... | collective-permute-start | bytes 147464 | tf_op jit(solution)/shard_map/ppermute | solution.py:394
  12.2 13.4 %collective-permute-start.4 = (bf16[6,32,128]{2,1,0:T(8,128)(2,1)S(1)}, bf16[6,32,128]{2,1,0:T(8,128)(2,1)S(1)}, u32[]{:S(2)}, u32[]{:S(2)}) collective-permute-start(bf16[6,32,128]{2,1,0:T(8,128)(2,1)S(1)} %get-tuple-element.27), channel_id=1, source_target_pairs={{0,8},{2,16},{4,24},{6,0},{8,10},{10,18},{12,26},{14,2},{16,12},{1... | collective-permute-start | bytes 147464 | tf_op jit(solution)/shard_map/ppermute | solution.py:394
  16.6 20.2 %copy-start.4 = (bf16[24,24,128]{2,1,0:T(8,128)(2,1)S(1)}, bf16[24,24,128]{2,1,0:T(8,128)(2,1)}, u32[]{:S(2)}) copy-start(bf16[24,24,128]{2,1,0:T(8,128)(2,1)} %param.21) | copy-start | bytes 442372
  16.6 20.2 %copy-start.16 = (f32[128]{0:T(128)S(1)}, f32[128]{0:T(128)}, u32[]{:S(2)}) copy-start(f32[128]{0:T(128)} %param.25) | copy-start | bytes 1540
  16.8 12.3 %copy-start.6 = (bf16[6,32,128]{2,1,0:T(8,128)(2,1)}, bf16[6,32,128]{2,1,0:T(8,128)(2,1)S(1)}, u32[]{:S(2)}) copy-start(bf16[6,32,128]{2,1,0:T(8,128)(2,1)S(1)} %collective-permute-done.refs_1_) | copy-start | bytes 147460
  16.8 8.9 %collective-permute-start.5 = (bf16[6,32,128]{2,1,0:T(8,128)(2,1)S(1)}, bf16[6,32,128]{2,1,0:T(8,128)(2,1)S(1)}, u32[]{:S(2)}, u32[]{:S(2)}) collective-permute-start(bf16[6,32,128]{2,1,0:T(8,128)(2,1)S(1)} %get-tuple-element.27), channel_id=1, source_target_pairs={{0,16},{2,24},{4,0},{6,8},{8,18},{10,26},{12,2},{14,10},{16,20},{1... | collective-permute-start | bytes 147464 | tf_op jit(solution)/shard_map/ppermute | solution.py:394
  20.2 8.9 %copy-start.7 = (bf16[6,32,128]{2,1,0:T(8,128)(2,1)}, bf16[6,32,128]{2,1,0:T(8,128)(2,1)S(1)}, u32[]{:S(2)}) copy-start(bf16[6,32,128]{2,1,0:T(8,128)(2,1)S(1)} %collective-permute-done.1.refs_2_) | copy-start | bytes 147460
  20.2 8.9 %collective-permute-start.6 = (bf16[6,32,128]{2,1,0:T(8,128)(2,1)S(1)}, bf16[6,32,128]{2,1,0:T(8,128)(2,1)S(1)}, u32[]{:S(2)}, u32[]{:S(2)}) collective-permute-start(bf16[6,32,128]{2,1,0:T(8,128)(2,1)S(1)} %get-tuple-element.27), channel_id=1, source_target_pairs={{0,24},{2,0},{4,8},{6,16},{8,26},{10,2},{12,10},{14,18},{16,28},{1... | collective-permute-start | bytes 147464 | tf_op jit(solution)/shard_map/ppermute | solution.py:394
  24.0 13.3 %copy-start.20 = (f32[128,8]{0,1:T(8,128)S(1)}, f32[128,8]{0,1:T(8,128)}, u32[]{:S(2)}) copy-start(f32[128,8]{0,1:T(8,128)} %param.28) | copy-start | bytes 12292
  24.0 13.3 %copy-start.22 = (f32[128]{0:T(128)S(1)}, f32[128]{0:T(128)}, u32[]{:S(2)}) copy-start(f32[128]{0:T(128)} %param.27) | copy-start | bytes 1540
  25.6 13.7 %copy-start.17 = (f32[128]{0:T(128)S(1)}, f32[128]{0:T(128)}, u32[]{:S(2)}) copy-start(f32[128]{0:T(128)} %param.32) | copy-start | bytes 1540
  25.6 3.4 %copy-start.8 = (bf16[6,32,128]{2,1,0:T(8,128)(2,1)}, bf16[6,32,128]{2,1,0:T(8,128)(2,1)S(1)}, u32[]{:S(2)}) copy-start(bf16[6,32,128]{2,1,0:T(8,128)(2,1)S(1)} %collective-permute-done.2.refs_3_) | copy-start | bytes 147460
  25.7 3.4 %copy-start.9 = (bf16[6,32,128]{2,1,0:T(8,128)(2,1)}, bf16[6,32,128]{2,1,0:T(8,128)(2,1)S(1)}, u32[]{:S(2)}) copy-start(bf16[6,32,128]{2,1,0:T(8,128)(2,1)S(1)} %collective-permute-done.3.refs_4_) | copy-start | bytes 147460
  25.7 3.4 %copy-start.10 = (bf16[6,32,128]{2,1,0:T(8,128)(2,1)}, bf16[6,32,128]{2,1,0:T(8,128)(2,1)S(1)}, u32[]{:S(2)}) copy-start(bf16[6,32,128]{2,1,0:T(8,128)(2,1)S(1)} %collective-permute-done.4.refs_5_) | copy-start | bytes 147460
  34.0 1.8 %collective-permute-start.7 = (f32[576,128]{1,0:T(8,128)}, f32[576,128]{1,0:T(8,128)S(1)}, u32[]{:S(2)}, u32[]{:S(2)}) collective-permute-start(f32[576,128]{1,0:T(8,128)} %outer_stage.1), channel_id=1, source_target_pairs={{0,1},{1,0},{2,3},{3,2},{4,5},{5,4},{6,7},{7,6},{8,9},{9,8},{10,11... | collective-permute-start | bytes 884744 | tf_op jit(solution)/shard_map/ppermute | solution.py:400
  73.4 12.1 %all-to-all-start.1 = ((bf16[16,48,128]{2,1,0:T(8,128)(2,1)}), bf16[16,48,128]{2,1,0:T(8,128)(2,1)S(1)}, u32[]{:S(2)}, u32[]{:S(2)}) async-start(bf16[16,48,128]{2,1,0:T(8,128)(2,1)} %fusion.35), calls=%async_computation.1 | async-start | bytes 393216 | tf_op jit(solution)/shard_map/all_to_all | solution.py:414
  85.5 1.9 %collective-permute-start.8 = (bf16[16,24,128]{2,1,0:T(8,128)(2,1)S(1)}, bf16[16,24,128]{2,1,0:T(8,128)(2,1)S(1)}, u32[]{:S(2)}, u32[]{:S(2)}) collective-permute-start(bf16[16,24,128]{2,1,0:T(8,128)(2,1)S(1)} %slice.113), channel_id=1, source_target_pairs={{0,1},{1,0},{2,3},{3,2},{4,5},{5,4},{6,7},{7,6},{8,9},{9,8},{10,11... | collective-permute-start | bytes 294920 | tf_op jit(solution)/shard_map/ppermute | solution.py:416
  (10 other events, 13.3 us)

commit v3 on v2

--- a/solution.py
+++ b/solution.py
@@ -1,3 +1,5 @@
+import functools
+
 import jax
 import jax.numpy as jnp
 from jax import lax
@@ -297,45 +299,135 @@
     return pair_one, block
 
 
-def middle_stage(block, n, rows, cols, heads, seq_scale, content, sigmoid_matrix, final):
-    parts = n * n
-    ch = final.shape[1]
-    feats = 128 // cols - (1 if (128 // cols) * cols > 96 else 0)
-    left = block[:, :rows]
-    right = block[:, rows : 2 * rows]
-    expo = jnp.concatenate([block[:, 2 * rows : 3 * rows], left[..., feats * cols :], right[..., feats * cols :]], -1)
-    stats = block[:, 3 * rows : 3 * rows + 8]
-    slab = block[:, 3 * rows + 8 :]
-
-    def whole(operand):
-        operand = operand[..., : feats * cols].reshape(n, n, rows, feats, cols)
-        return operand.transpose(3, 0, 2, 1, 4).reshape(feats, n * rows, n * cols)
-
-    product = jnp.einsum("fik,fjk->fij", whole(left), whole(right), preferred_element_type=f32)
-    product = product.astype(bf16).reshape(feats, n, rows, n, cols)
-    product = product.transpose(1, 3, 2, 0, 4).reshape(parts, rows, feats * cols)
-    product = jnp.pad(product, ((0, 0), (0, 0), (0, 128 - feats * cols)))
-    stats = stats[..., : rows // 8 * 3 * heads].reshape(parts, 8, rows // 8, 3, heads)
-    peak = stats.astype(f32).sum(3).transpose(0, 2, 1, 3).reshape(n, n, rows, heads)
-    expo = expo.reshape(n, n, rows, heads, cols).astype(f32)
-    top = jnp.max(peak, 1, keepdims=True)
-    factor = jnp.exp(peak - top)
-    total = jnp.sum(factor * jnp.sum(expo, -1), 1, keepdims=True)
-    weights = (expo * (factor / total)[..., None]).astype(bf16)
-    weights = weights.transpose(3, 0, 2, 1, 4).reshape(heads, n * rows, n * cols)
-    groups = slab.shape[1] // 8
-    tokens = slab.reshape(parts, groups, 8, 128 // ch, ch).transpose(2, 0, 1, 3, 4).reshape(8, n * rows, ch)
-    normed = standardize_features(tokens, seq_scale).astype(bf16)
-    values = jnp.dot(normed, content, preferred_element_type=f32).astype(bf16)
-    gates = jax.nn.sigmoid(jnp.dot(normed, sigmoid_matrix, preferred_element_type=f32))
-    values = values.reshape(8, n * rows, heads, -1)
-    averaged = jnp.einsum("hij,sjhe->sihe", weights, values, preferred_element_type=f32)
-    gated = gates * averaged.reshape(8, n * rows, -1)
-    delta = jnp.dot(gated, final.astype(f32), precision=lax.Precision.HIGHEST)
-    revised = (tokens.astype(f32) + delta).astype(bf16)
-    revised = revised.reshape(8, parts, groups, 128 // ch, ch).transpose(1, 2, 0, 3, 4)
-    revised = revised.reshape(parts, groups * 8, 128)
-    return jnp.concatenate([product, revised], 1)
+def halves(value):
+    high = value.astype(bf16)
+    return high, (value - high.astype(f32)).astype(bf16)
+
+
+def two_pass_dot(value, matrix, axis=0):
+    high, low = halves(value)
+    over = (((1,), (axis,)), ((), ()))
+    return lax.dot_general(high, matrix, over, preferred_element_type=f32) + lax.dot_general(
+        low, matrix, over, preferred_element_type=f32
+    )
+
+
+def middle_kernel(sizes, block, seq_scale, content, sigmoid_matrix, final, out, wide, lhs, rhs, product, weights, x, values, gated, masked, revised):
+    n, rows, cols, heads, feats, groups, order = sizes
+    parts, tokens, ch = n * n, n * rows, final.shape[0]
+    s, per = 8, 128 // final.shape[0]
+    t = rows // n
+    wide[...] = block[...].astype(f32)
+    lane = lax.broadcasted_iota(jnp.int32, (tokens, 128), 1)
+    small = lax.broadcasted_iota(jnp.int32, (rows, 128), 1)
+    tiny = lax.broadcasted_iota(jnp.int32, (8, 128), 1)
+    spare = 128 - feats * cols
+
+    def stacked(c, start, count):
+        return jnp.concatenate([wide[r * n + c, start : start + count] for r in range(n)], 0)
+
+    rhs[...] = jnp.zeros_like(rhs)
+    for c in range(n):
+        mine = stacked(c, 0, rows)
+        for f in range(feats):
+            keep = (lane >= f * cols) & (lane < (f + 1) * cols)
+            lhs[f * tokens : (f + 1) * tokens, c * 128 : (c + 1) * 128] = jnp.where(keep, mine, 0.0).astype(bf16)
+        rhs[:tokens, c * 128 : (c + 1) * 128] = stacked(c, rows, rows).astype(bf16)
+    product[...] = lax.dot_general(lhs[...], rhs[...], (((1,), (1,)), ((), ())), preferred_element_type=f32)
+    up = lax.broadcasted_iota(jnp.int32, (256, 128), 0)
+    across = lax.broadcasted_iota(jnp.int32, (256, 128), 1)
+    gather = ((up >= across * cols) & (up < (across + 1) * cols) & (across < heads)).astype(bf16)
+    up = lax.broadcasted_iota(jnp.int32, (128, 256), 0)
+    across = lax.broadcasted_iota(jnp.int32, (128, 256), 1)
+    spread = ((across >= up * cols) & (across < (up + 1) * cols) & (up < heads)).astype(bf16)
+    expos, peaks = [], []
+    for c in range(n):
+        a, b = stacked(c, 0, rows), stacked(c, rows, rows)
+        rest = jnp.where(lane < spare, pltpu.roll(a, spare, 1), jnp.where(lane < 2 * spare, pltpu.roll(b, 2 * spare, 1), 0.0))
+        expos.append(jnp.concatenate([stacked(c, 2 * rows, rows), rest], 1))
+        peak = []
+        for r in range(n):
+            stats = wide[r * n + c, 3 * rows : 3 * rows + 8]
+            for q in range(rows // 8):
+                one = pltpu.roll(stats, (128 - 3 * heads * q) % 128, 1) if q else stats
+                peak.append(one + pltpu.roll(one, 128 - heads, 1) + pltpu.roll(one, 128 - 2 * heads, 1))
+        peaks.append(jnp.concatenate(peak, 0))
+    top = peaks[0]
+    for c in range(1, n):
+        top = jnp.maximum(top, peaks[c])
+    factors = [jnp.exp(peak - top) for peak in peaks]
+    total = jnp.zeros_like(top)
+    for c in range(n):
+        total = total + factors[c] * jnp.dot(expos[c].astype(bf16), gather, preferred_element_type=f32)
+    for c in range(n):
+        scale = jnp.where(lane < heads, factors[c] / jnp.where(lane < heads, total, 1.0), 0.0)
+        weights[:, c * 256 : (c + 1) * 256] = (expos[c] * two_pass_dot(scale, spread)).astype(bf16)
+    for p in range(parts):
+        for g in range(groups):
+            pair = wide[p, 3 * rows + 8 + 8 * g : 3 * rows + 16 + 8 * g]
+            for k in range(per):
+                x[pl.ds(p * t + g * per + k, s, stride=tokens), :] = pltpu.roll(pair, 128 - k * ch, 1) if k else pair
+    raw = x[...][:, :ch]
+    centred = raw - jnp.mean(raw, -1, keepdims=True)
+    variance = jnp.mean(centred * centred, -1, keepdims=True)
+    normed = (centred * lax.rsqrt(variance + epsilon) * seq_scale[...]).astype(bf16)
+    values[...] = jnp.dot(normed, content[...], preferred_element_type=f32).astype(bf16).astype(f32)
+    gates = jax.nn.sigmoid(jnp.dot(normed, sigmoid_matrix[...], preferred_element_type=f32))
+    width = gates.shape[1]
+    head_of = lax.broadcasted_iota(jnp.int32, (cols, width), 1) // (width // heads)
+    used = heads * cols
+    masked[...] = jnp.zeros_like(masked)
+    for q in range(s):
+        for c in range(n):
+            local = jnp.concatenate([values[q * tokens + a : q * tokens + a + m] for a, m in order[c]], 0)
+            spread_out = jnp.concatenate([jnp.where(head_of == h, local, 0.0) for h in range(heads)], 0)
+            masked[q, c * 256 : c * 256 + used] = spread_out.astype(bf16)
+        averaged = jnp.dot(weights[...], masked[q], preferred_element_type=f32)
+        gated[q * tokens : (q + 1) * tokens] = gates[q * tokens : (q + 1) * tokens] * averaged
+    delta = two_pass_dot(gated[...], final[...], 1)
+    revised[:, :ch] = raw + delta
+    for p in range(parts):
+        r, c = p // n, p % n
+        slab = jnp.zeros((rows, 128), f32)
+        for f in range(feats):
+            shift = ((f - c) * cols) % 128
+            piece = product[f * tokens + r * rows : f * tokens + (r + 1) * rows]
+            piece = pltpu.roll(piece, shift, 1) if shift else piece
+            slab = jnp.where((small >= f * cols) & (small < (f + 1) * cols), piece, slab)
+        slabs = [slab]
+        for g in range(groups):
+            merged = revised[pl.ds(p * t + g * per, s, stride=tokens), :]
+            for k in range(1, per):
+                piece = revised[pl.ds(p * t + g * per + k, s, stride=tokens), :]
+                merged = jnp.where(tiny >= k * ch, pltpu.roll(piece, k * ch, 1), merged)
+            slabs.append(merged)
+        out[p] = jnp.concatenate(slabs, 0).astype(bf16)
+
+
+def middle_stage(block, n, rows, cols, heads, feats, order, seq_scale, content, sigmoid_matrix, final):
+    parts, tokens = n * n, n * rows
+    groups = (block.shape[1] - 3 * rows - 8) // 8
+    width = content.shape[1]
+    vmem = pl.BlockSpec(memory_space=pltpu.VMEM)
+    return pl.pallas_call(
+        functools.partial(middle_kernel, (n, rows, cols, heads, feats, groups, order)),
+        out_shape=jax.ShapeDtypeStruct((parts, rows + 8 * groups, 128), bf16),
+        in_specs=[vmem] * 5,
+        out_specs=vmem,
+        scratch_shapes=[
+            pltpu.VMEM(block.shape, f32),
+            pltpu.VMEM((feats * tokens, n * 128), bf16),
+            pltpu.VMEM((128, n * 128), bf16),
+            pltpu.VMEM((feats * tokens, 128), f32),
+            pltpu.VMEM((tokens, n * 256), bf16),
+            pltpu.VMEM((8 * tokens, 128), f32),
+            pltpu.VMEM((8 * tokens, width), f32),
+            pltpu.VMEM((8 * tokens, width), f32),
+            pltpu.VMEM((8, n * 256, width), bf16),
+            pltpu.VMEM((8 * tokens, 128), f32),
+        ],
+        name="middle_stage",
+    )(block, seq_scale.reshape(1, -1), content, sigmoid_matrix, final.T)
 
 
 def final_stage(product, pair_one, tri_scale, entry, result_scale, final):
@@ -381,6 +473,8 @@
     count, t, ch = sequence_stack.shape
     hidden = tensor_entry_matrix.shape[1] // 2
     heads = mean_score_matrix.shape[1]
+    feats = width // (2 * parts)
+    order = tuple(((c * cols, cols),) for c in range(n))
     token_weight = genuine_residue_flags.astype(f32)
     flags = present_sequence_flags.astype(f32)
     inverse = 1.0 / (jnp.sum(flags) + 0.001)
@@ -408,7 +502,7 @@
     slab = slab.reshape(parts, -1, 128)
     block = lax.all_to_all(jnp.concatenate([block, slab], 1), ("row", "col"), 0, 0, tiled=True)
     block = middle_stage(
-        block, n, rows, cols, heads, mean_sequence_scale, mean_content_matrix, mean_sigmoid_matrix,
+        block, n, rows, cols, heads, feats, order, mean_sequence_scale, mean_content_matrix, mean_sigmoid_matrix,
         mean_final_matrix,
     )
     block = lax.all_to_all(block, ("row", "col"), 0, 0, tiled=True)

time: 92.2 us -> 82.5 us (0.89)
  local copies, waits for them, and re-layouts: 14 us -> 6.42 us
  other arithmetic: 11.1 us -> 6.99 us
  Pallas kernels: 4.25 us -> 8.28 us
  matrix products: 7.86 us -> 6.11 us
    pallas_call x0 -> x1, Pallas kernels: none -> 4.02 us  [middle_stage(): pl.pallas_call(functools.partial(middle_kernel, (n, rows, cols, heads, fe...]
    reshape x12 -> x1, local copies, waits for them, and re-layouts: 2.66 us -> 0.05 us  [on_device(): block[:, rows:].reshape(parts, t * ch // 128, 8, 128).transpose(0, 2, 1, 3)]
    dot_general x5 -> x0, matrix products: 1.76 us -> none  [the longest x1 0.58 us: middle_stage(): delta = jnp.dot(gated, final.astype(f32), precision=lax.Precision.HIGHEST)]
    convert_element_type x8 -> x0, local copies, waits for them, and re-layouts: 1.71 us -> none  [the longest x4 0.6 us: middle_stage(): revised = (tokens.astype(f32) + delta).astype(bf16)]
    transpose x7 -> x0, local copies, waits for them, and re-layouts: 1.6 us -> none  [the longest x1 0.61 us: middle_stage(): weights.transpose(3, 0, 2, 1, 4).reshape(heads, n * rows, n * cols)]
    reduce_sum x2 -> x1, other arithmetic: 1.46 us -> 0.27 us  [standardize_features(): variance = jnp.mean(centred * centred, -1, keepdims=True)]
    unnamed x51 -> x43, local copies, waits for them, and re-layouts: 2.48 us -> 1.87 us
where the time goes in v3:
time: 82.5 us; the launch traced here: 81.9 us
  starting transfers between devices  20.5 us (25%)
  blocking collectives  18.1 us (22%)
  waiting for transfers between devices  13.7 us (17%)
  Pallas kernels  8.28 us (10%)
  other arithmetic  6.99 us (8%)
  local copies, waits for them, and re-layouts  6.42 us (8%)
  matrix products  6.11 us (7%)
  between operations  1.88 us (2%)
    all_to_all x1, blocking collectives, on_device(): lax.all_to_all(jnp.concatenate([block, slab], 1), ('row', 'col'), 0, 0, t...  18.1 us
    ppermute x7, starting transfers between devices, move(): return lax.ppermute(array, ('row', 'col'), pairs)  16.7 us
    all_to_all x1, waiting for transfers between devices, on_device(): block = lax.all_to_all(block, ('row', 'col'), 0, 0, tiled=True)  8.39 us
    pallas_call x1, Pallas kernels, outer_stage(): pl.pallas_call(outer_kernel, out_shape=jax.ShapeDtypeStruct((tokens * tok...  4.25 us
    pallas_call x1, Pallas kernels, middle_stage(): pl.pallas_call(functools.partial(middle_kernel, (n, rows, cols, heads, fe...  4.02 us
    all_to_all x1, starting transfers between devices, on_device(): block = lax.all_to_all(block, ('row', 'col'), 0, 0, tiled=True)  3.7 us
    ppermute x7, waiting for transfers between devices, move(): return lax.ppermute(array, ('row', 'col'), pairs)  3.65 us
    unnamed x43, local copies, waits for them, and re-layouts  1.87 us
  transfers between devices with their start and end apart: 10, of which 3 were waited for; matrix products, arithmetic and copies ran while one was open for 6% of the time, Pallas kernels for 0%

profile of v3, /device:TPU:0, one launch (start us, length us, event | category | flops | bytes accessed | tf_op | source)
XLA Modules:
  0.0 81.9 jit_solution(11379977311119058398)
XLA Ops:
  0.7 0.7 convert_element_type.89
  1.4 0.9 %bitcast_reduce_fusion.1 = f32[6,128]{1,0:T(8,128)S(1)} fusion(bf16[128,6,64]{0,2,1:T(8,128)(2,1)} %param.18), kind=kLoop, calls=%fused_computation.48 | loop fusion | flops 97536 | bytes 101376 | tf_op jit(solution)/shard_map/reduce_sum | solution.py:172
  2.3 0.9 %fusion.32 = f32[6,128]{1,0:T(8,128)S(1)} fusion(bf16[128,6,64]{0,2,1:T(8,128)(2,1)} %param.18, f32[6,128]{1,0:T(8,128)S(1)} %broadcast_multiply_fusion.3), kind=kLoop, calls=%fused_computation.51 | loop fusion | flops 195840 | bytes 104448 | tf_op jit(solution)/shard_map/reduce_sum | solution.py:174
  3.4 1.2 %fusion.11 = bf16[6,64,128]{2,1,0:T(8,128)(2,1)S(1)} fusion(bf16[128,6,64]{0,2,1:T(8,128)(2,1)} %param.18, f32[128]{0:T(128)S(1)} %dynamic_slice.13, f32[64]{0:T(128)} %param.22, f32[6,128]{1,0:T(8,128)S(1)} %add_rsqrt_fusion.2, f32[6,128]{1,0:T(8,128)S(1)} %broadcast_multiply_fusion.3, bf16[64,64]{1,0:T(8,128)(2,1)} %param.23), kind=kOutput, calls=%fused_computation.17 | convolution fusion | flops 6635520 | bytes 211712 | tf_op jit(solution)/shard_map/tcs,cf->tfs/dot_general | solution.py:176
  4.5 3.1 %collective-permute-start = (bf16[6,32,128]{2,1,0:T(8,128)(2,1)S(1)}, bf16[6,32,128]{2,1,0:T(8,128)(2,1)S(1)}, u32[]{:S(2)}, u32[]{:S(2)}) collective-permute-start(bf16[6,32,128]{2,1,0:T(8,128)(2,1)S(1)} %get-tuple-element.20.refs_0_), channel_id=1, source_target_pairs={{0,2},{2,4},{4,6},{6,0},{8,10},{10,12},{12,14},{14,8},{16,18},{18,... | collective-permute-start | bytes 147464 | tf_op jit(solution)/shard_map/ppermute | solution.py:488
  7.6 2.6 %collective-permute-start.1 = (bf16[6,32,128]{2,1,0:T(8,128)(2,1)S(1)}, bf16[6,32,128]{2,1,0:T(8,128)(2,1)S(1)}, u32[]{:S(2)}, u32[]{:S(2)}) collective-permute-start(bf16[6,32,128]{2,1,0:T(8,128)(2,1)S(1)} %get-tuple-element.20.refs_0_), channel_id=1, source_target_pairs={{0,4},{2,6},{4,0},{6,2},{8,12},{10,14},{12,8},{14,10},{16,20},{18,... | collective-permute-start | bytes 147464 | tf_op jit(solution)/shard_map/ppermute | solution.py:488
  10.2 1.3 %collective-permute-start.2 = (bf16[6,32,128]{2,1,0:T(8,128)(2,1)S(1)}, bf16[6,32,128]{2,1,0:T(8,128)(2,1)S(1)}, u32[]{:S(2)}, u32[]{:S(2)}) collective-permute-start(bf16[6,32,128]{2,1,0:T(8,128)(2,1)S(1)} %get-tuple-element.20.refs_0_), channel_id=1, source_target_pairs={{0,6},{2,0},{4,2},{6,4},{8,14},{10,8},{12,10},{14,12},{16,22},{18,... | collective-permute-start | bytes 147464 | tf_op jit(solution)/shard_map/ppermute | solution.py:488
  12.2 3.4 %collective-permute-start.4 = (bf16[6,32,128]{2,1,0:T(8,128)(2,1)S(1)}, bf16[6,32,128]{2,1,0:T(8,128)(2,1)S(1)}, u32[]{:S(2)}, u32[]{:S(2)}) collective-permute-start(bf16[6,32,128]{2,1,0:T(8,128)(2,1)S(1)} %get-tuple-element.19), channel_id=1, source_target_pairs={{0,8},{2,16},{4,24},{6,0},{8,10},{10,18},{12,26},{14,2},{16,12},{1... | collective-permute-start | bytes 147464 | tf_op jit(solution)/shard_map/ppermute | solution.py:488
  15.7 0.9 %slice.46 = bf16[128,512]{1,0:T(8,128)(2,1)S(1)} slice(bf16[128,640]{1,0:T(8,128)(2,1)} %param.33), slice={[0:128], [0:512]} | slice | bytes 262144 | tf_op jit(solution)/shard_map/slice | solution.py:268
  16.8 3.4 %collective-permute-start.5 = (bf16[6,32,128]{2,1,0:T(8,128)(2,1)S(1)}, bf16[6,32,128]{2,1,0:T(8,128)(2,1)S(1)}, u32[]{:S(2)}, u32[]{:S(2)}) collective-permute-start(bf16[6,32,128]{2,1,0:T(8,128)(2,1)S(1)} %get-tuple-element.19), channel_id=1, source_target_pairs={{0,16},{2,24},{4,0},{6,8},{8,18},{10,26},{12,2},{14,10},{16,20},{1... | collective-permute-start | bytes 147464 | tf_op jit(solution)/shard_map/ppermute | solution.py:488
  20.2 2.2 %collective-permute-start.6 = (bf16[6,32,128]{2,1,0:T(8,128)(2,1)S(1)}, bf16[6,32,128]{2,1,0:T(8,128)(2,1)S(1)}, u32[]{:S(2)}, u32[]{:S(2)}) collective-permute-start(bf16[6,32,128]{2,1,0:T(8,128)(2,1)S(1)} %get-tuple-element.19), channel_id=1, source_target_pairs={{0,24},{2,0},{4,8},{6,16},{8,26},{10,2},{12,10},{14,18},{16,28},{1... | collective-permute-start | bytes 147464 | tf_op jit(solution)/shard_map/ppermute | solution.py:488
  22.4 1.3 %convert_reduce_fusion.1 = f32[]{:T(128)} fusion(s32[256]{0:T(256)} %param.19), kind=kLoop, calls=%fused_computation.92 | loop fusion | flops 511 | bytes 1028 | tf_op jit(solution)/shard_map/reduce_sum | solution.py:480
  25.4 3.6 %collective-permute-done.6.refs_7_ = bf16[6,32,128]{2,1,0:T(8,128)(2,1)S(1)} collective-permute-done((bf16[6,32,128]{2,1,0:T(8,128)(2,1)S(1)}, bf16[6,32,128]{2,1,0:T(8,128)(2,1)S(1)}, u32[]{:S(2)}, u32[]{:S(2)}) %collective-permute-start.6) | collective-permute-done | bytes 49184 | tf_op jit(solution)/shard_map/ppermute | solution.py:488
  29.7 4.3 %outer_stage.1 = f32[576,128]{1,0:T(8,128)} custom-call(s32[8]{0:T(128)} %stack.44.place, bf16[6,32,128]{2,1,0:T(8,128)(2,1)} %copy-done.3, bf16[6,32,128]{2,1,0:T(8,128)(2,1)} %copy-done.6, bf16[6,32,128]{2,1,0:T(8,128)(2,1)} %copy-done.7, bf16[6,32,128]{2,1,0:T(8,128)(2,1)} %copy-done.8, bf16[6,32,128]{2,1,0:T(8,128)(2,1)} %copy-done.9, ...), custom_call_target="tpu_custom_call" | custom-call | tf_op jit(solution)/shard_map/outer_stage/pallas_call | solution.py:235
  34.1 1.6 %collective-permute-done.7 = f32[576,128]{1,0:T(8,128)S(1)} collective-permute-done((f32[576,128]{1,0:T(8,128)}, f32[576,128]{1,0:T(8,128)S(1)}, u32[]{:S(2)}, u32[]{:S(2)}) %collective-permute-start.7) | collective-permute-done | bytes 294944 | tf_op jit(solution)/shard_map/ppermute | solution.py:494
  35.8 1.0 %add_multiply_fusion = f32[576,128]{1,0:T(8,128)S(1)} fusion(f32[576,128]{1,0:T(8,128)} %outer_stage.1, f32[576,128]{1,0:T(8,128)S(1)} %collective-permute-done.7, f32[]{:T(128)S(6)} %div.42), kind=kLoop, calls=%fused_computation.44 | loop fusion | flops 147456 | bytes 884740 | tf_op jit(solution)/shard_map/mul | solution.py:256
  37.3 1.7 %fusion.54 = (f32[24,8]{1,0:T(8,128)S(1)}, f32[24,8,24]{2,1,0:T(8,128)S(1)}) fusion(f32[24]{0:T(128)S(1)} %get-tuple-element.10, f32[128,8]{0,1:T(8,128)S(1)} %copy-done.16, bf16[24,24,128]{2,1,0:T(8,128)(2,1)S(1)} %get-tuple-element.13, f32[128]{0:T(128)S(1)} %copy-done.18, f32[24,24]{1,0:T(8,128)S(1)} %add_rsqrt_fusion.1, ...), kind=kOutput, calls=%fused_computation.95 | convolution fusion | flops 7381824 | bytes 175968 | tf_op jit(solution)/shard_map/ijc,ch->ihj/dot_general | solution.py:262
  42.1 18.1 %all_to_all.10.block = bf16[16,104,128]{2,1,0:T(8,128)(2,1)} all-to-all(bf16[16,104,128]{2,1,0:T(8,128)(2,1)S(1)} %bitcast_dynamic-update-slice_fusion), channel_id=1, replica_groups=mesh['row'=4,'col'=4,'depth'=2] {'row','col'}, dimensions={0} | all-to-all | bytes 851968 | tf_op jit(solution)/shard_map/all_to_all | solution.py:503
  60.1 4.0 %middle_stage.1 = bf16[16,48,128]{2,1,0:T(8,128)(2,1)} custom-call(bf16[16,104,128]{2,1,0:T(8,128)(2,1)} %all_to_all.10.block, f32[1,64]{1,0:T(1,128)} %bitcast.101, bf16[64,256]{1,0:T(8,128)(2,1)} %content.1, bf16[64,256]{1,0:T(8,128)(2,1)} %sigmoid_matrix.1, bf16[64,256]{1,0:T(8,128)(2,1)} %bitcast.100), custom_call_target="tpu_custom_call" | custom-call | tf_op jit(solution)/shard_map/middle_stage/pallas_call | solution.py:412
  64.2 3.7 %all-to-all-start.1 = ((bf16[16,48,128]{2,1,0:T(8,128)(2,1)}), bf16[16,48,128]{2,1,0:T(8,128)(2,1)S(1)}, u32[]{:S(2)}, u32[]{:S(2)}) async-start(bf16[16,48,128]{2,1,0:T(8,128)(2,1)} %middle_stage.1), calls=%async_computation.1 | async-start | bytes 393216 | tf_op jit(solution)/shard_map/all_to_all | solution.py:508
  67.9 8.4 %all-to-all-done.1 = bf16[16,48,128]{2,1,0:T(8,128)(2,1)S(1)} async-done(((bf16[16,48,128]{2,1,0:T(8,128)(2,1)}), bf16[16,48,128]{2,1,0:T(8,128)(2,1)S(1)}, u32[]{:S(2)}, u32[]{:S(2)}) %all-to-all-start.1) | async-done | bytes 196640 | tf_op jit(solution)/shard_map/all_to_all | solution.py:508
  76.4 1.8 %fusion.7 = f32[24,24,128]{2,1,0:T(8,128)} fusion(bf16[24,24,128]{2,1,0:T(8,128)(2,1)S(1)} %get-tuple-element.13, f32[128]{0:T(128)S(1)} %copy-done.14, f32[24,24]{1,0:T(8,128)S(1)} %add_rsqrt_fusion.1, f32[24,24]{1,0:T(8,128)S(1)} %broadcast_multiply_fusion.2, bf16[128,640]{1,0:T(8,128)(2,1)} %param.33), kind=kOutput, calls=%fused_computation.12 | convolution fusion | flops 19464192 | bytes 480256 | tf_op jit(solution)/shard_map/dot_general | solution.py:440
  79.8 0.8 copy.91
  80.9 1.0 %fusion.9 = bf16[24,24,128]{2,1,0:T(8,128)(2,1)} fusion(f32[24,24,128]{2,1,0:T(8,128)S(1)} %copy-done.2, bf16[24,24,128]{1,0,2:T(8,128)(2,1)S(1)} %fusion.2, bf16[24,24,128]{2,1,0:T(8,128)(2,1)S(1)} %get-tuple-element.13, bf16[128,128]{1,0:T(8,128)(2,1)S(1)} %copy-done), kind=kOutput, calls=%fused_computation.14 | convolution fusion | flops 19169280 | bytes 770048 | tf_op jit(solution)/shard_map/dot_general | solution.py:441
  (102 shorter events, 8.0 us)
Async XLA Ops:
  0.6 80.3 %copy-start = (bf16[128,128]{1,0:T(8,128)(2,1)S(1)}, bf16[128,128]{1,0:T(8,128)(2,1)}, u32[]{:S(2)}) copy-start(bf16[128,128]{1,0:T(8,128)(2,1)} %param.35) | copy-start | bytes 98308
  0.6 23.0 %copy-start.1 = (bf16[128,6,64]{0,2,1:T(8,128)(2,1)S(1)}, bf16[128,6,64]{0,2,1:T(8,128)(2,1)}, u32[]{:S(2)}) copy-start(bf16[128,6,64]{0,2,1:T(8,128)(2,1)} %param.18) | copy-start | bytes 294916
  0.7 23.2 %copy-start.17 = (s32[96]{0:T(128)S(1)}, s32[96]{0:T(128)}, u32[]{:S(2)}) copy-start(s32[96]{0:T(128)} %param.20) | copy-start | bytes 1156
  4.5 24.5 %copy-start.3 = (bf16[6,32,128]{2,1,0:T(8,128)(2,1)}, bf16[6,32,128]{2,1,0:T(8,128)(2,1)S(1)}, u32[]{:S(2)}) copy-start(bf16[6,32,128]{2,1,0:T(8,128)(2,1)S(1)} %get-tuple-element.20.refs_0_) | copy-start | bytes 147460
  4.5 12.2 %collective-permute-start = (bf16[6,32,128]{2,1,0:T(8,128)(2,1)S(1)}, bf16[6,32,128]{2,1,0:T(8,128)(2,1)S(1)}, u32[]{:S(2)}, u32[]{:S(2)}) collective-permute-start(bf16[6,32,128]{2,1,0:T(8,128)(2,1)S(1)} %get-tuple-element.20.refs_0_), channel_id=1, source_target_pairs={{0,2},{2,4},{4,6},{6,0},{8,10},{10,12},{12,14},{14,8},{16,18},{18,... | collective-permute-start | bytes 147464 | tf_op jit(solution)/shard_map/ppermute | solution.py:488
  7.6 12.5 %collective-permute-start.1 = (bf16[6,32,128]{2,1,0:T(8,128)(2,1)S(1)}, bf16[6,32,128]{2,1,0:T(8,128)(2,1)S(1)}, u32[]{:S(2)}, u32[]{:S(2)}) collective-permute-start(bf16[6,32,128]{2,1,0:T(8,128)(2,1)S(1)} %get-tuple-element.20.refs_0_), channel_id=1, source_target_pairs={{0,4},{2,6},{4,0},{6,2},{8,12},{10,14},{12,8},{14,10},{16,20},{18,... | collective-permute-start | bytes 147464 | tf_op jit(solution)/shard_map/ppermute | solution.py:488
  10.2 15.1 %collective-permute-start.2 = (bf16[6,32,128]{2,1,0:T(8,128)(2,1)S(1)}, bf16[6,32,128]{2,1,0:T(8,128)(2,1)S(1)}, u32[]{:S(2)}, u32[]{:S(2)}) collective-permute-start(bf16[6,32,128]{2,1,0:T(8,128)(2,1)S(1)} %get-tuple-element.20.refs_0_), channel_id=1, source_target_pairs={{0,6},{2,0},{4,2},{6,4},{8,14},{10,8},{12,10},{14,12},{16,22},{18,... | collective-permute-start | bytes 147464 | tf_op jit(solution)/shard_map/ppermute | solution.py:488
  11.6 13.8 %collective-permute-start.3 = (bf16[6,32,128]{2,1,0:T(8,128)(2,1)S(1)}, bf16[6,32,128]{2,1,0:T(8,128)(2,1)S(1)}, u32[]{:S(2)}, u32[]{:S(2)}) collective-permute-start(bf16[6,32,128]{2,1,0:T(8,128)(2,1)S(1)} %get-tuple-element.19), channel_id=1, source_target_pairs={{0,0},{2,8},{4,16},{6,24},{8,2},{10,10},{12,18},{14,26},{16,4},{18... | collective-permute-start | bytes 147464 | tf_op jit(solution)/shard_map/ppermute | solution.py:488
  12.2 13.1 %collective-permute-start.4 = (bf16[6,32,128]{2,1,0:T(8,128)(2,1)S(1)}, bf16[6,32,128]{2,1,0:T(8,128)(2,1)S(1)}, u32[]{:S(2)}, u32[]{:S(2)}) collective-permute-start(bf16[6,32,128]{2,1,0:T(8,128)(2,1)S(1)} %get-tuple-element.19), channel_id=1, source_target_pairs={{0,8},{2,16},{4,24},{6,0},{8,10},{10,18},{12,26},{14,2},{16,12},{1... | collective-permute-start | bytes 147464 | tf_op jit(solution)/shard_map/ppermute | solution.py:488
  16.6 20.2 %copy-start.4 = (bf16[24,24,128]{2,1,0:T(8,128)(2,1)S(1)}, bf16[24,24,128]{2,1,0:T(8,128)(2,1)}, u32[]{:S(2)}) copy-start(bf16[24,24,128]{2,1,0:T(8,128)(2,1)} %param.21) | copy-start | bytes 442372
  16.6 20.2 %copy-start.13 = (f32[128]{0:T(128)S(1)}, f32[128]{0:T(128)}, u32[]{:S(2)}) copy-start(f32[128]{0:T(128)} %param.25) | copy-start | bytes 1540
  16.8 12.3 %copy-start.6 = (bf16[6,32,128]{2,1,0:T(8,128)(2,1)}, bf16[6,32,128]{2,1,0:T(8,128)(2,1)S(1)}, u32[]{:S(2)}) copy-start(bf16[6,32,128]{2,1,0:T(8,128)(2,1)S(1)} %collective-permute-done.refs_1_) | copy-start | bytes 147460
  16.8 8.6 %collective-permute-start.5 = (bf16[6,32,128]{2,1,0:T(8,128)(2,1)S(1)}, bf16[6,32,128]{2,1,0:T(8,128)(2,1)S(1)}, u32[]{:S(2)}, u32[]{:S(2)}) collective-permute-start(bf16[6,32,128]{2,1,0:T(8,128)(2,1)S(1)} %get-tuple-element.19), channel_id=1, source_target_pairs={{0,16},{2,24},{4,0},{6,8},{8,18},{10,26},{12,2},{14,10},{16,20},{1... | collective-permute-start | bytes 147464 | tf_op jit(solution)/shard_map/ppermute | solution.py:488
  20.2 8.9 %copy-start.7 = (bf16[6,32,128]{2,1,0:T(8,128)(2,1)}, bf16[6,32,128]{2,1,0:T(8,128)(2,1)S(1)}, u32[]{:S(2)}) copy-start(bf16[6,32,128]{2,1,0:T(8,128)(2,1)S(1)} %collective-permute-done.1.refs_2_) | copy-start | bytes 147460
  20.2 8.9 %collective-permute-start.6 = (bf16[6,32,128]{2,1,0:T(8,128)(2,1)S(1)}, bf16[6,32,128]{2,1,0:T(8,128)(2,1)S(1)}, u32[]{:S(2)}, u32[]{:S(2)}) collective-permute-start(bf16[6,32,128]{2,1,0:T(8,128)(2,1)S(1)} %get-tuple-element.19), channel_id=1, source_target_pairs={{0,24},{2,0},{4,8},{6,16},{8,26},{10,2},{12,10},{14,18},{16,28},{1... | collective-permute-start | bytes 147464 | tf_op jit(solution)/shard_map/ppermute | solution.py:488
  23.9 13.4 %copy-start.16 = (f32[128,8]{0,1:T(8,128)S(1)}, f32[128,8]{0,1:T(8,128)}, u32[]{:S(2)}) copy-start(f32[128,8]{0,1:T(8,128)} %param.28) | copy-start | bytes 12292
  23.9 13.4 %copy-start.18 = (f32[128]{0:T(128)S(1)}, f32[128]{0:T(128)}, u32[]{:S(2)}) copy-start(f32[128]{0:T(128)} %param.27) | copy-start | bytes 1540
  25.4 14.0 %copy-start.14 = (f32[128]{0:T(128)S(1)}, f32[128]{0:T(128)}, u32[]{:S(2)}) copy-start(f32[128]{0:T(128)} %param.32) | copy-start | bytes 1540
  25.4 3.7 %copy-start.8 = (bf16[6,32,128]{2,1,0:T(8,128)(2,1)}, bf16[6,32,128]{2,1,0:T(8,128)(2,1)S(1)}, u32[]{:S(2)}) copy-start(bf16[6,32,128]{2,1,0:T(8,128)(2,1)S(1)} %collective-permute-done.2.refs_3_) | copy-start | bytes 147460
  25.4 3.7 %copy-start.9 = (bf16[6,32,128]{2,1,0:T(8,128)(2,1)}, bf16[6,32,128]{2,1,0:T(8,128)(2,1)S(1)}, u32[]{:S(2)}) copy-start(bf16[6,32,128]{2,1,0:T(8,128)(2,1)S(1)} %collective-permute-done.3.refs_4_) | copy-start | bytes 147460
  25.4 3.7 %copy-start.10 = (bf16[6,32,128]{2,1,0:T(8,128)(2,1)}, bf16[6,32,128]{2,1,0:T(8,128)(2,1)S(1)}, u32[]{:S(2)}) copy-start(bf16[6,32,128]{2,1,0:T(8,128)(2,1)S(1)} %collective-permute-done.4.refs_5_) | copy-start | bytes 147460
  34.0 1.8 %collective-permute-start.7 = (f32[576,128]{1,0:T(8,128)}, f32[576,128]{1,0:T(8,128)S(1)}, u32[]{:S(2)}, u32[]{:S(2)}) collective-permute-start(f32[576,128]{1,0:T(8,128)} %outer_stage.1), channel_id=1, source_target_pairs={{0,1},{1,0},{2,3},{3,2},{4,5},{5,4},{6,7},{7,6},{8,9},{9,8},{10,11... | collective-permute-start | bytes 884744 | tf_op jit(solution)/shard_map/ppermute | solution.py:494
  64.2 12.1 %all-to-all-start.1 = ((bf16[16,48,128]{2,1,0:T(8,128)(2,1)}), bf16[16,48,128]{2,1,0:T(8,128)(2,1)S(1)}, u32[]{:S(2)}, u32[]{:S(2)}) async-start(bf16[16,48,128]{2,1,0:T(8,128)(2,1)} %middle_stage.1), calls=%async_computation.1 | async-start | bytes 393216 | tf_op jit(solution)/shard_map/all_to_all | solution.py:508
  76.3 1.9 %collective-permute-start.8 = (bf16[16,24,128]{2,1,0:T(8,128)(2,1)S(1)}, bf16[16,24,128]{2,1,0:T(8,128)(2,1)S(1)}, u32[]{:S(2)}, u32[]{:S(2)}) collective-permute-start(bf16[16,24,128]{2,1,0:T(8,128)(2,1)S(1)} %slice.70), channel_id=1, source_target_pairs={{0,1},{1,0},{2,3},{3,2},{4,5},{5,4},{6,7},{7,6},{8,9},{9,8},{10,11... | collective-permute-start | bytes 294920 | tf_op jit(solution)/shard_map/ppermute | solution.py:510
  (6 other events, 9.2 us)

commit v4 on v3

--- a/solution.py
+++ b/solution.py
@@ -158,46 +158,111 @@
     return (revised_sequences, pair_output)
 
 
-def split_pieces(value, count):
-    pieces = []
-    for _ in range(count):
-        piece = lax.reduce_precision(value, 8, 7)
-        pieces.append(piece.astype(bf16))
-        value = value - piece
-    return pieces
-
-
-def factor_stage(tokens, flags, scale, entry):
-    value = tokens.astype(f32)
-    average = jnp.mean(value, 1, keepdims=True)
-    centred = value - average
-    variance = jnp.mean(centred * centred, 1, keepdims=True)
-    normed = (centred * lax.rsqrt(variance + epsilon) * scale[None, :, None]).astype(bf16)
-    factors = jnp.einsum("tcs,cf->tfs", normed, entry, preferred_element_type=f32)
-    return (factors * flags[None, None, :]).astype(bf16)
-
-
-def outer_kernel(place, *refs):
-    n, t, hidden = place.shape[0] // 2, refs[0].shape[0], refs[0].shape[1]
-    s = refs[0].shape[2]
+def in_vmem(array):
+    return pltpu.with_memory_space_constraint(array, pltpu.VMEM)
+
+
+def place_lanes(source, start, count, target, lane, base):
+    block, offset = start // 128, start % 128
+    shift = (target - offset) % 128
+    piece = source[:, block * 128 : (block + 1) * 128]
+    piece = pltpu.roll(piece, shift, 1) if shift else piece
+    if offset + count > 128:
+        rest = source[:, (block + 1) * 128 : (block + 2) * 128]
+        rest = pltpu.roll(rest, shift, 1) if shift else rest
+        piece = jnp.where(lane < target + 128 - offset, piece, rest)
+    return jnp.where((lane >= target) & (lane < target + count), piece, base)
+
+
+def unit_rows(value):
+    centred = value - jnp.mean(value, -1, keepdims=True)
+    variance = jnp.mean(centred * centred, -1, keepdims=True)
+    return centred * lax.rsqrt(variance + epsilon)
+
+
+def first_kernel(tokens_hbm, flags, scale, entry, couple_hbm, *refs):
+    n = len(refs) - 5
+    sends, right, pieces, tokens, couple, arrived = refs[:n], refs[n], *refs[n + 1 :]
+    t, ch, s = tokens.shape
+    hidden, part = entry.shape[1] // 2, couple.shape[0]
+    half, place = lax.axis_index("depth"), lax.axis_index("col")
+    copies = [
+        pltpu.make_async_copy(tokens_hbm, tokens, arrived.at[0]),
+        pltpu.make_async_copy(couple_hbm.at[pl.ds(half * part, part)], couple, arrived.at[1]),
+    ]
+    for copy in copies:
+        copy.start()
+    mask = flags[pl.ds(half, 1), :].astype(f32)
+    square = (ch, ch)
+    diagonal = lax.broadcasted_iota(jnp.int32, square, 0) == lax.broadcasted_iota(jnp.int32, square, 1)
+    column = jnp.sum(jnp.where(diagonal, scale[...], 0.0), 1, keepdims=True)
+    copies[0].wait()
+    lefts = []
+    for u in range(t):
+        value = tokens[u].astype(f32)
+        centred = value - jnp.mean(value, 0, keepdims=True)
+        variance = jnp.mean(centred * centred, 0, keepdims=True)
+        normed = (centred * lax.rsqrt(variance + epsilon) * column).astype(bf16)
+        factor = lax.dot_general(entry[...], normed, (((0,), (0,)), ((), ())), preferred_element_type=f32) * mask
+        lefts.append(factor[:hidden])
+        right[u] = factor[hidden:].astype(bf16)
+    copies[1].wait()
+    for i in range(part):
+        row = couple[i].astype(f32)
+        for k in range(n):
+            pieces[k, i * t : (i + 1) * t] = row[k * t : (k + 1) * t]
+    for k in range(n):
+        sends[k][...] = jnp.concatenate(lefts + [pieces[lax.rem(place + k, n)]], 0).astype(bf16)
+
+
+def first_stage(tokens, flags, scale, entry, couple, n):
+    t, ch, s = tokens.shape
+    rows, cols, width = couple.shape
+    hidden = entry.shape[1] // 2
+    vmem, hbm = pl.BlockSpec(memory_space=pltpu.VMEM), pl.BlockSpec(memory_space=pl.ANY)
+    length = t * hidden + rows // 2 * t
+    return pl.pallas_call(
+        first_kernel,
+        out_shape=[pltpu.VMEM((length, s), bf16)] * n + [pltpu.VMEM((t, hidden, s), bf16)],
+        in_specs=[hbm, vmem, vmem, vmem, hbm],
+        out_specs=[vmem] * (n + 1),
+        scratch_shapes=[
+            pltpu.VMEM((n, rows // 2 * t, width), f32),
+            pltpu.VMEM(tokens.shape, bf16),
+            pltpu.VMEM((rows // 2, cols, width), bf16),
+            pltpu.SemaphoreType.DMA((2,)),
+        ],
+        name="first_stage",
+    )(tokens, flags, scale, entry, couple)
+
+
+def outer_kernel(n, *refs):
+    half, row_index, col_index = lax.axis_index("depth"), lax.axis_index("row"), lax.axis_index("col")
     lefts, rights = refs[:n], refs[n : 2 * n]
-    final, out, left, pieces, right, plain, turned, outer, high, low = refs[2 * n :]
+    t, hidden, s = rights[0].shape
+    flags, final_hbm, out, left, pieces, right, plain, turned, outer, high, low, couples, couple, final, arrived = refs[2 * n :]
     tokens, ratio = n * t, 128 // hidden
+    copy = pltpu.make_async_copy(final_hbm, final, arrived)
+    copy.start()
     for k in range(n):
-        left[place[k]] = lefts[k][...].reshape(t * hidden, s)
-        pieces[place[n + k]] = rights[k][...].reshape(t * hidden, s).astype(f32)
+        sent = lefts[k][...].astype(f32)
+        place = lax.rem(col_index + (n - k), n)
+        left[place] = sent[: t * hidden].astype(bf16)
+        couples[place] = sent[t * hidden :]
+        pieces[row_index ^ k] = rights[k][...].reshape(t * hidden, s).astype(f32)
     for k in range(n):
         for u in range(t):
             right[pl.ds(k * t + u, hidden, stride=tokens), :] = pieces[k, u * hidden : (u + 1) * hidden, :]
-    plain[...] = final[...].astype(f32)
-    for d in range(hidden):
-        turned[d * hidden : (d + 1) * hidden, :] = plain[pl.ds(d, hidden, stride=hidden), :].astype(bf16)
     outer[...] = lax.dot_general(
         right[...].astype(bf16),
         left[...].reshape(tokens * hidden, s),
         (((1,), (1,)), ((), ())),
         preferred_element_type=f32,
     )
+    copy.wait()
+    plain[...] = final[...].astype(f32)
+    for d in range(hidden):
+        turned[d * hidden : (d + 1) * hidden, :] = plain[pl.ds(d, hidden, stride=hidden), :].astype(bf16)
     lane = lax.broadcasted_iota(jnp.int32, (tokens, 128), 1)
     for g in range(tokens // ratio):
         for q in range(hidden // ratio):
@@ -222,20 +287,28 @@
                 low[i * tokens : (i + 1) * tokens, q * 128 : (q + 1) * 128] = (
                     tiles[x] - rounded.astype(f32)
                 ).astype(bf16)
-    out[...] = jnp.dot(high[...], turned[...], preferred_element_type=f32) + jnp.dot(
+    part = tokens // 2
+    for k in range(n):
+        for i in range(part):
+            couple[i * tokens + k * t : i * tokens + (k + 1) * t] = couples[k, i * t : (i + 1) * t]
+    total = jnp.sum(flags[...].astype(f32)) + 0.001
+    update = jnp.dot(high[...], turned[...], preferred_element_type=f32) + jnp.dot(
         low[...], turned[...], preferred_element_type=f32
     )
-
-
-def outer_stage(place, lefts, rights, final):
+    out[...] = update / total
+    mine = pl.ds(pl.multiple_of(half * (part * tokens), 8), part * tokens)
+    out[mine, :] = out[mine, :] + couple[...]
+
+
+def outer_stage(lefts, rights, flags, final):
     n = len(lefts)
-    t, hidden, s = lefts[0].shape
+    t, hidden, s = rights[0].shape
     tokens, width = n * t, final.shape[1]
     vmem = pl.BlockSpec(memory_space=pltpu.VMEM)
     return pl.pallas_call(
-        outer_kernel,
-        out_shape=jax.ShapeDtypeStruct((tokens * tokens, width), f32),
-        in_specs=[pl.BlockSpec(memory_space=pltpu.SMEM)] + [vmem] * (2 * n + 1),
+        functools.partial(outer_kernel, n),
+        out_shape=pltpu.VMEM((tokens * tokens, width), f32),
+        in_specs=[vmem] * (2 * n + 1) + [pl.BlockSpec(memory_space=pl.ANY)],
         out_specs=vmem,
         scratch_shapes=[
             pltpu.VMEM((n, t * hidden, s), bf16),
@@ -246,57 +319,156 @@
             pltpu.VMEM((tokens * hidden, tokens * hidden), f32),
             pltpu.VMEM((tokens * tokens, hidden * hidden), bf16),
             pltpu.VMEM((tokens * tokens, hidden * hidden), bf16),
+            pltpu.VMEM((n, tokens // 2 * t, width), f32),
+            pltpu.VMEM((tokens // 2 * tokens, width), f32),
+            pltpu.VMEM(final.shape, bf16),
+            pltpu.SemaphoreType.DMA,
         ],
         name="outer_stage",
-    )(place, *lefts, *rights, final)
-
-
-def pair_stage(update, couple, inverse, offset, row_tokens, col_tokens, couple_scale, score, tri_scale, entry, half, parts):
-    rows, cols, width = couple.shape
-    pair_one = (couple.astype(f32) + update * inverse + offset).astype(bf16)
-    value = pair_one.astype(f32)
-    average = jnp.mean(value, -1, keepdims=True)
-    centred = value - average
-    variance = jnp.mean(centred * centred, -1, keepdims=True)
-    unit = centred * lax.rsqrt(variance + epsilon)
-    logits = jnp.einsum("ijc,ch->ihj", unit * couple_scale, score, precision=lax.Precision.HIGHEST)
-    logits = logits + 1000000000.0 * (col_tokens - 1.0)[None, None, :]
-    peak = jnp.max(logits, -1)
-    expo = jnp.exp(logits - peak[..., None]).astype(bf16).reshape(rows, -1)
-    normed = (unit * tri_scale).astype(bf16)
-    mine = lax.dynamic_slice_in_dim(
-        entry[:, : 4 * width].reshape(width, 4, 2, width // 2), half, 1, 2
-    ).reshape(width, 2 * width)
-    projected = jnp.einsum("ijz,zc->cij", normed, mine, preferred_element_type=f32)
-    projected = projected.reshape(4, width // 2, rows, cols)
-    mask = (row_tokens[:, None] * col_tokens[None, :])[None]
-    left = (jax.nn.sigmoid(projected[0]) * projected[1] * mask).astype(bf16)
-    right = (jax.nn.sigmoid(projected[2]) * projected[3] * mask).astype(bf16)
-
-    def by_peer(operand):
-        operand = operand.reshape(parts, -1, rows, cols)
-        return operand.transpose(0, 2, 1, 3).reshape(parts, rows, -1)
-
-    left, right = by_peer(left), by_peer(right)
-    spare = 128 - left.shape[-1]
-
-    def everyone(piece):
-        return jnp.broadcast_to(piece[None], (parts,) + piece.shape)
-
-    stats = jnp.concatenate(split_pieces(peak, 3), -1)
-    lanes = stats.shape[-1]
-    stats = stats.reshape(rows // 8, 8, lanes).transpose(1, 0, 2).reshape(8, -1)
-    stats = jnp.pad(stats, ((0, 0), (0, 128 - stats.shape[-1])))
-    block = jnp.concatenate(
-        [
-            jnp.concatenate([left, everyone(expo[:, 128 : 128 + spare])], -1),
-            jnp.concatenate([right, everyone(expo[:, 128 + spare : 128 + 2 * spare])], -1),
-            everyone(expo[:, :128]),
-            everyone(stats),
+    )(*map(in_vmem, lefts), *map(in_vmem, rights), flags, final)
+
+
+def pair_kernel(sizes, genuine, own, other, offset, couple_scale, score, tri_scale, entry_hbm, tokens_hbm, block, value, normed, projected, logits, tri, head_rows, entry, tokens, turned_entry, picked, arrived):
+    n, rows, cols, heads, feats = sizes
+    half, row_index, col_index = lax.axis_index("depth"), lax.axis_index("row"), lax.axis_index("col")
+    copies = [
+        pltpu.make_async_copy(entry_hbm.at[:, pl.ds(0, entry.shape[1])], entry, arrived.at[0]),
+        pltpu.make_async_copy(tokens_hbm, tokens, arrived.at[1]),
+    ]
+    for copy in copies:
+        copy.start()
+    parts, width = n * n, own.shape[1]
+    part, spare = rows // 2, 128 - feats * cols
+    total = own[...] + other[...] + offset[...]
+    value[...] = total.astype(bf16).astype(f32)
+    unit = unit_rows(value[...])
+    size = rows * cols
+    padded = normed.shape[0]
+    wide = lax.dot_general(
+        score[...], unit * couple_scale[...], (((1,), (1,)), ((), ())),
+        precision=lax.Precision.HIGHEST, preferred_element_type=f32,
+    )
+    logits[:, :size] = wide
+    lane8 = lax.broadcasted_iota(jnp.int32, (heads, 128), 1)
+    low = jnp.full((heads, 128), -jnp.inf, f32)
+    for i in range(rows):
+        head_rows[pl.ds(i, heads, stride=rows), :] = place_lanes(logits, i * cols, cols, 0, lane8, low)
+    t, ch, s = tokens.shape
+    line = lax.broadcasted_iota(jnp.int32, (8, 128), 1)
+    bias = jnp.zeros((8, 128), f32)
+    open_lanes = jnp.zeros((8, 128), f32)
+    for j in range(cols):
+        flag = genuine[j // t * rows + col_index * t + j % t].astype(f32)
+        bias = jnp.where(line == j, 1000000000.0 * (flag - 1.0), bias)
+        here = line == j
+        for f in range(1, feats):
+            here = here | (line == f * cols + j)
+        open_lanes = jnp.where(here, flag, open_lanes)
+    score_rows = head_rows[...] + bias[:1]
+    peak = jnp.max(score_rows, -1, keepdims=True)
+    expo = jnp.exp(score_rows - peak).astype(bf16).astype(f32)
+    lane = lax.broadcasted_iota(jnp.int32, (rows, 128), 1)
+    zero = jnp.zeros((rows, 128), f32)
+    tail = zero
+    flat = zero
+    for h in range(heads):
+        mine = expo[h * rows : (h + 1) * rows]
+        start = h * cols
+        if start < 128:
+            shifted = pltpu.roll(mine, start, 1) if start else mine
+            flat = jnp.where((lane >= start) & (lane < start + cols), shifted, flat)
+            if start + cols > 128:
+                tail = jnp.where(lane < start + cols - 128, shifted, tail)
+        else:
+            start -= 128
+            shifted = pltpu.roll(mine, start, 1) if start else mine
+            tail = jnp.where((lane >= start) & (lane < start + cols), shifted, tail)
+    first, second = pltpu.roll(tail, 128 - spare, 1), pltpu.roll(tail, 128 - 2 * spare, 1)
+    wide_peak = jnp.broadcast_to(peak, (heads * rows, 128))
+    tiny = lax.broadcasted_iota(jnp.int32, (8, 128), 1)
+    stats = jnp.zeros((8, 128), f32)
+    for q in range(3):
+        piece = wide_peak.astype(bf16).astype(f32)
+        wide_peak = wide_peak - piece
+        for a in range(rows // 8):
+            for h in range(heads):
+                stats = jnp.where(
+                    tiny == a * 3 * heads + q * heads + h, piece[h * rows + a * 8 : h * rows + a * 8 + 8], stats
+                )
+    normed[:size] = (unit * tri_scale[...]).astype(bf16)
+    normed[size:] = jnp.zeros((padded - size, width), bf16)
+    copies[0].wait()
+    turned_entry[...] = entry[...].astype(f32).T
+    group = feats * parts
+    for k in range(4):
+        start = pl.multiple_of(k * width + half * group, 8)
+        turned_entry[k * group : (k + 1) * group] = turned_entry[pl.ds(start, group), :]
+    for k in range(4):
+        for f in range(feats):
+            picked[(k * feats + f) * parts : (k * feats + f + 1) * parts] = turned_entry[
+                pl.ds(k * group + f, parts, stride=feats), :
+            ].astype(bf16)
+    raw = lax.dot_general(picked[...], normed[...], (((1,), (1,)), ((), ())), preferred_element_type=f32)
+    cut = lax.broadcasted_iota(jnp.int32, (parts, 128), 1)
+    empty = jnp.zeros((parts, 128), f32)
+    for side in range(2):
+        base = side * 2 * group
+        projected[...] = jax.nn.sigmoid(raw[base : base + group]) * raw[base + group : base + 2 * group]
+        for i in range(rows):
+            packed = empty
+            for f in range(feats):
+                packed = place_lanes(projected.at[f * parts : (f + 1) * parts], i * cols, cols, f * cols, cut, packed)
+            flag = genuine[row_index * rows + i].astype(f32)
+            tri[side, pl.ds(i, parts, stride=rows), :] = packed * (open_lanes[:1] * flag)
+    copies[1].wait()
+    turned = tokens[...].astype(f32).reshape(t * ch, s).T
+    keep = lane < feats * cols
+    for p in range(parts):
+        slabs = [
+            jnp.where(keep, tri[0, p * rows : (p + 1) * rows], first),
+            jnp.where(keep, tri[1, p * rows : (p + 1) * rows], second),
+            flat,
+            stats,
+        ]
+        slabs += [turned[p * 8 : (p + 1) * 8, a * 128 : (a + 1) * 128] for a in range(t * ch // 128)]
+        if p < part:
+            slabs.append(value[pl.ds(pl.multiple_of((half * part + p) * cols, 8), cols), :])
+        else:
+            slabs.append(jnp.zeros((cols, width), f32))
+        block[p] = jnp.concatenate(slabs, 0).astype(bf16)
+
+
+def pair_stage(genuine, own, other, offset, couple_scale, score, tri_scale, entry, tokens, n, rows, cols):
+    parts, width = n * n, own.shape[1]
+    heads = score.shape[0]
+    feats = width // (2 * parts)
+    t, ch, s = tokens.shape
+    padded = (rows * cols + 127) // 128 * 128
+    vmem, hbm = pl.BlockSpec(memory_space=pltpu.VMEM), pl.BlockSpec(memory_space=pl.ANY)
+    length = 3 * rows + 8 + t * ch // 128 * 8 + cols
+    return pl.pallas_call(
+        functools.partial(pair_kernel, (n, rows, cols, heads, feats)),
+        out_shape=pltpu.VMEM((parts, length, 128), bf16),
+        in_specs=[pl.BlockSpec(memory_space=pltpu.SMEM)] + [vmem] * 6 + [hbm] * 2,
+        out_specs=vmem,
+        scratch_shapes=[
+            pltpu.VMEM((rows * cols, width), f32),
+            pltpu.VMEM((padded, width), bf16),
+            pltpu.VMEM((feats * parts, padded), f32),
+            pltpu.VMEM((heads, padded), f32),
+            pltpu.VMEM((2, parts * rows, 128), f32),
+            pltpu.VMEM((heads * rows, 128), f32),
+            pltpu.VMEM((width, 4 * width), bf16),
+            pltpu.VMEM(tokens.shape, bf16),
+            pltpu.VMEM((4 * width, width), f32),
+            pltpu.VMEM((4 * feats * parts, width), bf16),
+            pltpu.SemaphoreType.DMA((2,)),
         ],
-        1,
-    )
-    return pair_one, block
+        name="pair_stage",
+    )(
+        genuine, in_vmem(own), in_vmem(other), offset.reshape(1, -1), couple_scale.reshape(1, -1), score, tri_scale.reshape(1, -1),
+        entry, tokens,
+    )
 
 
 def halves(value):
@@ -394,7 +566,8 @@
             piece = product[f * tokens + r * rows : f * tokens + (r + 1) * rows]
             piece = pltpu.roll(piece, shift, 1) if shift else piece
             slab = jnp.where((small >= f * cols) & (small < (f + 1) * cols), piece, slab)
-        slabs = [slab]
+        start = 3 * rows + 8 + 8 * groups + c * t
+        slabs = [slab] + [wide[r * n + k, start : start + t] for k in range(n)]
         for g in range(groups):
             merged = revised[pl.ds(p * t + g * per, s, stride=tokens), :]
             for k in range(1, per):
@@ -406,12 +579,12 @@
 
 def middle_stage(block, n, rows, cols, heads, feats, order, seq_scale, content, sigmoid_matrix, final):
     parts, tokens = n * n, n * rows
-    groups = (block.shape[1] - 3 * rows - 8) // 8
+    groups = (block.shape[1] - 3 * rows - 8 - cols) // 8
     width = content.shape[1]
     vmem = pl.BlockSpec(memory_space=pltpu.VMEM)
     return pl.pallas_call(
         functools.partial(middle_kernel, (n, rows, cols, heads, feats, groups, order)),
-        out_shape=jax.ShapeDtypeStruct((parts, rows + 8 * groups, 128), bf16),
+        out_shape=pltpu.VMEM((parts, rows + cols + 8 * groups, 128), bf16),
         in_specs=[vmem] * 5,
         out_specs=vmem,
         scratch_shapes=[
@@ -427,21 +600,88 @@
             pltpu.VMEM((8 * tokens, 128), f32),
         ],
         name="middle_stage",
-    )(block, seq_scale.reshape(1, -1), content, sigmoid_matrix, final.T)
-
-
-def final_stage(product, pair_one, tri_scale, entry, result_scale, final):
-    rows, cols, width = pair_one.shape
-    depth, parts = product.shape[:2]
-    feats = width // (depth * parts)
-    product = product[..., : feats * cols].reshape(depth, parts, rows, feats, cols)
-    product = product.transpose(2, 4, 0, 1, 3).reshape(rows, cols, width)
-    normed = standardize_features(pair_one, tri_scale).astype(bf16)
-    gate = jax.nn.sigmoid(jnp.dot(normed, entry[:, 4 * width :], preferred_element_type=f32))
-    final = gate * jnp.dot(
-        standardize_features(product, result_scale).astype(bf16), final, preferred_element_type=f32
-    )
-    return (pair_one.astype(f32) + final).astype(bf16)
+    )(in_vmem(block), seq_scale.reshape(1, -1), content, sigmoid_matrix, final.T)
+
+
+def last_kernel(sizes, own, other, tri_scale, result_scale, entry_hbm, final_hbm, pair_output, revised, product, turned, pair, entry, final, plain, mixed, arrived):
+    n, rows, cols, feats = sizes
+    copies = [
+        pltpu.make_async_copy(entry_hbm.at[:, pl.ds(4 * final.shape[1], final.shape[1])], entry, arrived.at[0]),
+        pltpu.make_async_copy(final_hbm, final, arrived.at[1]),
+    ]
+    for copy in copies:
+        copy.start()
+    parts, width = n * n, final.shape[1]
+    part, wide = rows // 2, 2 * n * n
+    mine = lax.axis_index("depth")
+    theirs = 1 - mine
+    for p in range(parts):
+        here, there = own[p].astype(f32), other[p].astype(f32)
+        product[mine, p * rows : (p + 1) * rows] = here[:rows]
+        product[theirs, p * rows : (p + 1) * rows] = there[:rows]
+        if p < part:
+            pair[pl.ds(pl.multiple_of((mine * part + p) * cols, 8), cols), :] = here[rows : rows + cols]
+            pair[pl.ds(pl.multiple_of((theirs * part + p) * cols, 8), cols), :] = there[rows : rows + cols]
+    lane = lax.broadcasted_iota(jnp.int32, (cols, 128), 1)
+    per = 128 // wide
+    for g in range(rows // per):
+        stacked = []
+        for k in range(per):
+            for d in range(2):
+                stacked.append(product[d, pl.ds(g * per + k, parts, stride=rows), :])
+        flipped = jnp.concatenate(stacked, 0).T
+        for k in range(per):
+            merged = jnp.zeros((cols, 128), f32)
+            for f in range(feats):
+                merged = place_lanes(flipped[f * cols : (f + 1) * cols], k * wide, wide, f * wide, lane, merged)
+            turned[(g * per + k) * cols : (g * per + k + 1) * cols] = merged
+    value = pair[...]
+    normed = (unit_rows(value) * tri_scale[...]).astype(bf16)
+    for copy in copies:
+        copy.wait()
+    gate = jax.nn.sigmoid(jnp.dot(normed, entry[...], preferred_element_type=f32))
+    plain[...] = final[...].astype(f32)
+    for f in range(feats):
+        mixed[f * wide : (f + 1) * wide] = plain[pl.ds(f, wide, stride=feats), :].astype(bf16)
+    at = lax.broadcasted_iota(jnp.int32, (width, width), 1)
+    origin = lax.broadcasted_iota(jnp.int32, (width, width), 0)
+    goal = lax.rem(origin, feats) * wide + lax.div(origin, feats)
+    scale = jnp.dot(
+        result_scale[...], (at == goal).astype(f32), precision=lax.Precision.HIGHEST, preferred_element_type=f32
+    )
+    result = (unit_rows(turned[...]) * scale).astype(bf16)
+    pair_output[...] = (value + gate * jnp.dot(result, mixed[...], preferred_element_type=f32)).astype(bf16)
+    for a in range((own.shape[1] - rows - cols) // 8):
+        start = rows + cols + 8 * a
+        flipped = jnp.concatenate([own[p, start : start + 8].astype(f32) for p in range(parts)], 0).T
+        revised[a * 128 : (a + 1) * 128] = flipped.astype(bf16)
+
+
+def last_stage(own, other, tri_scale, entry, result_scale, final, n, rows, cols, t, ch):
+    parts, width = n * n, final.shape[1]
+    feats = width // (2 * parts)
+    vmem, hbm = pl.BlockSpec(memory_space=pltpu.VMEM), pl.BlockSpec(memory_space=pl.ANY)
+    pair_output, revised = pl.pallas_call(
+        functools.partial(last_kernel, (n, rows, cols, feats)),
+        out_shape=[
+            jax.ShapeDtypeStruct((rows * cols, width), bf16),
+            jax.ShapeDtypeStruct((t * ch, 8 * parts), bf16),
+        ],
+        in_specs=[vmem] * 4 + [hbm] * 2,
+        out_specs=[vmem] * 2,
+        scratch_shapes=[
+            pltpu.VMEM((2, parts * rows, 128), f32),
+            pltpu.VMEM((rows * cols, 128), f32),
+            pltpu.VMEM((rows * cols, width), f32),
+            pltpu.VMEM((width, width), bf16),
+            pltpu.VMEM((width, width), bf16),
+            pltpu.VMEM((width, width), f32),
+            pltpu.VMEM((width, width), bf16),
+            pltpu.SemaphoreType.DMA((2,)),
+        ],
+        name="last_stage",
+    )(in_vmem(own), in_vmem(other), tri_scale.reshape(1, -1), result_scale.reshape(1, -1), entry, final)
+    return revised.reshape(t, ch, 8 * parts).transpose(2, 0, 1), pair_output.reshape(rows, cols, width)
 
 
 def on_device(
@@ -466,56 +706,38 @@
 ):
     n = lax.axis_size("row")
     parts = n * n
-    row_index = lax.axis_index("row")
-    col_index = lax.axis_index("col")
-    half = lax.axis_index("depth")
     rows, cols, width = couple_state.shape
     count, t, ch = sequence_stack.shape
     hidden = tensor_entry_matrix.shape[1] // 2
     heads = mean_score_matrix.shape[1]
     feats = width // (2 * parts)
-    order = tuple(((c * cols, cols),) for c in range(n))
-    token_weight = genuine_residue_flags.astype(f32)
-    flags = present_sequence_flags.astype(f32)
-    inverse = 1.0 / (jnp.sum(flags) + 0.001)
-    my_flags = lax.dynamic_slice_in_dim(flags, half * count, count)
+    order = tuple(tuple((r * rows + c * t, t) for r in range(n)) for c in range(n))
+    flags = present_sequence_flags.reshape(2, count)
     tokens = sequence_stack.transpose(1, 2, 0)
-    factors = factor_stage(tokens, my_flags, tensor_scale, tensor_entry_matrix)
-    left, right = factors[:, :hidden], factors[:, hidden:]
+    *sends, right = first_stage(tokens, flags, tensor_scale.reshape(1, ch), tensor_entry_matrix, couple_state, n)
 
     def move(array, where):
         pairs = [(r * n + c, where(r, c)[0] * n + where(r, c)[1]) for r in range(n) for c in range(n)]
         return lax.ppermute(array, ("row", "col"), pairs)
 
-    lefts = [left] + [move(left, lambda r, c, k=k: (r, (c + k) % n)) for k in range(1, n)]
-    rights = [move(right, lambda r, c, k=k: ((c + k) % n, r)) for k in range(n)]
-    place = jnp.stack([(col_index - k) % n for k in range(n)] + [(row_index - k) % n for k in range(n)])
-    update = outer_stage(place.astype(jnp.int32), lefts, rights, tensor_final_matrix)
-    update = update + lax.ppermute(update, "depth", [(0, 1), (1, 0)])
-    row_tokens = lax.dynamic_slice_in_dim(token_weight, row_index * rows, rows)
-    col_tokens = lax.dynamic_slice_in_dim(token_weight, col_index * cols, cols)
-    pair_one, block = pair_stage(
-        update.reshape(rows, cols, width), couple_state, inverse, tensor_offset, row_tokens, col_tokens, mean_couple_scale,
-        mean_score_matrix, trimul_scale, trimul_entry_matrix, half, parts,
-    )
-    slab = sequence_stack.reshape(parts, 8, t * ch // 128, 128).transpose(0, 2, 1, 3)
-    slab = slab.reshape(parts, -1, 128)
-    block = lax.all_to_all(jnp.concatenate([block, slab], 1), ("row", "col"), 0, 0, tiled=True)
+    rights = [right] + [move(right, lambda r, c, k=k: (r ^ k, c)) for k in range(1, n)]
+    lefts = [sends[0]] + [move(sends[k], lambda r, c, k=k: (r, (c + k) % n)) for k in range(1, n)]
+    share = outer_stage(lefts, rights, flags, tensor_final_matrix)
+    other = lax.ppermute(share, "depth", [(0, 1), (1, 0)])
+    block = pair_stage(
+        genuine_residue_flags, share, other, tensor_offset, mean_couple_scale, mean_score_matrix.T, trimul_scale,
+        trimul_entry_matrix, tokens, n, rows, cols,
+    )
+    block = lax.all_to_all(block, ("row", "col"), 0, 0, tiled=True)
     block = middle_stage(
         block, n, rows, cols, heads, feats, order, mean_sequence_scale, mean_content_matrix, mean_sigmoid_matrix,
         mean_final_matrix,
     )
     block = lax.all_to_all(block, ("row", "col"), 0, 0, tiled=True)
-    product = block[:, :rows]
-    other = lax.ppermute(product, "depth", [(0, 1), (1, 0)])
-    first = half == 0
-    product = jnp.stack([jnp.where(first, product, other), jnp.where(first, other, product)])
-    revised = block[:, rows:].reshape(parts, t * ch // 128, 8, 128).transpose(0, 2, 1, 3)
-    revised = revised.reshape(count, t, ch)
-    pair_output = final_stage(
-        product, pair_one, trimul_scale, trimul_entry_matrix, trimul_result_scale, trimul_final_matrix
-    )
-    return (revised, pair_output)
+    other = lax.ppermute(block[:, : rows + cols], "depth", [(0, 1), (1, 0)])
+    return last_stage(
+        block, other, trimul_scale, trimul_entry_matrix, trimul_result_scale, trimul_final_matrix, n, rows, cols, t, ch
+    )
 
 
 def suits(mesh):

time: 82.5 us -> 68.1 us (0.83)
  blocking collectives: 18.1 us -> 33.9 us
  starting transfers between devices: 20.5 us -> 10.7 us
  Pallas kernels: 8.28 us -> 15.7 us
  waiting for transfers between devices: 13.7 us -> 6.56 us
  other arithmetic: 6.99 us -> 0 us
  local copies, waits for them, and re-layouts: 6.42 us -> 0.01 us
  matrix products: 6.11 us -> 0 us
  between operations: 1.88 us -> 0.69 us
    all_to_all x1 -> x2, blocking collectives: 18.1 us -> 33.9 us  [on_device(): block = lax.all_to_all(block, ('row', 'col'), 0, 0, tiled=True)]
    all_to_all x1 -> x0, waiting for transfers between devices: 8.39 us -> none  [on_device(): block = lax.all_to_all(block, ('row', 'col'), 0, 0, tiled=True)]
    pallas_call x1 -> x4, Pallas kernels: 4.25 us -> 12.6 us  [the longest x1 4.18 us: outer_stage(): pl.pallas_call(functools.partial(outer_kernel, n), out_shape=pltpu.VMEM((...]
    ppermute x7 -> x6, starting transfers between devices: 16.7 us -> 10.5 us  [move(): return lax.ppermute(array, ('row', 'col'), pairs)]
    dot_general x5 -> x0, matrix products: 6.11 us -> none  [the longest x1 1.85 us: final_stage(): jnp.dot(normed, entry[:, 4 * width:], preferred_element_type=f32)]
    reduce_sum x7 -> x0, other arithmetic: 3.98 us -> none  [the longest x1 1.25 us: on_device(): inverse = 1.0 / (jnp.sum(flags) + 0.001)]
    all_to_all x1 -> x0, starting transfers between devices: 3.7 us -> none  [on_device(): block = lax.all_to_all(block, ('row', 'col'), 0, 0, tiled=True)]
    unnamed x43 -> x0, local copies, waits for them, and re-layouts: 1.87 us -> none
  transfers between devices with their start and end apart: 10 -> 8, of which waited for: 3 -> 4; matrix products, arithmetic and copies ran while one was open for 6% -> 0% of each run, Pallas kernels for 0% -> 0%
where the time goes in v4:
time: 68.1 us; the launch traced here: 67.6 us
  blocking collectives  33.9 us (50%)
  Pallas kernels  15.7 us (23%)
  starting transfers between devices  10.7 us (16%)
  waiting for transfers between devices  6.56 us (10%)
  between operations  0.69 us (1%)
    all_to_all x2, blocking collectives, on_device(): block = lax.all_to_all(block, ('row', 'col'), 0, 0, tiled=True)  33.9 us
    ppermute x6, starting transfers between devices, move(): return lax.ppermute(array, ('row', 'col'), pairs)  10.5 us
    pallas_call x1, Pallas kernels, outer_stage(): pl.pallas_call(functools.partial(outer_kernel, n), out_shape=pltpu.VMEM((...  4.18 us
    ppermute x6, waiting for transfers between devices, move(): return lax.ppermute(array, ('row', 'col'), pairs)  3.56 us
    pallas_call x1, Pallas kernels, pair_stage(): pl.pallas_call(functools.partial(pair_kernel, (n, rows, cols, heads, feat...  3.45 us
    pallas_call x1, Pallas kernels, middle_stage(): pl.pallas_call(functools.partial(middle_kernel, (n, rows, cols, heads, fe...  3.17 us
    pallas_call x1, Pallas kernels, last_stage(): pl.pallas_call(functools.partial(last_kernel, (n, rows, cols, feats)), ou...  2.99 us
    pallas_call x1, Pallas kernels, first_stage(): pl.pallas_call(first_kernel, out_shape=[pltpu.VMEM((length, s), bf16)] *...  1.93 us
  transfers between devices with their start and end apart: 8, of which 4 were waited for; matrix products, arithmetic and copies ran while one was open for 0% of the time, Pallas kernels for 0%

profile of v4, /device:TPU:0, one launch (start us, length us, event | category | flops | bytes accessed | tf_op | source)
XLA Modules:
  0.0 67.6 jit_solution(7915135873203949134)
XLA Ops:
  0.6 1.9 %first_stage.1 = (bf16[264,128]{1,0:T(8,128)(2,1)S(1)}, bf16[264,128]{1,0:T(8,128)(2,1)S(1)}, bf16[264,128]{1,0:T(8,128)(2,1)S(1)}, bf16[264,128]{1,0:T(8,128)(2,1)S(1)}, bf16[6,32,128]{2,1,0:T(8,128)(2,1)S(1)}) custom-call(bf16[6,64,128]{2,1,0:T(8,128)(2,1)} %bitcast.14, s32[2,128]{1,0:T(2,128)} %bitcast.18, f32[1,64]{1,0:T(1,128)} %bitcast.22, ...), custom_call_target="tpu_custom_call" | custom-call | tf_op jit(solution)/shard_map/first_stage/pallas_call | solution.py:224
  2.6 4.0 %collective-permute-start.5 = (bf16[6,32,128]{2,1,0:T(8,128)(2,1)S(1)}, bf16[6,32,128]{2,1,0:T(8,128)(2,1)S(1)}, u32[]{:S(2)}, u32[]{:S(2)}) collective-permute-start(bf16[6,32,128]{2,1,0:T(8,128)(2,1)S(1)} %get-tuple-element.13.refs_4_), channel_id=1, source_target_pairs={{0,24},{2,26},{4,28},{6,30},{8,16},{10,18},{12,20},{14,22},{16,8},... | collective-permute-start | bytes 147464 | tf_op jit(solution)/shard_map/ppermute | solution.py:721
  6.6 1.6 %collective-permute-start = (bf16[264,128]{1,0:T(8,128)(2,1)S(1)}, bf16[264,128]{1,0:T(8,128)(2,1)S(1)}, u32[]{:S(2)}, u32[]{:S(2)}) collective-permute-start(bf16[264,128]{1,0:T(8,128)(2,1)S(1)} %get-tuple-element.10), channel_id=1, source_target_pairs={{0,2},{2,4},{4,6},{6,0},{8,10},{10,12},{12,14},{14,8},{16,18},{18,... | collective-permute-start | bytes 202760 | tf_op jit(solution)/shard_map/ppermute | solution.py:721
  8.1 2.6 %collective-permute-start.1 = (bf16[264,128]{1,0:T(8,128)(2,1)S(1)}, bf16[264,128]{1,0:T(8,128)(2,1)S(1)}, u32[]{:S(2)}, u32[]{:S(2)}) collective-permute-start(bf16[264,128]{1,0:T(8,128)(2,1)S(1)} %get-tuple-element.11), channel_id=1, source_target_pairs={{0,4},{2,6},{4,0},{6,2},{8,12},{10,14},{12,8},{14,10},{16,20},{18,... | collective-permute-start | bytes 202760 | tf_op jit(solution)/shard_map/ppermute | solution.py:721
  10.7 1.3 %collective-permute-start.2 = (bf16[264,128]{1,0:T(8,128)(2,1)S(1)}, bf16[264,128]{1,0:T(8,128)(2,1)S(1)}, u32[]{:S(2)}, u32[]{:S(2)}) collective-permute-start(bf16[264,128]{1,0:T(8,128)(2,1)S(1)} %get-tuple-element.12), channel_id=1, source_target_pairs={{0,6},{2,0},{4,2},{6,4},{8,14},{10,8},{12,10},{14,12},{16,22},{18,... | collective-permute-start | bytes 202760 | tf_op jit(solution)/shard_map/ppermute | solution.py:721
  12.1 0.5 collective-permute-start.4
  12.6 0.0 collective-permute-done.5.refs_7_
  12.6 0.5 collective-permute-start.3
  13.1 3.0 %collective-permute-done.4.refs_6_ = bf16[6,32,128]{2,1,0:T(8,128)(2,1)S(1)} collective-permute-done((bf16[6,32,128]{2,1,0:T(8,128)(2,1)S(1)}, bf16[6,32,128]{2,1,0:T(8,128)(2,1)S(1)}, u32[]{:S(2)}, u32[]{:S(2)}) %collective-permute-start.4) | collective-permute-done | bytes 49184 | tf_op jit(solution)/shard_map/ppermute | solution.py:721
  16.2 0.5 collective-permute-done.3.refs_5_
  16.7 0.0 collective-permute-done.refs_1_
  16.7 0.0 collective-permute-done.1.refs_2_
  16.7 0.0 collective-permute-done.2.refs_3_
  16.7 4.2 %outer_stage.1.own = f32[576,128]{1,0:T(8,128)S(1)} custom-call(bf16[264,128]{1,0:T(8,128)(2,1)S(1)} %get-tuple-element.9.refs_0_, bf16[264,128]{1,0:T(8,128)(2,1)S(1)} %collective-permute-done.refs_1_, bf16[264,128]{1,0:T(8,128)(2,1)S(1)} %collective-permute-done.1.refs_2_, bf16[264,128]{1,0:T(8,128)(2,1)S(1)} %collective-permute-done.2.refs_3_, ...), custom_call_target="tpu_custom_call" | custom-call | tf_op jit(solution)/shard_map/outer_stage/pallas_call | solution.py:308
  20.9 0.1 collective-permute-start.6
  20.9 1.6 %collective-permute-done.6.other = f32[576,128]{1,0:T(8,128)S(1)} collective-permute-done((f32[576,128]{1,0:T(8,128)S(1)}, f32[576,128]{1,0:T(8,128)S(1)}, u32[]{:S(2)}, u32[]{:S(2)}) %collective-permute-start.6) | collective-permute-done | bytes 294944 | tf_op jit(solution)/shard_map/ppermute | solution.py:726
  22.5 3.5 %pair_stage.1 = bf16[16,128,128]{2,1,0:T(8,128)(2,1)S(1)} custom-call(s32[96]{0:T(128)} %genuine.1, f32[576,128]{1,0:T(8,128)S(1)} %outer_stage.1.own, f32[576,128]{1,0:T(8,128)S(1)} %collective-permute-done.6.other, f32[1,128]{1,0:T(1,128)} %bitcast.23, f32[1,128]{1,0:T(1,128)} %bitcast.24, f32[8,128]{1,0:T(8,128)} %bitcast.17, f32[1,128]{1,0:T(1,128)} %bitcast.20, ...), custom_call_target="tpu_custom_call" | custom-call | tf_op jit(solution)/shard_map/pair_stage/pallas_call | solution.py:449
  26.0 19.8 %all_to_all.10.block = bf16[16,128,128]{2,1,0:T(8,128)(2,1)S(1)} all-to-all(bf16[16,128,128]{2,1,0:T(8,128)(2,1)S(1)} %pair_stage.1), channel_id=1, replica_groups=mesh['row'=4,'col'=4,'depth'=2] {'row','col'}, dimensions={0} | all-to-all | bytes 1048576 | tf_op jit(solution)/shard_map/all_to_all | solution.py:731
  45.8 3.2 %middle_stage.1 = bf16[16,72,128]{2,1,0:T(8,128)(2,1)S(1)} custom-call(bf16[16,128,128]{2,1,0:T(8,128)(2,1)S(1)} %all_to_all.10.block, f32[1,64]{1,0:T(1,128)} %bitcast.25, bf16[64,256]{1,0:T(8,128)(2,1)} %content.1, bf16[64,256]{1,0:T(8,128)(2,1)} %sigmoid_matrix.1, bf16[64,256]{1,0:T(8,128)(2,1)} %bitcast.16), custom_call_target="tpu_custom_call" | custom-call | tf_op jit(solution)/shard_map/middle_stage/pallas_call | solution.py:585
  48.9 14.1 %all_to_all.11.own = bf16[16,72,128]{2,1,0:T(8,128)(2,1)S(1)} all-to-all(bf16[16,72,128]{2,1,0:T(8,128)(2,1)S(1)} %middle_stage.1), channel_id=1, replica_groups=mesh['row'=4,'col'=4,'depth'=2] {'row','col'}, dimensions={0} | all-to-all | bytes 589824 | tf_op jit(solution)/shard_map/all_to_all | solution.py:736
  63.1 0.1 collective-permute-start.7
  63.2 1.4 %collective-permute-done.7.other = bf16[16,48,128]{2,1,0:T(8,128)(2,1)S(1)} collective-permute-done((bf16[16,48,128]{2,1,0:T(8,128)(2,1)S(1)}, bf16[16,48,128]{2,1,0:T(8,128)(2,1)S(1)}, u32[]{:S(2)}, u32[]{:S(2)}) %collective-permute-start.7) | collective-permute-done | bytes 196640 | tf_op jit(solution)/shard_map/ppermute | solution.py:737
  64.6 3.0 %last_stage.1 = (bf16[576,128]{1,0:T(8,128)(2,1)}, bf16[384,128]{1,0:T(8,128)(2,1)}) custom-call(bf16[16,72,128]{2,1,0:T(8,128)(2,1)S(1)} %all_to_all.11.own, bf16[16,48,128]{2,1,0:T(8,128)(2,1)S(1)} %collective-permute-done.7.other, f32[1,128]{1,0:T(1,128)} %bitcast.21, f32[1,128]{1,0:T(1,128)} %bitcast.26, bf16[128,640]{1,0:T(8,128)(2,1)} %entry_hbm.3, ...), custom_call_target="tpu_custom_call" | custom-call | tf_op jit(solution)/shard_map/last_stage/pallas_call | solution.py:664
  (1 shorter events, 0.0 us)
Async XLA Ops:
  2.6 10.0 %collective-permute-start.5 = (bf16[6,32,128]{2,1,0:T(8,128)(2,1)S(1)}, bf16[6,32,128]{2,1,0:T(8,128)(2,1)S(1)}, u32[]{:S(2)}, u32[]{:S(2)}) collective-permute-start(bf16[6,32,128]{2,1,0:T(8,128)(2,1)S(1)} %get-tuple-element.13.refs_4_), channel_id=1, source_target_pairs={{0,24},{2,26},{4,28},{6,30},{8,16},{10,18},{12,20},{14,22},{16,8},... | collective-permute-start | bytes 147464 | tf_op jit(solution)/shard_map/ppermute | solution.py:721
  6.6 10.1 %collective-permute-start = (bf16[264,128]{1,0:T(8,128)(2,1)S(1)}, bf16[264,128]{1,0:T(8,128)(2,1)S(1)}, u32[]{:S(2)}, u32[]{:S(2)}) collective-permute-start(bf16[264,128]{1,0:T(8,128)(2,1)S(1)} %get-tuple-element.10), channel_id=1, source_target_pairs={{0,2},{2,4},{4,6},{6,0},{8,10},{10,12},{12,14},{14,8},{16,18},{18,... | collective-permute-start | bytes 202760 | tf_op jit(solution)/shard_map/ppermute | solution.py:721
  8.1 8.5 %collective-permute-start.1 = (bf16[264,128]{1,0:T(8,128)(2,1)S(1)}, bf16[264,128]{1,0:T(8,128)(2,1)S(1)}, u32[]{:S(2)}, u32[]{:S(2)}) collective-permute-start(bf16[264,128]{1,0:T(8,128)(2,1)S(1)} %get-tuple-element.11), channel_id=1, source_target_pairs={{0,4},{2,6},{4,0},{6,2},{8,12},{10,14},{12,8},{14,10},{16,20},{18,... | collective-permute-start | bytes 202760 | tf_op jit(solution)/shard_map/ppermute | solution.py:721
  10.7 6.0 %collective-permute-start.2 = (bf16[264,128]{1,0:T(8,128)(2,1)S(1)}, bf16[264,128]{1,0:T(8,128)(2,1)S(1)}, u32[]{:S(2)}, u32[]{:S(2)}) collective-permute-start(bf16[264,128]{1,0:T(8,128)(2,1)S(1)} %get-tuple-element.12), channel_id=1, source_target_pairs={{0,6},{2,0},{4,2},{6,4},{8,14},{10,8},{12,10},{14,12},{16,22},{18,... | collective-permute-start | bytes 202760 | tf_op jit(solution)/shard_map/ppermute | solution.py:721
  12.1 4.1 %collective-permute-start.4 = (bf16[6,32,128]{2,1,0:T(8,128)(2,1)S(1)}, bf16[6,32,128]{2,1,0:T(8,128)(2,1)S(1)}, u32[]{:S(2)}, u32[]{:S(2)}) collective-permute-start(bf16[6,32,128]{2,1,0:T(8,128)(2,1)S(1)} %get-tuple-element.13.refs_4_), channel_id=1, source_target_pairs={{0,16},{2,18},{4,20},{6,22},{8,24},{10,26},{12,28},{14,30},{16,0},... | collective-permute-start | bytes 147464 | tf_op jit(solution)/shard_map/ppermute | solution.py:721
  12.6 4.1 %collective-permute-start.3 = (bf16[6,32,128]{2,1,0:T(8,128)(2,1)S(1)}, bf16[6,32,128]{2,1,0:T(8,128)(2,1)S(1)}, u32[]{:S(2)}, u32[]{:S(2)}) collective-permute-start(bf16[6,32,128]{2,1,0:T(8,128)(2,1)S(1)} %get-tuple-element.13.refs_4_), channel_id=1, source_target_pairs={{0,8},{2,10},{4,12},{6,14},{8,0},{10,2},{12,4},{14,6},{16,24},{18,... | collective-permute-start | bytes 147464 | tf_op jit(solution)/shard_map/ppermute | solution.py:721
  20.9 1.6 %collective-permute-start.6 = (f32[576,128]{1,0:T(8,128)S(1)}, f32[576,128]{1,0:T(8,128)S(1)}, u32[]{:S(2)}, u32[]{:S(2)}) collective-permute-start(f32[576,128]{1,0:T(8,128)S(1)} %outer_stage.1.own), channel_id=1, source_target_pairs={{0,1},{1,0},{2,3},{3,2},{4,5},{5,4},{6,7},{7,6},{8,9},{9,8},{10,11... | collective-permute-start | bytes 884744 | tf_op jit(solution)/shard_map/ppermute | solution.py:726
  63.1 1.5 %collective-permute-start.7 = (bf16[16,48,128]{2,1,0:T(8,128)(2,1)S(1)}, bf16[16,48,128]{2,1,0:T(8,128)(2,1)S(1)}, u32[]{:S(2)}, u32[]{:S(2)}) collective-permute-start(bf16[16,48,128]{2,1,0:T(8,128)(2,1)S(1)} %slice.4), channel_id=1, source_target_pairs={{0,1},{1,0},{2,3},{3,2},{4,5},{5,4},{6,7},{7,6},{8,9},{9,8},{10,11... | collective-permute-start | bytes 589832 | tf_op jit(solution)/shard_map/ppermute | solution.py:737

commit v5 on v4

--- a/solution.py
+++ b/solution.py
@@ -236,14 +236,93 @@
     )(tokens, flags, scale, entry, couple)
 
 
+def ready_kernel(sizes, *refs):
+    n, rows, cols, feats = sizes
+    parts = n * n
+    kept = (len(refs) - 17) // 2
+    after, result_scale_hbm, entry_hbm, tokens_hbm, final_hbm = refs[:5]
+    picked, slab, gate_entry, mixed, scale = refs[5 + kept : 10 + kept]
+    entry, tokens, turned_entry, final, plain, result_scale, arrived = refs[10 + 2 * kept :]
+    half = lax.axis_index("depth")
+    width, group, wide = entry.shape[0], feats * parts, 2 * parts
+    copies = [
+        pltpu.make_async_copy(entry_hbm.at[:, pl.ds(0, 4 * width)], entry, arrived.at[0]),
+        pltpu.make_async_copy(tokens_hbm, tokens, arrived.at[1]),
+        pltpu.make_async_copy(entry_hbm.at[:, pl.ds(4 * width, width)], gate_entry, arrived.at[2]),
+        pltpu.make_async_copy(final_hbm, final, arrived.at[3]),
+        pltpu.make_async_copy(result_scale_hbm, result_scale, arrived.at[4]),
+    ]
+    for k in range(kept):
+        copies.append(pltpu.make_async_copy(refs[5 + k], refs[10 + kept + k], arrived.at[5 + k]))
+    for copy in copies:
+        copy.start()
+    t, ch, s = tokens.shape
+    copies[4].wait()
+    at = lax.broadcasted_iota(jnp.int32, (width, width), 1)
+    origin = lax.broadcasted_iota(jnp.int32, (width, width), 0)
+    goal = lax.rem(origin, feats) * wide + lax.div(origin, feats)
+    scale[...] = jnp.dot(
+        result_scale[...], (at == goal).astype(f32), precision=lax.Precision.HIGHEST, preferred_element_type=f32
+    )
+    copies[0].wait()
+    turned_entry[...] = entry[...].astype(f32).T
+    for k in range(4):
+        start = pl.multiple_of(k * width + half * group, 8)
+        turned_entry[k * group : (k + 1) * group] = turned_entry[pl.ds(start, group), :]
+    for k in range(4):
+        for f in range(feats):
+            picked[(k * feats + f) * parts : (k * feats + f + 1) * parts] = turned_entry[
+                pl.ds(k * group + f, parts, stride=feats), :
+            ].astype(bf16)
+    copies[1].wait()
+    turned = tokens[...].astype(f32).reshape(t * ch, s).T
+    for p in range(parts):
+        slab[p] = jnp.concatenate(
+            [turned[p * 8 : (p + 1) * 8, a * 128 : (a + 1) * 128] for a in range(t * ch // 128)], 0
+        )
+    for copy in copies[2:4] + copies[5:]:
+        copy.wait()
+    plain[...] = final[...].astype(f32)
+    for f in range(feats):
+        mixed[f * wide : (f + 1) * wide] = plain[pl.ds(f, wide, stride=feats), :].astype(bf16)
+
+
+def ready_stage(after, entry, tokens, result_scale, final, kept, n, rows, cols):
+    parts, width = n * n, entry.shape[0]
+    feats = width // (2 * parts)
+    t, ch, s = tokens.shape
+    vmem, hbm = pl.BlockSpec(memory_space=pltpu.VMEM), pl.BlockSpec(memory_space=pl.ANY)
+    return pl.pallas_call(
+        functools.partial(ready_kernel, (n, rows, cols, feats)),
+        out_shape=[
+            pltpu.VMEM((4 * feats * parts, width), bf16),
+            pltpu.VMEM((parts, t * ch // 128 * 8, 128), f32),
+            pltpu.VMEM((width, width), bf16),
+            pltpu.VMEM((width, width), bf16),
+            pltpu.VMEM((1, width), f32),
+        ]
+        + [pltpu.VMEM(array.shape, array.dtype) for array in kept],
+        in_specs=[hbm] * (5 + len(kept)),
+        out_specs=[vmem] * (5 + len(kept)),
+        scratch_shapes=[
+            pltpu.VMEM((width, 4 * width), bf16),
+            pltpu.VMEM(tokens.shape, bf16),
+            pltpu.VMEM((4 * width, width), f32),
+            pltpu.VMEM((width, width), bf16),
+            pltpu.VMEM((width, width), f32),
+            pltpu.VMEM((1, width), f32),
+            pltpu.SemaphoreType.DMA((5 + len(kept),)),
+        ],
+        name="ready_stage",
+    )(in_vmem(after), result_scale.reshape(1, -1), entry, tokens, final, *kept)
+
+
 def outer_kernel(n, *refs):
     half, row_index, col_index = lax.axis_index("depth"), lax.axis_index("row"), lax.axis_index("col")
     lefts, rights = refs[:n], refs[n : 2 * n]
     t, hidden, s = rights[0].shape
-    flags, final_hbm, out, left, pieces, right, plain, turned, outer, high, low, couples, couple, final, arrived = refs[2 * n :]
+    flags, final, out, left, pieces, right, plain, turned, outer, high, low, couples, couple = refs[2 * n :]
     tokens, ratio = n * t, 128 // hidden
-    copy = pltpu.make_async_copy(final_hbm, final, arrived)
-    copy.start()
     for k in range(n):
         sent = lefts[k][...].astype(f32)
         place = lax.rem(col_index + (n - k), n)
@@ -259,7 +338,6 @@
         (((1,), (1,)), ((), ())),
         preferred_element_type=f32,
     )
-    copy.wait()
     plain[...] = final[...].astype(f32)
     for d in range(hidden):
         turned[d * hidden : (d + 1) * hidden, :] = plain[pl.ds(d, hidden, stride=hidden), :].astype(bf16)
@@ -308,7 +386,7 @@
     return pl.pallas_call(
         functools.partial(outer_kernel, n),
         out_shape=pltpu.VMEM((tokens * tokens, width), f32),
-        in_specs=[vmem] * (2 * n + 1) + [pl.BlockSpec(memory_space=pl.ANY)],
+        in_specs=[vmem] * (2 * n + 2),
         out_specs=vmem,
         scratch_shapes=[
             pltpu.VMEM((n, t * hidden, s), bf16),
@@ -321,24 +399,18 @@
             pltpu.VMEM((tokens * tokens, hidden * hidden), bf16),
             pltpu.VMEM((n, tokens // 2 * t, width), f32),
             pltpu.VMEM((tokens // 2 * tokens, width), f32),
-            pltpu.VMEM(final.shape, bf16),
-            pltpu.SemaphoreType.DMA,
         ],
         name="outer_stage",
-    )(*map(in_vmem, lefts), *map(in_vmem, rights), flags, final)
-
-
-def pair_kernel(sizes, genuine, own, other, offset, couple_scale, score, tri_scale, entry_hbm, tokens_hbm, block, value, normed, projected, logits, tri, head_rows, entry, tokens, turned_entry, picked, arrived):
+    )(*map(in_vmem, lefts), *map(in_vmem, rights), in_vmem(flags), in_vmem(final))
+
+
+def pair_kernel(sizes, genuine_hbm, own, other, offset, couple_scale, score, tri_scale, picked, slab, block, value, normed, projected, logits, tri, head_rows, genuine, arrived):
     n, rows, cols, heads, feats = sizes
     half, row_index, col_index = lax.axis_index("depth"), lax.axis_index("row"), lax.axis_index("col")
-    copies = [
-        pltpu.make_async_copy(entry_hbm.at[:, pl.ds(0, entry.shape[1])], entry, arrived.at[0]),
-        pltpu.make_async_copy(tokens_hbm, tokens, arrived.at[1]),
-    ]
-    for copy in copies:
-        copy.start()
     parts, width = n * n, own.shape[1]
     part, spare = rows // 2, 128 - feats * cols
+    copy = pltpu.make_async_copy(genuine_hbm, genuine, arrived)
+    copy.start()
     total = own[...] + other[...] + offset[...]
     value[...] = total.astype(bf16).astype(f32)
     unit = unit_rows(value[...])
@@ -353,7 +425,8 @@
     low = jnp.full((heads, 128), -jnp.inf, f32)
     for i in range(rows):
         head_rows[pl.ds(i, heads, stride=rows), :] = place_lanes(logits, i * cols, cols, 0, lane8, low)
-    t, ch, s = tokens.shape
+    t = cols // n
+    copy.wait()
     line = lax.broadcasted_iota(jnp.int32, (8, 128), 1)
     bias = jnp.zeros((8, 128), f32)
     open_lanes = jnp.zeros((8, 128), f32)
@@ -397,17 +470,7 @@
                 )
     normed[:size] = (unit * tri_scale[...]).astype(bf16)
     normed[size:] = jnp.zeros((padded - size, width), bf16)
-    copies[0].wait()
-    turned_entry[...] = entry[...].astype(f32).T
     group = feats * parts
-    for k in range(4):
-        start = pl.multiple_of(k * width + half * group, 8)
-        turned_entry[k * group : (k + 1) * group] = turned_entry[pl.ds(start, group), :]
-    for k in range(4):
-        for f in range(feats):
-            picked[(k * feats + f) * parts : (k * feats + f + 1) * parts] = turned_entry[
-                pl.ds(k * group + f, parts, stride=feats), :
-            ].astype(bf16)
     raw = lax.dot_general(picked[...], normed[...], (((1,), (1,)), ((), ())), preferred_element_type=f32)
     cut = lax.broadcasted_iota(jnp.int32, (parts, 128), 1)
     empty = jnp.zeros((parts, 128), f32)
@@ -420,8 +483,6 @@
                 packed = place_lanes(projected.at[f * parts : (f + 1) * parts], i * cols, cols, f * cols, cut, packed)
             flag = genuine[row_index * rows + i].astype(f32)
             tri[side, pl.ds(i, parts, stride=rows), :] = packed * (open_lanes[:1] * flag)
-    copies[1].wait()
-    turned = tokens[...].astype(f32).reshape(t * ch, s).T
     keep = lane < feats * cols
     for p in range(parts):
         slabs = [
@@ -429,8 +490,8 @@
             jnp.where(keep, tri[1, p * rows : (p + 1) * rows], second),
             flat,
             stats,
+            slab[p],
         ]
-        slabs += [turned[p * 8 : (p + 1) * 8, a * 128 : (a + 1) * 128] for a in range(t * ch // 128)]
         if p < part:
             slabs.append(value[pl.ds(pl.multiple_of((half * part + p) * cols, 8), cols), :])
         else:
@@ -438,18 +499,17 @@
         block[p] = jnp.concatenate(slabs, 0).astype(bf16)
 
 
-def pair_stage(genuine, own, other, offset, couple_scale, score, tri_scale, entry, tokens, n, rows, cols):
+def pair_stage(genuine, own, other, offset, couple_scale, score, tri_scale, picked, slab, n, rows, cols):
     parts, width = n * n, own.shape[1]
     heads = score.shape[0]
     feats = width // (2 * parts)
-    t, ch, s = tokens.shape
     padded = (rows * cols + 127) // 128 * 128
-    vmem, hbm = pl.BlockSpec(memory_space=pltpu.VMEM), pl.BlockSpec(memory_space=pl.ANY)
-    length = 3 * rows + 8 + t * ch // 128 * 8 + cols
+    vmem = pl.BlockSpec(memory_space=pltpu.VMEM)
+    length = 3 * rows + 8 + slab.shape[1] + cols
     return pl.pallas_call(
         functools.partial(pair_kernel, (n, rows, cols, heads, feats)),
         out_shape=pltpu.VMEM((parts, length, 128), bf16),
-        in_specs=[pl.BlockSpec(memory_space=pltpu.SMEM)] + [vmem] * 6 + [hbm] * 2,
+        in_specs=[pl.BlockSpec(memory_space=pl.ANY)] + [vmem] * 8,
         out_specs=vmem,
         scratch_shapes=[
             pltpu.VMEM((rows * cols, width), f32),
@@ -458,17 +518,11 @@
             pltpu.VMEM((heads, padded), f32),
             pltpu.VMEM((2, parts * rows, 128), f32),
             pltpu.VMEM((heads * rows, 128), f32),
-            pltpu.VMEM((width, 4 * width), bf16),
-            pltpu.VMEM(tokens.shape, bf16),
-            pltpu.VMEM((4 * width, width), f32),
-            pltpu.VMEM((4 * feats * parts, width), bf16),
-            pltpu.SemaphoreType.DMA((2,)),
+            pltpu.SMEM(genuine.shape, genuine.dtype),
+            pltpu.SemaphoreType.DMA,
         ],
         name="pair_stage",
-    )(
-        genuine, in_vmem(own), in_vmem(other), offset.reshape(1, -1), couple_scale.reshape(1, -1), score, tri_scale.reshape(1, -1),
-        entry, tokens,
-    )
+    )(genuine, *map(in_vmem, (own, other, offset, couple_scale, score, tri_scale, picked, slab)))
 
 
 def halves(value):
@@ -600,18 +654,18 @@
             pltpu.VMEM((8 * tokens, 128), f32),
         ],
         name="middle_stage",
-    )(in_vmem(block), seq_scale.reshape(1, -1), content, sigmoid_matrix, final.T)
-
-
-def last_kernel(sizes, own, other, tri_scale, result_scale, entry_hbm, final_hbm, pair_output, revised, product, turned, pair, entry, final, plain, mixed, arrived):
+    )(*map(in_vmem, (block, seq_scale, content, sigmoid_matrix, final)))
+
+
+def turn_kernel(start, own, revised):
+    for a in range((own.shape[1] - start) // 8):
+        piece = [own[p, start + 8 * a : start + 8 * a + 8].astype(f32) for p in range(own.shape[0])]
+        revised[a * 128 : (a + 1) * 128] = jnp.concatenate(piece, 0).T.astype(bf16)
+
+
+def last_kernel(sizes, own, other, tri_scale, scale, entry, mixed, pair_output, product, turned, pair):
     n, rows, cols, feats = sizes
-    copies = [
-        pltpu.make_async_copy(entry_hbm.at[:, pl.ds(4 * final.shape[1], final.shape[1])], entry, arrived.at[0]),
-        pltpu.make_async_copy(final_hbm, final, arrived.at[1]),
-    ]
-    for copy in copies:
-        copy.start()
-    parts, width = n * n, final.shape[1]
+    parts = n * n
     part, wide = rows // 2, 2 * n * n
     mine = lax.axis_index("depth")
     theirs = 1 - mine
@@ -637,50 +691,34 @@
             turned[(g * per + k) * cols : (g * per + k + 1) * cols] = merged
     value = pair[...]
     normed = (unit_rows(value) * tri_scale[...]).astype(bf16)
-    for copy in copies:
-        copy.wait()
     gate = jax.nn.sigmoid(jnp.dot(normed, entry[...], preferred_element_type=f32))
-    plain[...] = final[...].astype(f32)
-    for f in range(feats):
-        mixed[f * wide : (f + 1) * wide] = plain[pl.ds(f, wide, stride=feats), :].astype(bf16)
-    at = lax.broadcasted_iota(jnp.int32, (width, width), 1)
-    origin = lax.broadcasted_iota(jnp.int32, (width, width), 0)
-    goal = lax.rem(origin, feats) * wide + lax.div(origin, feats)
-    scale = jnp.dot(
-        result_scale[...], (at == goal).astype(f32), precision=lax.Precision.HIGHEST, preferred_element_type=f32
-    )
-    result = (unit_rows(turned[...]) * scale).astype(bf16)
+    result = (unit_rows(turned[...]) * scale[...]).astype(bf16)
     pair_output[...] = (value + gate * jnp.dot(result, mixed[...], preferred_element_type=f32)).astype(bf16)
-    for a in range((own.shape[1] - rows - cols) // 8):
-        start = rows + cols + 8 * a
-        flipped = jnp.concatenate([own[p, start : start + 8].astype(f32) for p in range(parts)], 0).T
-        revised[a * 128 : (a + 1) * 128] = flipped.astype(bf16)
-
-
-def last_stage(own, other, tri_scale, entry, result_scale, final, n, rows, cols, t, ch):
-    parts, width = n * n, final.shape[1]
+
+
+def last_stage(own, other, tri_scale, gate_entry, scale, mixed, n, rows, cols, t, ch):
+    parts, width = n * n, mixed.shape[1]
     feats = width // (2 * parts)
-    vmem, hbm = pl.BlockSpec(memory_space=pltpu.VMEM), pl.BlockSpec(memory_space=pl.ANY)
-    pair_output, revised = pl.pallas_call(
+    vmem = pl.BlockSpec(memory_space=pltpu.VMEM)
+    revised = pl.pallas_call(
+        functools.partial(turn_kernel, rows + cols),
+        out_shape=jax.ShapeDtypeStruct((t * ch, 8 * parts), bf16),
+        in_specs=[vmem],
+        out_specs=vmem,
+        name="turn_stage",
+    )(in_vmem(own))
+    pair_output = pl.pallas_call(
         functools.partial(last_kernel, (n, rows, cols, feats)),
-        out_shape=[
-            jax.ShapeDtypeStruct((rows * cols, width), bf16),
-            jax.ShapeDtypeStruct((t * ch, 8 * parts), bf16),
-        ],
-        in_specs=[vmem] * 4 + [hbm] * 2,
-        out_specs=[vmem] * 2,
+        out_shape=jax.ShapeDtypeStruct((rows * cols, width), bf16),
+        in_specs=[vmem] * 6,
+        out_specs=vmem,
         scratch_shapes=[
             pltpu.VMEM((2, parts * rows, 128), f32),
             pltpu.VMEM((rows * cols, 128), f32),
             pltpu.VMEM((rows * cols, width), f32),
-            pltpu.VMEM((width, width), bf16),
-            pltpu.VMEM((width, width), bf16),
-            pltpu.VMEM((width, width), f32),
-            pltpu.VMEM((width, width), bf16),
-            pltpu.SemaphoreType.DMA((2,)),
         ],
         name="last_stage",
-    )(in_vmem(own), in_vmem(other), tri_scale.reshape(1, -1), result_scale.reshape(1, -1), entry, final)
+    )(*map(in_vmem, (own, other, tri_scale, scale, gate_entry, mixed)))
     return revised.reshape(t, ch, 8 * parts).transpose(2, 0, 1), pair_output.reshape(rows, cols, width)
 
 
@@ -708,7 +746,6 @@
     parts = n * n
     rows, cols, width = couple_state.shape
     count, t, ch = sequence_stack.shape
-    hidden = tensor_entry_matrix.shape[1] // 2
     heads = mean_score_matrix.shape[1]
     feats = width // (2 * parts)
     order = tuple(tuple((r * rows + c * t, t) for r in range(n)) for c in range(n))
@@ -722,22 +759,36 @@
 
     rights = [right] + [move(right, lambda r, c, k=k: (r ^ k, c)) for k in range(1, n)]
     lefts = [sends[0]] + [move(sends[k], lambda r, c, k=k: (r, (c + k) % n)) for k in range(1, n)]
-    share = outer_stage(lefts, rights, flags, tensor_final_matrix)
+    kept = (
+        flags,
+        tensor_final_matrix,
+        tensor_offset.reshape(1, -1),
+        mean_couple_scale.reshape(1, -1),
+        mean_score_matrix.T,
+        trimul_scale.reshape(1, -1),
+        mean_sequence_scale.reshape(1, -1),
+        mean_content_matrix,
+        mean_sigmoid_matrix,
+        mean_final_matrix.T,
+    )
+    ready = ready_stage(
+        right, trimul_entry_matrix, tokens, trimul_result_scale, trimul_final_matrix, kept, n, rows, cols
+    )
+    lefts, ready = lax.optimization_barrier((lefts, ready))
+    picked, slab, gate_entry, mixed, scale, *kept = ready
+    flags, outer_final, offset, couple_scale, score, tri_scale, seq_scale, content, sigmoid_matrix, mean_final = kept
+    share = outer_stage(lefts, rights, flags, outer_final)
     other = lax.ppermute(share, "depth", [(0, 1), (1, 0)])
     block = pair_stage(
-        genuine_residue_flags, share, other, tensor_offset, mean_couple_scale, mean_score_matrix.T, trimul_scale,
-        trimul_entry_matrix, tokens, n, rows, cols,
+        genuine_residue_flags, share, other, offset, couple_scale, score, tri_scale, picked, slab, n, rows, cols
     )
     block = lax.all_to_all(block, ("row", "col"), 0, 0, tiled=True)
     block = middle_stage(
-        block, n, rows, cols, heads, feats, order, mean_sequence_scale, mean_content_matrix, mean_sigmoid_matrix,
-        mean_final_matrix,
+        block, n, rows, cols, heads, feats, order, seq_scale, content, sigmoid_matrix, mean_final
     )
     block = lax.all_to_all(block, ("row", "col"), 0, 0, tiled=True)
     other = lax.ppermute(block[:, : rows + cols], "depth", [(0, 1), (1, 0)])
-    return last_stage(
-        block, other, trimul_scale, trimul_entry_matrix, trimul_result_scale, trimul_final_matrix, n, rows, cols, t, ch
-    )
+    return last_stage(block, other, tri_scale, gate_entry, scale, mixed, n, rows, cols, t, ch)
 
 
 def suits(mesh):

time: 68.1 us -> 61.7 us (0.906)
  Pallas kernels: 15.7 us -> 12 us
  waiting for transfers between devices: 6.56 us -> 4.4 us
    pallas_call x0 -> x2, Pallas kernels: none -> 2.13 us  [the longest x1 1.39 us: ready_stage(): pl.pallas_call(functools.partial(ready_kernel, (n, rows, cols, feats)), o...]
    pallas_call x1, Pallas kernels: 3.45 us -> 1.48 us  [pair_stage(): pl.pallas_call(functools.partial(pair_kernel, (n, rows, cols, heads, feat...]
    pallas_call x1, Pallas kernels: 4.18 us -> 2.45 us  [outer_stage(): pl.pallas_call(functools.partial(outer_kernel, n), out_shape=pltpu.VMEM((...]
    ppermute x6, waiting for transfers between devices: 3.56 us -> 2.15 us  [move(): return lax.ppermute(array, ('row', 'col'), pairs)]
    pallas_call x1, Pallas kernels: 2.99 us -> 1.59 us  [last_stage(): pl.pallas_call(functools.partial(last_kernel, (n, rows, cols, feats)), ou...]
    pallas_call x1, Pallas kernels: 3.17 us -> 2.37 us  [middle_stage(): pl.pallas_call(functools.partial(middle_kernel, (n, rows, cols, heads, fe...]
    ppermute x1, waiting for transfers between devices: 1.43 us -> 0.68 us  [on_device(): other = lax.ppermute(block[:, :rows + cols], 'depth', [(0, 1), (1, 0)])]
  transfers between devices with their start and end apart: 8 -> 8, of which waited for: 4 -> 5; matrix products, arithmetic and copies ran while one was open for 0% -> 0% of each run, Pallas kernels for 0% -> 3%
where the time goes in v5:
time: 61.7 us; the launch traced here: 61.4 us
  blocking collectives  33.6 us (54%)
  Pallas kernels  12 us (19%)
  starting transfers between devices  10.7 us (17%)
  waiting for transfers between devices  4.4 us (7%)
  between operations  0.71 us (1%)
    all_to_all x2, blocking collectives, on_device(): block = lax.all_to_all(block, ('row', 'col'), 0, 0, tiled=True)  33.6 us
    ppermute x6, starting transfers between devices, move(): return lax.ppermute(array, ('row', 'col'), pairs)  10.5 us
    pallas_call x1, Pallas kernels, outer_stage(): pl.pallas_call(functools.partial(outer_kernel, n), out_shape=pltpu.VMEM((...  2.45 us
    pallas_call x1, Pallas kernels, middle_stage(): pl.pallas_call(functools.partial(middle_kernel, (n, rows, cols, heads, fe...  2.37 us
    ppermute x6, waiting for transfers between devices, move(): return lax.ppermute(array, ('row', 'col'), pairs)  2.15 us
    pallas_call x1, Pallas kernels, first_stage(): pl.pallas_call(first_kernel, out_shape=[pltpu.VMEM((length, s), bf16)] *...  1.93 us
    pallas_call x1, Pallas kernels, last_stage(): pl.pallas_call(functools.partial(last_kernel, (n, rows, cols, feats)), ou...  1.59 us
    ppermute x1, waiting for transfers between devices, on_device(): other = lax.ppermute(share, 'depth', [(0, 1), (1, 0)])  1.57 us
  transfers between devices with their start and end apart: 8, of which 5 were waited for; matrix products, arithmetic and copies ran while one was open for 0% of the time, Pallas kernels for 3%

profile of v5, /device:TPU:0, one launch (start us, length us, event | category | flops | bytes accessed | tf_op | source)
XLA Modules:
  0.0 61.4 jit_solution(12710439116393703142)
XLA Ops:
  0.6 1.9 %first_stage.1 = (bf16[264,128]{1,0:T(8,128)(2,1)S(1)}, bf16[264,128]{1,0:T(8,128)(2,1)S(1)}, bf16[264,128]{1,0:T(8,128)(2,1)S(1)}, bf16[264,128]{1,0:T(8,128)(2,1)S(1)}, bf16[6,32,128]{2,1,0:T(8,128)(2,1)S(1)}) custom-call(bf16[6,64,128]{2,1,0:T(8,128)(2,1)} %bitcast.14, s32[2,128]{1,0:T(2,128)} %bitcast.20, f32[1,64]{1,0:T(1,128)} %bitcast.22, ...), custom_call_target="tpu_custom_call" | custom-call | tf_op jit(solution)/shard_map/first_stage/pallas_call | solution.py:224
  2.6 3.1 %collective-permute-start = (bf16[264,128]{1,0:T(8,128)(2,1)S(1)}, bf16[264,128]{1,0:T(8,128)(2,1)S(1)}, u32[]{:S(2)}, u32[]{:S(2)}) collective-permute-start(bf16[264,128]{1,0:T(8,128)(2,1)S(1)} %get-tuple-element.42), channel_id=1, source_target_pairs={{0,2},{2,4},{4,6},{6,0},{8,10},{10,12},{12,14},{14,8},{16,18},{18,... | collective-permute-start | bytes 202760 | tf_op jit(solution)/shard_map/ppermute | solution.py:758
  5.7 2.6 %collective-permute-start.1 = (bf16[264,128]{1,0:T(8,128)(2,1)S(1)}, bf16[264,128]{1,0:T(8,128)(2,1)S(1)}, u32[]{:S(2)}, u32[]{:S(2)}) collective-permute-start(bf16[264,128]{1,0:T(8,128)(2,1)S(1)} %get-tuple-element.43), channel_id=1, source_target_pairs={{0,4},{2,6},{4,0},{6,2},{8,12},{10,14},{12,8},{14,10},{16,20},{18,... | collective-permute-start | bytes 202760 | tf_op jit(solution)/shard_map/ppermute | solution.py:758
  8.3 1.3 %collective-permute-start.2 = (bf16[264,128]{1,0:T(8,128)(2,1)S(1)}, bf16[264,128]{1,0:T(8,128)(2,1)S(1)}, u32[]{:S(2)}, u32[]{:S(2)}) collective-permute-start(bf16[264,128]{1,0:T(8,128)(2,1)S(1)} %get-tuple-element.44), channel_id=1, source_target_pairs={{0,6},{2,0},{4,2},{6,4},{8,14},{10,8},{12,10},{14,12},{16,22},{18,... | collective-permute-start | bytes 202760 | tf_op jit(solution)/shard_map/ppermute | solution.py:758
  9.6 2.4 %collective-permute-start.5 = (bf16[6,32,128]{2,1,0:T(8,128)(2,1)S(1)}, bf16[6,32,128]{2,1,0:T(8,128)(2,1)S(1)}, u32[]{:S(2)}, u32[]{:S(2)}) collective-permute-start(bf16[6,32,128]{2,1,0:T(8,128)(2,1)S(1)} %get-tuple-element.45.refs_0_.refs_4_), channel_id=1, source_target_pairs={{0,24},{2,26},{4,28},{6,30},{8,16},{10,18},{12,20},{14,22},{16,8},... | collective-permute-start | bytes 147464 | tf_op jit(solution)/shard_map/ppermute | solution.py:758
  12.1 0.5 collective-permute-start.4
  12.6 0.0 collective-permute-done.refs_1_
  12.6 0.5 collective-permute-start.3
  13.1 1.4 %ready_stage.1 = (bf16[256,128]{1,0:T(8,128)(2,1)S(1)}, f32[16,24,128]{2,1,0:T(8,128)S(1)}, bf16[128,128]{1,0:T(8,128)(2,1)S(1)}, bf16[128,128]{1,0:T(8,128)(2,1...) custom-call(bf16[6,32,128]{2,1,0:T(8,128)(2,1)S(1)} %get-tuple-eleme, ...), custom_call_target="tpu_custom_call" | custom-call | tf_op jit(solution)/shard_map/ready_stage/pallas_call | solution.py:295
  14.5 0.0 collective-permute-done.2.refs_3_
  14.5 0.1 collective-permute-done.5.refs_7_
  14.6 1.5 %collective-permute-done.4.refs_6_ = bf16[6,32,128]{2,1,0:T(8,128)(2,1)S(1)} collective-permute-done((bf16[6,32,128]{2,1,0:T(8,128)(2,1)S(1)}, bf16[6,32,128]{2,1,0:T(8,128)(2,1)S(1)}, u32[]{:S(2)}, u32[]{:S(2)}) %collective-permute-start.4) | collective-permute-done | bytes 49184 | tf_op jit(solution)/shard_map/ppermute | solution.py:758
  16.1 0.5 collective-permute-done.3.refs_5_
  16.7 2.5 %outer_stage.1.own = f32[576,128]{1,0:T(8,128)S(1)} custom-call(bf16[264,128]{1,0:T(8,128)(2,1)S(1)} %get-tuple-element.61.refs_0_, bf16[264,128]{1,0:T(8,128)(2,1)S(1)} %collective-permute-done.refs_1_, bf16[264,128]{1,0:T(8,128)(2,1)S(1)} %collective-permute-done.1.refs_2_, bf16[264,128]{1,0:T(8,128)(2,1)S(1)} %collective-permute-done.2.refs_3_, ...), custom_call_target="tpu_custom_call" | custom-call | tf_op jit(solution)/shard_map/outer_stage/pallas_call | solution.py:386
  19.1 0.1 collective-permute-start.6
  19.2 1.6 %collective-permute-done.6.other = f32[576,128]{1,0:T(8,128)S(1)} collective-permute-done((f32[576,128]{1,0:T(8,128)S(1)}, f32[576,128]{1,0:T(8,128)S(1)}, u32[]{:S(2)}, u32[]{:S(2)}) %collective-permute-start.6) | collective-permute-done | bytes 294944 | tf_op jit(solution)/shard_map/ppermute | solution.py:781
  20.8 1.5 %pair_stage.1 = bf16[16,128,128]{2,1,0:T(8,128)(2,1)S(1)} custom-call(s32[96]{0:T(128)} %genuine_hbm.1, f32[576,128]{1,0:T(8,128)S(1)} %outer_stage.1.own, f32[576,128]{1,0:T(8,128)S(1)} %collective-permute-done.6.other, f32[1,128]{1,0:T(1,128)S(1)} %get-tuple-element.67.offset, f32[1,128]{1,0:T(1,128)S(1)} %get-tuple-element.68.couple_scale, ...), custom_call_target="tpu_custom_call" | custom-call | tf_op jit(solution)/shard_map/pair_stage/pallas_call | solution.py:509
  22.3 19.5 %all_to_all.10.block = bf16[16,128,128]{2,1,0:T(8,128)(2,1)S(1)} all-to-all(bf16[16,128,128]{2,1,0:T(8,128)(2,1)S(1)} %pair_stage.1), channel_id=1, replica_groups=mesh['row'=4,'col'=4,'depth'=2] {'row','col'}, dimensions={0} | all-to-all | bytes 1048576 | tf_op jit(solution)/shard_map/all_to_all | solution.py:785
  41.8 2.4 %middle_stage.1 = bf16[16,72,128]{2,1,0:T(8,128)(2,1)S(1)} custom-call(bf16[16,128,128]{2,1,0:T(8,128)(2,1)S(1)} %all_to_all.10.block, f32[1,64]{1,0:T(1,128)S(1)} %get-tuple-element.73.seq_scale, bf16[64,256]{1,0:T(8,128)(2,1)S(1)} %get-tuple-element.74.content, bf16[64,256]{1,0:T(8,128)(2,1)S(1)} %get-tuple-element.75.sigmoid_matrix, ...), custom_call_target="tpu_custom_call" | custom-call | tf_op jit(solution)/shard_map/middle_stage/pallas_call | solution.py:639
  44.1 14.1 %all_to_all.11.own = bf16[16,72,128]{2,1,0:T(8,128)(2,1)S(1)} all-to-all(bf16[16,72,128]{2,1,0:T(8,128)(2,1)S(1)} %middle_stage.1), channel_id=1, replica_groups=mesh['row'=4,'col'=4,'depth'=2] {'row','col'}, dimensions={0} | all-to-all | bytes 589824 | tf_op jit(solution)/shard_map/all_to_all | solution.py:789
  58.3 0.1 collective-permute-start.7
  58.4 0.7 %turn_stage.1 = bf16[384,128]{1,0:T(8,128)(2,1)} custom-call(bf16[16,72,128]{2,1,0:T(8,128)(2,1)S(1)} %all_to_all.11.own), custom_call_target="tpu_custom_call" | custom-call | tf_op jit(solution)/shard_map/turn_stage/pallas_call | solution.py:703
  59.1 0.7 %collective-permute-done.7.other = bf16[16,48,128]{2,1,0:T(8,128)(2,1)S(1)} collective-permute-done((bf16[16,48,128]{2,1,0:T(8,128)(2,1)S(1)}, bf16[16,48,128]{2,1,0:T(8,128)(2,1)S(1)}, u32[]{:S(2)}, u32[]{:S(2)}) %collective-permute-start.7) | collective-permute-done | bytes 196640 | tf_op jit(solution)/shard_map/ppermute | solution.py:790
  59.8 1.6 %last_stage.1 = bf16[576,128]{1,0:T(8,128)(2,1)} custom-call(bf16[16,72,128]{2,1,0:T(8,128)(2,1)S(1)} %all_to_all.11.own, bf16[16,48,128]{2,1,0:T(8,128)(2,1)S(1)} %collective-permute-done.7.other, f32[1,128]{1,0:T(1,128)S(1)} %get-tuple-element.70.tri_scale, f32[1,128]{1,0:T(1,128)S(1)} %get-tuple-element.77.scale, ...), custom_call_target="tpu_custom_call" | custom-call | tf_op jit(solution)/shard_map/last_stage/pallas_call | solution.py:710
  (2 shorter events, 0.0 us)
Async XLA Ops:
  2.6 10.0 %collective-permute-start = (bf16[264,128]{1,0:T(8,128)(2,1)S(1)}, bf16[264,128]{1,0:T(8,128)(2,1)S(1)}, u32[]{:S(2)}, u32[]{:S(2)}) collective-permute-start(bf16[264,128]{1,0:T(8,128)(2,1)S(1)} %get-tuple-element.42), channel_id=1, source_target_pairs={{0,2},{2,4},{4,6},{6,0},{8,10},{10,12},{12,14},{14,8},{16,18},{18,... | collective-permute-start | bytes 202760 | tf_op jit(solution)/shard_map/ppermute | solution.py:758
  5.7 8.8 %collective-permute-start.1 = (bf16[264,128]{1,0:T(8,128)(2,1)S(1)}, bf16[264,128]{1,0:T(8,128)(2,1)S(1)}, u32[]{:S(2)}, u32[]{:S(2)}) collective-permute-start(bf16[264,128]{1,0:T(8,128)(2,1)S(1)} %get-tuple-element.43), channel_id=1, source_target_pairs={{0,4},{2,6},{4,0},{6,2},{8,12},{10,14},{12,8},{14,10},{16,20},{18,... | collective-permute-start | bytes 202760 | tf_op jit(solution)/shard_map/ppermute | solution.py:758
  8.3 6.3 %collective-permute-start.2 = (bf16[264,128]{1,0:T(8,128)(2,1)S(1)}, bf16[264,128]{1,0:T(8,128)(2,1)S(1)}, u32[]{:S(2)}, u32[]{:S(2)}) collective-permute-start(bf16[264,128]{1,0:T(8,128)(2,1)S(1)} %get-tuple-element.44), channel_id=1, source_target_pairs={{0,6},{2,0},{4,2},{6,4},{8,14},{10,8},{12,10},{14,12},{16,22},{18,... | collective-permute-start | bytes 202760 | tf_op jit(solution)/shard_map/ppermute | solution.py:758
  9.6 5.0 %collective-permute-start.5 = (bf16[6,32,128]{2,1,0:T(8,128)(2,1)S(1)}, bf16[6,32,128]{2,1,0:T(8,128)(2,1)S(1)}, u32[]{:S(2)}, u32[]{:S(2)}) collective-permute-start(bf16[6,32,128]{2,1,0:T(8,128)(2,1)S(1)} %get-tuple-element.45.refs_0_.refs_4_), channel_id=1, source_target_pairs={{0,24},{2,26},{4,28},{6,30},{8,16},{10,18},{12,20},{14,22},{16,8},... | collective-permute-start | bytes 147464 | tf_op jit(solution)/shard_map/ppermute | solution.py:758
  12.1 4.1 %collective-permute-start.4 = (bf16[6,32,128]{2,1,0:T(8,128)(2,1)S(1)}, bf16[6,32,128]{2,1,0:T(8,128)(2,1)S(1)}, u32[]{:S(2)}, u32[]{:S(2)}) collective-permute-start(bf16[6,32,128]{2,1,0:T(8,128)(2,1)S(1)} %get-tuple-element.45.refs_0_.refs_4_), channel_id=1, source_target_pairs={{0,16},{2,18},{4,20},{6,22},{8,24},{10,26},{12,28},{14,30},{16,0},... | collective-permute-start | bytes 147464 | tf_op jit(solution)/shard_map/ppermute | solution.py:758
  12.6 4.1 %collective-permute-start.3 = (bf16[6,32,128]{2,1,0:T(8,128)(2,1)S(1)}, bf16[6,32,128]{2,1,0:T(8,128)(2,1)S(1)}, u32[]{:S(2)}, u32[]{:S(2)}) collective-permute-start(bf16[6,32,128]{2,1,0:T(8,128)(2,1)S(1)} %get-tuple-element.45.refs_0_.refs_4_), channel_id=1, source_target_pairs={{0,8},{2,10},{4,12},{6,14},{8,0},{10,2},{12,4},{14,6},{16,24},{18,... | collective-permute-start | bytes 147464 | tf_op jit(solution)/shard_map/ppermute | solution.py:758
  19.1 1.6 %collective-permute-start.6 = (f32[576,128]{1,0:T(8,128)S(1)}, f32[576,128]{1,0:T(8,128)S(1)}, u32[]{:S(2)}, u32[]{:S(2)}) collective-permute-start(f32[576,128]{1,0:T(8,128)S(1)} %outer_stage.1.own), channel_id=1, source_target_pairs={{0,1},{1,0},{2,3},{3,2},{4,5},{5,4},{6,7},{7,6},{8,9},{9,8},{10,11... | collective-permute-start | bytes 884744 | tf_op jit(solution)/shard_map/ppermute | solution.py:781
  58.3 1.5 %collective-permute-start.7 = (bf16[16,48,128]{2,1,0:T(8,128)(2,1)S(1)}, bf16[16,48,128]{2,1,0:T(8,128)(2,1)S(1)}, u32[]{:S(2)}, u32[]{:S(2)}) collective-permute-start(bf16[16,48,128]{2,1,0:T(8,128)(2,1)S(1)} %slice.4), channel_id=1, source_target_pairs={{0,1},{1,0},{2,3},{3,2},{4,5},{5,4},{6,7},{7,6},{8,9},{9,8},{10,11... | collective-permute-start | bytes 589832 | tf_op jit(solution)/shard_map/ppermute | solution.py:790

commit v6 on v5

--- a/solution.py
+++ b/solution.py
@@ -180,18 +180,23 @@
     return centred * lax.rsqrt(variance + epsilon)
 
 
-def first_kernel(tokens_hbm, flags, scale, entry, couple_hbm, *refs):
-    n = len(refs) - 5
-    sends, right, pieces, tokens, couple, arrived = refs[:n], refs[n], *refs[n + 1 :]
+def first_kernel(tokens_hbm, flags_hbm, scale_hbm, entry_hbm, couple_hbm, *refs):
+    n = len(refs) - 8
+    sends, right, pieces, tokens, couple, flags, scale, entry, arrived = refs[:n], refs[n], *refs[n + 1 :]
     t, ch, s = tokens.shape
     hidden, part = entry.shape[1] // 2, couple.shape[0]
     half, place = lax.axis_index("depth"), lax.axis_index("col")
     copies = [
         pltpu.make_async_copy(tokens_hbm, tokens, arrived.at[0]),
         pltpu.make_async_copy(couple_hbm.at[pl.ds(half * part, part)], couple, arrived.at[1]),
+        pltpu.make_async_copy(flags_hbm, flags, arrived.at[2]),
+        pltpu.make_async_copy(scale_hbm, scale, arrived.at[3]),
+        pltpu.make_async_copy(entry_hbm, entry, arrived.at[4]),
     ]
     for copy in copies:
         copy.start()
+    for copy in copies[2:]:
+        copy.wait()
     mask = flags[pl.ds(half, 1), :].astype(f32)
     square = (ch, ch)
     diagonal = lax.broadcasted_iota(jnp.int32, square, 0) == lax.broadcasted_iota(jnp.int32, square, 1)
@@ -224,13 +229,16 @@
     return pl.pallas_call(
         first_kernel,
         out_shape=[pltpu.VMEM((length, s), bf16)] * n + [pltpu.VMEM((t, hidden, s), bf16)],
-        in_specs=[hbm, vmem, vmem, vmem, hbm],
+        in_specs=[hbm] * 5,
         out_specs=[vmem] * (n + 1),
         scratch_shapes=[
             pltpu.VMEM((n, rows // 2 * t, width), f32),
             pltpu.VMEM(tokens.shape, bf16),
             pltpu.VMEM((rows // 2, cols, width), bf16),
-            pltpu.SemaphoreType.DMA((2,)),
+            pltpu.VMEM(flags.shape, flags.dtype),
+            pltpu.VMEM(scale.shape, f32),
+            pltpu.VMEM(entry.shape, bf16),
+            pltpu.SemaphoreType.DMA((5,)),
         ],
         name="first_stage",
     )(tokens, flags, scale, entry, couple)
@@ -550,7 +558,7 @@
     spare = 128 - feats * cols
 
     def stacked(c, start, count):
-        return jnp.concatenate([wide[r * n + c, start : start + count] for r in range(n)], 0)
+        return jnp.concatenate([wide[c * n + r, start : start + count] for r in range(n)], 0)
 
     rhs[...] = jnp.zeros_like(rhs)
     for c in range(n):
@@ -573,7 +581,7 @@
         expos.append(jnp.concatenate([stacked(c, 2 * rows, rows), rest], 1))
         peak = []
         for r in range(n):
-            stats = wide[r * n + c, 3 * rows : 3 * rows + 8]
+            stats = wide[c * n + r, 3 * rows : 3 * rows + 8]
             for q in range(rows // 8):
                 one = pltpu.roll(stats, (128 - 3 * heads * q) % 128, 1) if q else stats
                 peak.append(one + pltpu.roll(one, 128 - heads, 1) + pltpu.roll(one, 128 - 2 * heads, 1))
@@ -588,11 +596,12 @@
     for c in range(n):
         scale = jnp.where(lane < heads, factors[c] / jnp.where(lane < heads, total, 1.0), 0.0)
         weights[:, c * 256 : (c + 1) * 256] = (expos[c] * two_pass_dot(scale, spread)).astype(bf16)
+    first_token = [((p % n) * n + p // n) * t for p in range(parts)]
     for p in range(parts):
         for g in range(groups):
             pair = wide[p, 3 * rows + 8 + 8 * g : 3 * rows + 16 + 8 * g]
             for k in range(per):
-                x[pl.ds(p * t + g * per + k, s, stride=tokens), :] = pltpu.roll(pair, 128 - k * ch, 1) if k else pair
+                x[pl.ds(first_token[p] + g * per + k, s, stride=tokens), :] = pltpu.roll(pair, 128 - k * ch, 1) if k else pair
     raw = x[...][:, :ch]
     centred = raw - jnp.mean(raw, -1, keepdims=True)
     variance = jnp.mean(centred * centred, -1, keepdims=True)
@@ -613,7 +622,7 @@
     delta = two_pass_dot(gated[...], final[...], 1)
     revised[:, :ch] = raw + delta
     for p in range(parts):
-        r, c = p // n, p % n
+        c, r = p // n, p % n
         slab = jnp.zeros((rows, 128), f32)
         for f in range(feats):
             shift = ((f - c) * cols) % 128
@@ -621,11 +630,11 @@
             piece = pltpu.roll(piece, shift, 1) if shift else piece
             slab = jnp.where((small >= f * cols) & (small < (f + 1) * cols), piece, slab)
         start = 3 * rows + 8 + 8 * groups + c * t
-        slabs = [slab] + [wide[r * n + k, start : start + t] for k in range(n)]
+        slabs = [slab] + [wide[k * n + r, start : start + t] for k in range(n)]
         for g in range(groups):
-            merged = revised[pl.ds(p * t + g * per, s, stride=tokens), :]
+            merged = revised[pl.ds(first_token[p] + g * per, s, stride=tokens), :]
             for k in range(1, per):
-                piece = revised[pl.ds(p * t + g * per + k, s, stride=tokens), :]
+                piece = revised[pl.ds(first_token[p] + g * per + k, s, stride=tokens), :]
                 merged = jnp.where(tiny >= k * ch, pltpu.roll(piece, k * ch, 1), merged)
             slabs.append(merged)
         out[p] = jnp.concatenate(slabs, 0).astype(bf16)
@@ -782,11 +791,11 @@
     block = pair_stage(
         genuine_residue_flags, share, other, offset, couple_scale, score, tri_scale, picked, slab, n, rows, cols
     )
-    block = lax.all_to_all(block, ("row", "col"), 0, 0, tiled=True)
+    block = lax.all_to_all(block, ("col", "row"), 0, 0, tiled=True)
     block = middle_stage(
         block, n, rows, cols, heads, feats, order, seq_scale, content, sigmoid_matrix, mean_final
     )
-    block = lax.all_to_all(block, ("row", "col"), 0, 0, tiled=True)
+    block = lax.all_to_all(block, ("col", "row"), 0, 0, tiled=True)
     other = lax.ppermute(block[:, : rows + cols], "depth", [(0, 1), (1, 0)])
     return last_stage(block, other, tri_scale, gate_entry, scale, mixed, n, rows, cols, t, ch)
 

time: 61.7 us -> 59.5 us (0.964)
  blocking collectives: 33.6 us -> 32.1 us
  Pallas kernels: 12 us -> 11.2 us
    all_to_all x2, blocking collectives: 33.6 us -> 32.1 us  [on_device(): block = lax.all_to_all(block, ('col', 'row'), 0, 0, tiled=True)]
    pallas_call x1, Pallas kernels: 1.93 us -> 1.23 us  [first_stage(): pl.pallas_call(first_kernel, out_shape=[pltpu.VMEM((length, s), bf16)] *...]
  transfers between devices with their start and end apart: 8 -> 8, of which waited for: 5 -> 5; matrix products, arithmetic and copies ran while one was open for 0% -> 0% of each run, Pallas kernels for 3% -> 4%
where the time goes in v6:
time: 59.5 us; the launch traced here: 59.2 us
  blocking collectives  32.1 us (54%)
  Pallas kernels  11.2 us (19%)
  starting transfers between devices  10.7 us (18%)
  waiting for transfers between devices  4.4 us (7%)
  between operations  0.71 us (1%)
    all_to_all x2, blocking collectives, on_device(): block = lax.all_to_all(block, ('col', 'row'), 0, 0, tiled=True)  32.1 us
    ppermute x6, starting transfers between devices, move(): return lax.ppermute(array, ('row', 'col'), pairs)  10.5 us
    pallas_call x1, Pallas kernels, outer_stage(): pl.pallas_call(functools.partial(outer_kernel, n), out_shape=pltpu.VMEM((...  2.45 us
    pallas_call x1, Pallas kernels, middle_stage(): pl.pallas_call(functools.partial(middle_kernel, (n, rows, cols, heads, fe...  2.36 us
    ppermute x6, waiting for transfers between devices, move(): return lax.ppermute(array, ('row', 'col'), pairs)  2.14 us
    pallas_call x1, Pallas kernels, last_stage(): pl.pallas_call(functools.partial(last_kernel, (n, rows, cols, feats)), ou...  1.59 us
    ppermute x1, waiting for transfers between devices, on_device(): other = lax.ppermute(share, 'depth', [(0, 1), (1, 0)])  1.57 us
    pallas_call x1, Pallas kernels, pair_stage(): pl.pallas_call(functools.partial(pair_kernel, (n, rows, cols, heads, feat...  1.48 us
  transfers between devices with their start and end apart: 8, of which 5 were waited for; matrix products, arithmetic and copies ran while one was open for 0% of the time, Pallas kernels for 4%

profile of v6, /device:TPU:0, one launch (start us, length us, event | category | flops | bytes accessed | tf_op | source)
XLA Modules:
  0.0 59.2 jit_solution(10119973121475315611)
XLA Ops:
  0.6 1.2 %first_stage.1 = (bf16[264,128]{1,0:T(8,128)(2,1)S(1)}, bf16[264,128]{1,0:T(8,128)(2,1)S(1)}, bf16[264,128]{1,0:T(8,128)(2,1)S(1)}, bf16[264,128]{1,0:T(8,128)(2,1)S(1)}, bf16[6,32,128]{2,1,0:T(8,128)(2,1)S(1)}) custom-call(bf16[6,64,128]{2,1,0:T(8,128)(2,1)} %bitcast.14, s32[2,128]{1,0:T(2,128)} %bitcast.20, f32[1,64]{1,0:T(1,128)} %bitcast.22, ...), custom_call_target="tpu_custom_call" | custom-call | tf_op jit(solution)/shard_map/first_stage/pallas_call | solution.py:229
  1.9 3.1 %collective-permute-start = (bf16[264,128]{1,0:T(8,128)(2,1)S(1)}, bf16[264,128]{1,0:T(8,128)(2,1)S(1)}, u32[]{:S(2)}, u32[]{:S(2)}) collective-permute-start(bf16[264,128]{1,0:T(8,128)(2,1)S(1)} %get-tuple-element.42), channel_id=1, source_target_pairs={{0,2},{2,4},{4,6},{6,0},{8,10},{10,12},{12,14},{14,8},{16,18},{18,... | collective-permute-start | bytes 202760 | tf_op jit(solution)/shard_map/ppermute | solution.py:767
  5.0 2.6 %collective-permute-start.1 = (bf16[264,128]{1,0:T(8,128)(2,1)S(1)}, bf16[264,128]{1,0:T(8,128)(2,1)S(1)}, u32[]{:S(2)}, u32[]{:S(2)}) collective-permute-start(bf16[264,128]{1,0:T(8,128)(2,1)S(1)} %get-tuple-element.43), channel_id=1, source_target_pairs={{0,4},{2,6},{4,0},{6,2},{8,12},{10,14},{12,8},{14,10},{16,20},{18,... | collective-permute-start | bytes 202760 | tf_op jit(solution)/shard_map/ppermute | solution.py:767
  7.6 1.3 %collective-permute-start.2 = (bf16[264,128]{1,0:T(8,128)(2,1)S(1)}, bf16[264,128]{1,0:T(8,128)(2,1)S(1)}, u32[]{:S(2)}, u32[]{:S(2)}) collective-permute-start(bf16[264,128]{1,0:T(8,128)(2,1)S(1)} %get-tuple-element.44), channel_id=1, source_target_pairs={{0,6},{2,0},{4,2},{6,4},{8,14},{10,8},{12,10},{14,12},{16,22},{18,... | collective-permute-start | bytes 202760 | tf_op jit(solution)/shard_map/ppermute | solution.py:767
  8.9 2.4 %collective-permute-start.5 = (bf16[6,32,128]{2,1,0:T(8,128)(2,1)S(1)}, bf16[6,32,128]{2,1,0:T(8,128)(2,1)S(1)}, u32[]{:S(2)}, u32[]{:S(2)}) collective-permute-start(bf16[6,32,128]{2,1,0:T(8,128)(2,1)S(1)} %get-tuple-element.45.refs_0_.refs_4_), channel_id=1, source_target_pairs={{0,24},{2,26},{4,28},{6,30},{8,16},{10,18},{12,20},{14,22},{16,8},... | collective-permute-start | bytes 147464 | tf_op jit(solution)/shard_map/ppermute | solution.py:767
  11.4 0.5 collective-permute-start.4
  11.9 0.0 collective-permute-done.refs_1_
  11.9 0.5 collective-permute-start.3
  12.4 1.4 %ready_stage.1 = (bf16[256,128]{1,0:T(8,128)(2,1)S(1)}, f32[16,24,128]{2,1,0:T(8,128)S(1)}, bf16[128,128]{1,0:T(8,128)(2,1)S(1)}, bf16[128,128]{1,0:T(8,128)(2,1...) custom-call(bf16[6,32,128]{2,1,0:T(8,128)(2,1)S(1)} %get-tuple-eleme, ...), custom_call_target="tpu_custom_call" | custom-call | tf_op jit(solution)/shard_map/ready_stage/pallas_call | solution.py:303
  13.8 0.0 collective-permute-done.1.refs_2_
  13.8 0.1 collective-permute-done.5.refs_7_
  13.9 1.5 %collective-permute-done.4.refs_6_ = bf16[6,32,128]{2,1,0:T(8,128)(2,1)S(1)} collective-permute-done((bf16[6,32,128]{2,1,0:T(8,128)(2,1)S(1)}, bf16[6,32,128]{2,1,0:T(8,128)(2,1)S(1)}, u32[]{:S(2)}, u32[]{:S(2)}) %collective-permute-start.4) | collective-permute-done | bytes 49184 | tf_op jit(solution)/shard_map/ppermute | solution.py:767
  15.4 0.5 collective-permute-done.3.refs_5_
  16.0 2.5 %outer_stage.1.own = f32[576,128]{1,0:T(8,128)S(1)} custom-call(bf16[264,128]{1,0:T(8,128)(2,1)S(1)} %get-tuple-element.61.refs_0_, bf16[264,128]{1,0:T(8,128)(2,1)S(1)} %collective-permute-done.refs_1_, bf16[264,128]{1,0:T(8,128)(2,1)S(1)} %collective-permute-done.1.refs_2_, bf16[264,128]{1,0:T(8,128)(2,1)S(1)} %collective-permute-done.2.refs_3_, ...), custom_call_target="tpu_custom_call" | custom-call | tf_op jit(solution)/shard_map/outer_stage/pallas_call | solution.py:394
  18.4 0.1 collective-permute-start.6
  18.5 1.6 %collective-permute-done.6.other = f32[576,128]{1,0:T(8,128)S(1)} collective-permute-done((f32[576,128]{1,0:T(8,128)S(1)}, f32[576,128]{1,0:T(8,128)S(1)}, u32[]{:S(2)}, u32[]{:S(2)}) %collective-permute-start.6) | collective-permute-done | bytes 294944 | tf_op jit(solution)/shard_map/ppermute | solution.py:790
  20.1 1.5 %pair_stage.1 = bf16[16,128,128]{2,1,0:T(8,128)(2,1)S(1)} custom-call(s32[96]{0:T(128)} %genuine_hbm.1, f32[576,128]{1,0:T(8,128)S(1)} %outer_stage.1.own, f32[576,128]{1,0:T(8,128)S(1)} %collective-permute-done.6.other, f32[1,128]{1,0:T(1,128)S(1)} %get-tuple-element.67.offset, f32[1,128]{1,0:T(1,128)S(1)} %get-tuple-element.68.couple_scale, ...), custom_call_target="tpu_custom_call" | custom-call | tf_op jit(solution)/shard_map/pair_stage/pallas_call | solution.py:517
  21.6 18.4 %all_to_all.10.block = bf16[16,128,128]{2,1,0:T(8,128)(2,1)S(1)} all-to-all(bf16[16,128,128]{2,1,0:T(8,128)(2,1)S(1)} %pair_stage.1), channel_id=1, replica_groups=mesh['row'=4,'col'=4,'depth'=2] {'col','row'}, dimensions={0} | all-to-all | bytes 1048576 | tf_op jit(solution)/shard_map/all_to_all | solution.py:794
  40.0 2.4 %middle_stage.1 = bf16[16,72,128]{2,1,0:T(8,128)(2,1)S(1)} custom-call(bf16[16,128,128]{2,1,0:T(8,128)(2,1)S(1)} %all_to_all.10.block, f32[1,64]{1,0:T(1,128)S(1)} %get-tuple-element.73.seq_scale, bf16[64,256]{1,0:T(8,128)(2,1)S(1)} %get-tuple-element.74.content, bf16[64,256]{1,0:T(8,128)(2,1)S(1)} %get-tuple-element.75.sigmoid_matrix, ...), custom_call_target="tpu_custom_call" | custom-call | tf_op jit(solution)/shard_map/middle_stage/pallas_call | solution.py:648
  42.3 13.7 %all_to_all.11.own = bf16[16,72,128]{2,1,0:T(8,128)(2,1)S(1)} all-to-all(bf16[16,72,128]{2,1,0:T(8,128)(2,1)S(1)} %middle_stage.1), channel_id=1, replica_groups=mesh['row'=4,'col'=4,'depth'=2] {'col','row'}, dimensions={0} | all-to-all | bytes 589824 | tf_op jit(solution)/shard_map/all_to_all | solution.py:798
  56.0 0.1 collective-permute-start.7
  56.1 0.7 %turn_stage.1 = bf16[384,128]{1,0:T(8,128)(2,1)} custom-call(bf16[16,72,128]{2,1,0:T(8,128)(2,1)S(1)} %all_to_all.11.own), custom_call_target="tpu_custom_call" | custom-call | tf_op jit(solution)/shard_map/turn_stage/pallas_call | solution.py:712
  56.9 0.7 %collective-permute-done.7.other = bf16[16,48,128]{2,1,0:T(8,128)(2,1)S(1)} collective-permute-done((bf16[16,48,128]{2,1,0:T(8,128)(2,1)S(1)}, bf16[16,48,128]{2,1,0:T(8,128)(2,1)S(1)}, u32[]{:S(2)}, u32[]{:S(2)}) %collective-permute-start.7) | collective-permute-done | bytes 196640 | tf_op jit(solution)/shard_map/ppermute | solution.py:799
  57.6 1.6 %last_stage.1 = bf16[576,128]{1,0:T(8,128)(2,1)} custom-call(bf16[16,72,128]{2,1,0:T(8,128)(2,1)S(1)} %all_to_all.11.own, bf16[16,48,128]{2,1,0:T(8,128)(2,1)S(1)} %collective-permute-done.7.other, f32[1,128]{1,0:T(1,128)S(1)} %get-tuple-element.70.tri_scale, f32[1,128]{1,0:T(1,128)S(1)} %get-tuple-element.77.scale, ...), custom_call_target="tpu_custom_call" | custom-call | tf_op jit(solution)/shard_map/last_stage/pallas_call | solution.py:719
  (2 shorter events, 0.0 us)
Async XLA Ops:
  1.9 10.0 %collective-permute-start = (bf16[264,128]{1,0:T(8,128)(2,1)S(1)}, bf16[264,128]{1,0:T(8,128)(2,1)S(1)}, u32[]{:S(2)}, u32[]{:S(2)}) collective-permute-start(bf16[264,128]{1,0:T(8,128)(2,1)S(1)} %get-tuple-element.42), channel_id=1, source_target_pairs={{0,2},{2,4},{4,6},{6,0},{8,10},{10,12},{12,14},{14,8},{16,18},{18,... | collective-permute-start | bytes 202760 | tf_op jit(solution)/shard_map/ppermute | solution.py:767
  5.0 8.8 %collective-permute-start.1 = (bf16[264,128]{1,0:T(8,128)(2,1)S(1)}, bf16[264,128]{1,0:T(8,128)(2,1)S(1)}, u32[]{:S(2)}, u32[]{:S(2)}) collective-permute-start(bf16[264,128]{1,0:T(8,128)(2,1)S(1)} %get-tuple-element.43), channel_id=1, source_target_pairs={{0,4},{2,6},{4,0},{6,2},{8,12},{10,14},{12,8},{14,10},{16,20},{18,... | collective-permute-start | bytes 202760 | tf_op jit(solution)/shard_map/ppermute | solution.py:767
  7.6 6.3 %collective-permute-start.2 = (bf16[264,128]{1,0:T(8,128)(2,1)S(1)}, bf16[264,128]{1,0:T(8,128)(2,1)S(1)}, u32[]{:S(2)}, u32[]{:S(2)}) collective-permute-start(bf16[264,128]{1,0:T(8,128)(2,1)S(1)} %get-tuple-element.44), channel_id=1, source_target_pairs={{0,6},{2,0},{4,2},{6,4},{8,14},{10,8},{12,10},{14,12},{16,22},{18,... | collective-permute-start | bytes 202760 | tf_op jit(solution)/shard_map/ppermute | solution.py:767
  8.9 5.0 %collective-permute-start.5 = (bf16[6,32,128]{2,1,0:T(8,128)(2,1)S(1)}, bf16[6,32,128]{2,1,0:T(8,128)(2,1)S(1)}, u32[]{:S(2)}, u32[]{:S(2)}) collective-permute-start(bf16[6,32,128]{2,1,0:T(8,128)(2,1)S(1)} %get-tuple-element.45.refs_0_.refs_4_), channel_id=1, source_target_pairs={{0,24},{2,26},{4,28},{6,30},{8,16},{10,18},{12,20},{14,22},{16,8},... | collective-permute-start | bytes 147464 | tf_op jit(solution)/shard_map/ppermute | solution.py:767
  11.4 4.1 %collective-permute-start.4 = (bf16[6,32,128]{2,1,0:T(8,128)(2,1)S(1)}, bf16[6,32,128]{2,1,0:T(8,128)(2,1)S(1)}, u32[]{:S(2)}, u32[]{:S(2)}) collective-permute-start(bf16[6,32,128]{2,1,0:T(8,128)(2,1)S(1)} %get-tuple-element.45.refs_0_.refs_4_), channel_id=1, source_target_pairs={{0,16},{2,18},{4,20},{6,22},{8,24},{10,26},{12,28},{14,30},{16,0},... | collective-permute-start | bytes 147464 | tf_op jit(solution)/shard_map/ppermute | solution.py:767
  11.9 4.1 %collective-permute-start.3 = (bf16[6,32,128]{2,1,0:T(8,128)(2,1)S(1)}, bf16[6,32,128]{2,1,0:T(8,128)(2,1)S(1)}, u32[]{:S(2)}, u32[]{:S(2)}) collective-permute-start(bf16[6,32,128]{2,1,0:T(8,128)(2,1)S(1)} %get-tuple-element.45.refs_0_.refs_4_), channel_id=1, source_target_pairs={{0,8},{2,10},{4,12},{6,14},{8,0},{10,2},{12,4},{14,6},{16,24},{18,... | collective-permute-start | bytes 147464 | tf_op jit(solution)/shard_map/ppermute | solution.py:767
  18.4 1.6 %collective-permute-start.6 = (f32[576,128]{1,0:T(8,128)S(1)}, f32[576,128]{1,0:T(8,128)S(1)}, u32[]{:S(2)}, u32[]{:S(2)}) collective-permute-start(f32[576,128]{1,0:T(8,128)S(1)} %outer_stage.1.own), channel_id=1, source_target_pairs={{0,1},{1,0},{2,3},{3,2},{4,5},{5,4},{6,7},{7,6},{8,9},{9,8},{10,11... | collective-permute-start | bytes 884744 | tf_op jit(solution)/shard_map/ppermute | solution.py:790
  56.0 1.5 %collective-permute-start.7 = (bf16[16,48,128]{2,1,0:T(8,128)(2,1)S(1)}, bf16[16,48,128]{2,1,0:T(8,128)(2,1)S(1)}, u32[]{:S(2)}, u32[]{:S(2)}) collective-permute-start(bf16[16,48,128]{2,1,0:T(8,128)(2,1)S(1)} %slice.4), channel_id=1, source_target_pairs={{0,1},{1,0},{2,3},{3,2},{4,5},{5,4},{6,7},{7,6},{8,9},{9,8},{10,11... | collective-permute-start | bytes 589832 | tf_op jit(solution)/shard_map/ppermute | solution.py:799
